TPU v7x, 32 devices: a whole 2x2x4 slice. The times are simulated.
32 devices in a mesh: fsdp: 4 (over z), ctx: 4 (over x, core), tp: 2 (over y).
Axes of the slice: x: 2, y: 2, z: 4, core: 2. Of those that a mesh axis runs over, the one named last changes fastest.
Arguments:
- layer_input: float32 [4, 4096, 512], P('fsdp', 'ctx'), may hold values from -6 to 6
- out_grad: float32 [4, 4096, 512], P('fsdp', 'ctx'), may hold values from -6 to 6
- lengths: int32 [4], P('fsdp'), may hold values from 1024 to 4096, as said below
- norm_gains: float32 [5, 512], replicated, may hold values from 0.5 to 1.5
- feed_up: bfloat16 [512, 2048], P('fsdp', 'tp'), may hold values from -0.25 to 0.25
- feed_down: bfloat16 [512, 2048], P('fsdp', 'tp'), may hold values from -0.125 to 0.125
- attend_in: bfloat16 [512, 3, 512], P('fsdp', None, 'tp'), may hold values from -0.25 to 0.25
- attend_out: bfloat16 [512, 512], P('fsdp', 'tp'), may hold values from -6 to 6
- mixer_in: bfloat16 [512, 2, 512], P('fsdp', None, 'tp'), may hold values from -0.25 to 0.25
- mixer_out: bfloat16 [512, 512], P('fsdp', 'tp'), may hold values from -0.25 to 0.25
- depth_kernel: float32 [31, 512], P(None, 'tp'), may hold values from -1.5 to 1.5
- batch_norm: float32 [2, 512], P(None, 'tp'), may hold values from 0.5 to 1.5
- final_up: bfloat16 [512, 2048], P('fsdp', 'tp'), may hold values from -0.25 to 0.25
- final_down: bfloat16 [512, 2048], P('fsdp', 'tp'), may hold values from -0.125 to 0.125
Outputs:
- layer_output: float32 [4, 4096, 512], P('fsdp', 'ctx')
- input_grad: float32 [4, 4096, 512], P('fsdp', 'ctx')
- gains_grad: float32 [5, 512], replicated
- feed_up_grad: float32 [512, 2048], P('fsdp', 'tp')
- feed_down_grad: float32 [512, 2048], P('fsdp', 'tp')
- attend_in_grad: float32 [512, 3, 512], P('fsdp', None, 'tp')
- attend_out_grad: float32 [512, 512], P('fsdp', 'tp')
- mixer_in_grad: float32 [512, 2, 512], P('fsdp', None, 'tp')
- mixer_out_grad: float32 [512, 512], P('fsdp', 'tp')
- kernel_grad: float32 [31, 512], P(None, 'tp')
- norm_grad: float32 [2, 512], P(None, 'tp')
- final_up_grad: float32 [512, 2048], P('fsdp', 'tp')
- final_down_grad: float32 [512, 2048], P('fsdp', 'tp')
Inputs may be any that keep to these rules, and one draw needn't show every extreme that they name: `lengths`: every utterance has at least a quarter of its 4096 frames, and one of them has all 4096.
All inputs are finite; a program needn't handle non-finite values.
Results may differ from a plain program's by a relative error of at most 0.038.
Values may be sent and summed in bfloat16 or wider, within the bound.
A program may use at most 384 MiB of HBM per device.

v0:
```python
import jax
import jax.numpy as jnp
from jax import lax
from jax.sharding import PartitionSpec as P

HEAD = 64
KERNEL = 31


norm_eps = 1e-05
masked_score = -1000000000.0


def with_halo(cells, sides, width):
    for axis, dim in sides:
        count = lax.axis_size(axis)
        ends = count - 1
        head = lax.slice_in_dim(cells, 0, width, axis=dim)
        tail = lax.slice_in_dim(cells, cells.shape[dim] - width, cells.shape[dim], axis=dim)
        cells = jnp.concatenate(
            [
                lax.ppermute(tail, axis, [(i, (i + 1) % count) for i in range(ends)]),
                cells,
                lax.ppermute(head, axis, [((i + 1) % count, i) for i in range(ends)]),
            ],
            axis=dim,
        )
    return cells


def layer_norm(values, gain):
    center = values - jnp.mean(values, -1, keepdims=True)
    spread = jnp.mean(center * center, -1, keepdims=True)
    return center * lax.rsqrt(spread + norm_eps) * gain


def rotary(values, position):
    half = values.shape[-1] // 2
    inverse = 10000.0 ** (-2.0 * jnp.arange(half, dtype=jnp.float32) / values.shape[-1])
    angle = position.astype(jnp.float32)[:, None] * inverse[None, :]
    cosine = jnp.cos(angle)[:, None, :]
    sine = jnp.sin(angle)[:, None, :]
    lower = values[..., :half]
    upper = values[..., half:]
    return jnp.concatenate([lower * cosine - upper * sine, lower * sine + upper * cosine], -1)


def swish(values):
    return values * jax.nn.sigmoid(values)


def tensor_total(partial_value):
    return lax.psum(partial_value.astype(jnp.bfloat16), "tp").astype(jnp.float32)


def product_rows(left, right):
    return lax.dot_general(
        left, right, (((1,), (1,)), ((), ())), preferred_element_type=jnp.float32
    )


def product_cols(left, right):
    return lax.dot_general(
        left, right, (((0,), (0,)), ((), ())), preferred_element_type=jnp.float32
    )


def feed_forward(stream, gain, weight_up, weight_down):
    normed, norm_back = jax.vjp(layer_norm, stream, gain)
    normed_low = normed.astype(jnp.bfloat16)
    hidden = jnp.dot(normed_low, weight_up, preferred_element_type=jnp.float32)
    active, active_back = jax.vjp(swish, hidden)
    active_low = active.astype(jnp.bfloat16)
    branch = tensor_total(product_rows(active_low, weight_down))
    return (branch, (norm_back, normed_low, active_back, active_low))


def feed_backward(branch_grad, saved, weight_up, weight_down):
    norm_back, normed_low, active_back, active_low = saved
    grad_low = branch_grad.astype(jnp.bfloat16)
    down_grad = product_cols(grad_low, active_low)
    hidden_grad = active_back(jnp.dot(grad_low, weight_down, preferred_element_type=jnp.float32))[
        0
    ].astype(jnp.bfloat16)
    up_grad = product_cols(normed_low, hidden_grad)
    normed_grad = tensor_total(product_rows(hidden_grad, weight_up))
    stream_grad, gain_grad = norm_back(normed_grad)
    return (stream_grad, gain_grad, up_grad, down_grad)


def split_joined(joined, heads):
    width = heads * HEAD
    keys = joined[:, :width].reshape(joined.shape[0], heads, HEAD)
    values = joined[:, width:].reshape(joined.shape[0], heads, HEAD)
    return (keys, values)


def attend_scores(query, keys, length):
    scores = jnp.einsum("fhe,lhe->hfl", query, keys, preferred_element_type=jnp.float32)
    live_keys = jnp.arange(keys.shape[0]) < length
    return jnp.where(live_keys[None, None, :], scores, masked_score)


def attend_one(inputs):
    query, joined, length = inputs
    keys, values = split_joined(joined, query.shape[1])
    scores = attend_scores(query, keys, length)
    top = jnp.max(scores, -1, keepdims=True)
    raised = jnp.exp(scores - top)
    total = jnp.sum(raised, -1, keepdims=True)
    weights = (raised / total).astype(jnp.bfloat16)
    mixed = jnp.einsum("hfl,lhe->fhe", weights, values, preferred_element_type=jnp.float32)
    return (mixed.astype(jnp.bfloat16), (top + jnp.log(total))[..., 0])


def attend_back(inputs):
    query, joined, length, log_total, mixed_grad = inputs
    keys, values = split_joined(joined, query.shape[1])
    scores = attend_scores(query, keys, length)
    probs = jnp.exp(scores - log_total[..., None])
    probs_grad = jnp.einsum("fhe,lhe->hfl", mixed_grad, values, preferred_element_type=jnp.float32)
    center = jnp.sum(probs * probs_grad, -1, keepdims=True)
    score_grad = (probs * (probs_grad - center)).astype(jnp.bfloat16)
    query_grad = jnp.einsum("hfl,lhe->fhe", score_grad, keys, preferred_element_type=jnp.float32)
    keys_grad = jnp.einsum("hfl,fhe->lhe", score_grad, query, preferred_element_type=jnp.float32)
    values_grad = jnp.einsum(
        "hfl,fhe->lhe", probs.astype(jnp.bfloat16), mixed_grad, preferred_element_type=jnp.float32
    )
    frames_all = keys.shape[0]
    joined_grad = jnp.concatenate(
        [keys_grad.reshape(frames_all, -1), values_grad.reshape(frames_all, -1)], -1
    )
    return (query_grad, joined_grad)


def per_device(
    layer_input,
    out_grad,
    lengths,
    norm_gains,
    feed_up,
    feed_down,
    attend_in,
    attend_out,
    mixer_in,
    mixer_out,
    depth_kernel,
    batch_norm,
    final_up,
    final_down,
):
    batch, frames, width = layer_input.shape
    rows = batch * frames
    place = lax.axis_index("ctx") * frames + jnp.arange(frames, dtype=jnp.int32)
    live = (place[None, :] < lengths[:, None]).astype(jnp.float32)
    live_rows = live.reshape(rows, 1)
    live_cube = live[:, :, None]
    gathered = (
        lax.all_gather(feed_up, "fsdp", axis=0, tiled=True),
        lax.all_gather(feed_down, "fsdp", axis=0, tiled=True),
        lax.all_gather(attend_in, "fsdp", axis=0, tiled=True),
        lax.all_gather(attend_out, "fsdp", axis=0, tiled=True),
        lax.all_gather(mixer_in, "fsdp", axis=0, tiled=True),
        lax.all_gather(mixer_out, "fsdp", axis=0, tiled=True),
        lax.all_gather(final_up, "fsdp", axis=0, tiled=True),
        lax.all_gather(final_down, "fsdp", axis=0, tiled=True),
    )
    up_one, down_one, proj_in, proj_out, conv_in, conv_out, up_two, down_two = gathered
    stream = layer_input.reshape(rows, width)
    cotangent = out_grad.reshape(rows, width)
    branch_one, saved_one = feed_forward(stream, norm_gains[0], up_one, down_one)
    after_one = stream + 0.5 * branch_one
    normed, norm_back_two = jax.vjp(layer_norm, after_one, norm_gains[1])
    normed_two = normed.astype(jnp.bfloat16)
    projected = jnp.einsum("nd,dke->nke", normed_two, proj_in, preferred_element_type=jnp.float32)
    local_width = projected.shape[2]
    heads = local_width // HEAD
    split = projected.reshape(batch, frames, 3, heads, HEAD)

    def rotate_pair(query_raw, key_raw):
        return (rotary(query_raw, place) * HEAD ** (-0.5), rotary(key_raw, place))

    (query_rot, key_rot), rotate_back = jax.vjp(rotate_pair, split[:, :, 0], split[:, :, 1])
    query_low = query_rot.astype(jnp.bfloat16)
    joined = jnp.concatenate(
        [
            key_rot.astype(jnp.bfloat16).reshape(batch, frames, local_width),
            split[:, :, 2].astype(jnp.bfloat16).reshape(batch, frames, local_width),
        ],
        -1,
    )
    joined_all = lax.all_gather(joined, "ctx", axis=1, tiled=True)
    mixed, log_total = lax.map(attend_one, (query_low, joined_all, lengths))
    mixed_rows = mixed.reshape(rows, local_width)
    after_two = after_one + tensor_total(product_rows(mixed_rows, proj_out))
    normed, norm_back_three = jax.vjp(layer_norm, after_two, norm_gains[2])
    normed_three = normed.astype(jnp.bfloat16)
    gates = jnp.einsum("nd,dke->nke", normed_three, conv_in, preferred_element_type=jnp.float32)

    def gate_linear(values):
        return values[:, 0] * jax.nn.sigmoid(values[:, 1]) * live_rows

    gated, gate_back = jax.vjp(gate_linear, gates)
    channels = gated.shape[1]
    gated_low = gated.astype(jnp.bfloat16).reshape(batch, frames, channels)
    reach = KERNEL // 2
    padded = with_halo(gated_low, (("ctx", 1),), reach)
    filtered = jnp.zeros((batch, frames, channels), jnp.float32)
    for offset in range(KERNEL):
        filtered = filtered + depth_kernel[offset] * padded[:, offset : offset + frames].astype(
            jnp.float32
        )
    sums = lax.psum(
        (
            jnp.sum(live_cube * filtered, (0, 1)),
            jnp.sum(live_cube * filtered * filtered, (0, 1)),
            jnp.sum(live),
        ),
        ("fsdp", "ctx"),
    )
    count = sums[2]
    mean = sums[0] / count
    variance = sums[1] / count - mean * mean
    rescale = lax.rsqrt(variance + norm_eps)
    unit = (filtered - mean) * rescale
    shifted = unit * batch_norm[0] + batch_norm[1]
    active, active_back = jax.vjp(swish, shifted.reshape(rows, channels))
    active_low = active.astype(jnp.bfloat16)
    after_three = after_two + tensor_total(product_rows(active_low, conv_out))
    branch_four, saved_four = feed_forward(after_three, norm_gains[3], up_two, down_two)
    after_four = after_three + 0.5 * branch_four
    result, final_back = jax.vjp(layer_norm, after_four, norm_gains[4])
    grad_four, gain_five = final_back(cotangent)
    stream_grad, gain_four, up_two_grad, down_two_grad = feed_backward(
        0.5 * grad_four, saved_four, up_two, down_two
    )
    grad_three = grad_four + stream_grad
    branch_low = grad_three.astype(jnp.bfloat16)
    conv_out_grad = product_cols(branch_low, active_low)
    shifted_grad = active_back(jnp.dot(branch_low, conv_out, preferred_element_type=jnp.float32))[
        0
    ].reshape(batch, frames, channels)
    bias_sum, scale_sum = lax.psum(
        (jnp.sum(shifted_grad, (0, 1)), jnp.sum(shifted_grad * unit, (0, 1))), ("fsdp", "ctx")
    )
    var_grad = -0.5 * rescale * rescale * batch_norm[0] * scale_sum
    first_grad = (-rescale * batch_norm[0] * bias_sum - 2.0 * mean * var_grad) / count
    second_grad = var_grad / count
    filtered_grad = (
        rescale * batch_norm[0] * shifted_grad
        + live_cube * (first_grad + 2.0 * filtered * second_grad)
    ).astype(jnp.bfloat16)
    padded_grad = with_halo(filtered_grad, (("ctx", 1),), reach)
    filtered_wide = filtered_grad.astype(jnp.float32)
    gated_grad = jnp.zeros((batch, frames, channels), jnp.float32)
    kernel_terms = []
    for offset in range(KERNEL):
        start = 2 * reach - offset
        gated_grad = gated_grad + depth_kernel[offset] * padded_grad[
            :, start : start + frames
        ].astype(jnp.float32)
        kernel_terms.append(
            jnp.sum(filtered_wide * padded[:, offset : offset + frames].astype(jnp.float32), (0, 1))
        )
    kernel_local = jnp.stack(kernel_terms)
    gates_grad = gate_back(gated_grad.reshape(rows, channels))[0].astype(jnp.bfloat16)
    conv_in_grad = jnp.einsum(
        "nd,nke->dke", normed_three, gates_grad, preferred_element_type=jnp.float32
    )
    normed_grad = tensor_total(
        jnp.einsum("nke,dke->nd", gates_grad, conv_in, preferred_element_type=jnp.float32)
    )
    stream_grad, gain_three = norm_back_three(normed_grad)
    grad_two = grad_three + stream_grad
    branch_low = grad_two.astype(jnp.bfloat16)
    proj_out_grad = product_cols(branch_low, mixed_rows)
    mixed_grad = (
        jnp.dot(branch_low, proj_out, preferred_element_type=jnp.float32)
        .astype(jnp.bfloat16)
        .reshape(batch, frames, heads, HEAD)
    )
    query_grad, joined_grad = lax.map(
        attend_back, (query_low, joined_all, lengths, log_total, mixed_grad)
    )
    joined_local = lax.psum_scatter(
        joined_grad.astype(jnp.bfloat16), "ctx", scatter_dimension=1, tiled=True
    ).astype(jnp.float32)
    key_grad = joined_local[..., :local_width].reshape(batch, frames, heads, HEAD)
    value_grad = joined_local[..., local_width:].reshape(batch, frames, heads, HEAD)
    query_raw_grad, key_raw_grad = rotate_back((query_grad, key_grad))
    proj_grad = (
        jnp.stack([query_raw_grad, key_raw_grad, value_grad], 2)
        .reshape(rows, 3, local_width)
        .astype(jnp.bfloat16)
    )
    proj_in_grad = jnp.einsum(
        "nd,nke->dke", normed_two, proj_grad, preferred_element_type=jnp.float32
    )
    normed_grad = tensor_total(
        jnp.einsum("nke,dke->nd", proj_grad, proj_in, preferred_element_type=jnp.float32)
    )
    stream_grad, gain_two = norm_back_two(normed_grad)
    grad_one = grad_two + stream_grad
    stream_grad, gain_one, up_one_grad, down_one_grad = feed_backward(
        0.5 * grad_one, saved_one, up_one, down_one
    )
    input_grad = grad_one + stream_grad
    gain_terms = jnp.stack([gain_one, gain_two, gain_three, gain_four, gain_five])
    gain_total, kernel_total = lax.psum((gain_terms, kernel_local), ("fsdp", "ctx"))
    weight_grads = (
        up_one_grad,
        down_one_grad,
        proj_in_grad,
        proj_out_grad,
        conv_in_grad,
        conv_out_grad,
        up_two_grad,
        down_two_grad,
    )
    owned = (
        lax.psum_scatter(
            weight_grads[0].astype(jnp.bfloat16), "fsdp", scatter_dimension=0, tiled=True
        ).astype(jnp.float32),
        lax.psum_scatter(
            weight_grads[1].astype(jnp.bfloat16), "fsdp", scatter_dimension=0, tiled=True
        ).astype(jnp.float32),
        lax.psum_scatter(
            weight_grads[2].astype(jnp.bfloat16), "fsdp", scatter_dimension=0, tiled=True
        ).astype(jnp.float32),
        lax.psum_scatter(
            weight_grads[3].astype(jnp.bfloat16), "fsdp", scatter_dimension=0, tiled=True
        ).astype(jnp.float32),
        lax.psum_scatter(
            weight_grads[4].astype(jnp.bfloat16), "fsdp", scatter_dimension=0, tiled=True
        ).astype(jnp.float32),
        lax.psum_scatter(
            weight_grads[5].astype(jnp.bfloat16), "fsdp", scatter_dimension=0, tiled=True
        ).astype(jnp.float32),
        lax.psum_scatter(
            weight_grads[6].astype(jnp.bfloat16), "fsdp", scatter_dimension=0, tiled=True
        ).astype(jnp.float32),
        lax.psum_scatter(
            weight_grads[7].astype(jnp.bfloat16), "fsdp", scatter_dimension=0, tiled=True
        ).astype(jnp.float32),
    )
    owned = (
        lax.psum(owned[0].astype(jnp.bfloat16), "ctx").astype(jnp.float32),
        lax.psum(owned[1].astype(jnp.bfloat16), "ctx").astype(jnp.float32),
        lax.psum(owned[2].astype(jnp.bfloat16), "ctx").astype(jnp.float32),
        lax.psum(owned[3].astype(jnp.bfloat16), "ctx").astype(jnp.float32),
        lax.psum(owned[4].astype(jnp.bfloat16), "ctx").astype(jnp.float32),
        lax.psum(owned[5].astype(jnp.bfloat16), "ctx").astype(jnp.float32),
        lax.psum(owned[6].astype(jnp.bfloat16), "ctx").astype(jnp.float32),
        lax.psum(owned[7].astype(jnp.bfloat16), "ctx").astype(jnp.float32),
    )
    return (
        result.reshape(batch, frames, width),
        input_grad.reshape(batch, frames, width),
        gain_total,
        owned[0],
        owned[1],
        owned[2],
        owned[3],
        owned[4],
        owned[5],
        kernel_total,
        jnp.stack([scale_sum, bias_sum]),
        owned[6],
        owned[7],
    )


def solution(mesh):
    placed = (
        P("fsdp", "ctx", None),
        P("fsdp", "ctx", None),
        P("fsdp"),
        P(),
        P("fsdp", "tp"),
        P("fsdp", "tp"),
        P("fsdp", None, "tp"),
        P("fsdp", "tp"),
        P("fsdp", None, "tp"),
        P("fsdp", "tp"),
        P(None, "tp"),
        P(None, "tp"),
        P("fsdp", "tp"),
        P("fsdp", "tp"),
    )
    return jax.shard_map(
        per_device,
        mesh=mesh,
        in_specs=placed,
        out_specs=(
            P("fsdp", "ctx", None),
            P("fsdp", "ctx", None),
            P(),
            P("fsdp", "tp"),
            P("fsdp", "tp"),
            P("fsdp", None, "tp"),
            P("fsdp", "tp"),
            P("fsdp", None, "tp"),
            P("fsdp", "tp"),
            P(None, "tp"),
            P(None, "tp"),
            P("fsdp", "tp"),
            P("fsdp", "tp"),
        ),
        check_vma=False,
    )
```

profile of v0, /device:TPU:0, one launch (start us, length us, event | category | flops | bytes accessed | tf_op | source)
XLA Modules:
  0.0 1221.6 jit_solution(15383758015206890385)
XLA Ops:
  11.6 28.7 %all-gather.6.cloned.1.call-done = bf16[512,1024]{1,0:T(8,128)(2,1)} async-done(((bf16[128,1024]{1,0:T(8,128)(2,1)}), bf16[512,1024]{1,0:T(8,128)(2,1)}) %all-gather.6.cloned.1.call-update) | async-done | bytes 1048592 | tf_op jit(solution)/shard_map/all_gather | solution.py:159
  40.3 5.1 multiply_convert_fusion.2
  45.4 23.9 %all-gather.8.cloned.1.call-done = bf16[512,1024]{1,0:T(8,128)(2,1)} async-done(((bf16[128,1024]{1,0:T(8,128)(2,1)}), bf16[512,1024]{1,0:T(8,128)(2,1)}) %all-gather.8.cloned.1.call-update) | async-done | bytes 1048592 | tf_op jit(solution)/shard_map/all_gather | solution.py:160
  69.3 4.1 convolution_convert_fusion.10
  74.3 17.5 %all_gather.29 = bf16[512,3,256]{0,2,1:T(8,128)(2,1)S(1)} all-gather(bf16[128,3,256]{0,2,1:T(8,128)(2,1)S(1)} %copy.27), channel_id=1, replica_groups=mesh['fsdp'=4,'ctx'=4,'tp'=2] {'fsdp'}, dimensions={0}, use_global_device_ids=true | all-gather | bytes 983040 | tf_op jit(solution)/shard_map/all_gather | solution.py:161
  91.8 21.3 %all-reduce.20.cloned.1.call-done = bf16[1024,512]{1,0:T(8,128)(2,1)} async-done(((bf16[1024,512]{1,0:T(8,128)(2,1)}), bf16[1024,512]{1,0:T(8,128)(2,1)}) %all-reduce.20.cloned.1.call-update) | async-done | bytes 1048592 | tf_op jit(solution)/shard_map/psum | solution.py:53
  119.6 14.0 %all_gather.31 = bf16[512,256]{1,0:T(8,128)(2,1)S(1)} all-gather(bf16[128,256]{1,0:T(8,128)(2,1)S(1)} %copy-done.69), channel_id=1, replica_groups=mesh['fsdp'=4,'ctx'=4,'tp'=2] {'fsdp'}, dimensions={0}, use_global_device_ids=true | all-gather | bytes 327680 | tf_op jit(solution)/shard_map/all_gather | solution.py:162
  133.7 19.9 %all-gather.10.cloned.1.call-done = bf16[1,4096,512]{1,2,0:T(8,128)(2,1)} async-done(((bf16[1,1024,512]{1,2,0:T(8,128)(2,1)}), bf16[1,4096,512]{1,2,0:T(8,128)(2,1)}) %all-gather.10.cloned.1.call-update) | async-done | bytes 4194320 | tf_op jit(solution)/shard_map/all_gather | solution.py:192
  153.5 4.1 fusion.240
  157.6 23.1 %select_reduce_fusion = (f32[4,1024]{1,0:T(4,128)S(1)}, f32[4,1024,4096]{2,1,0:T(8,128)}) fusion(pred[4096]{0:T(1024)(128)(4,1)S(1)} %iota_compare_fusion, bf16[4096,4,64]{0,2,1:T(8,128)(2,1)S(1)} %bitcast.233, f32[1024,4,32]{0,2,1:T(8,128)S(1)} %get-tuple-element.156, f32[1024,4,32]{0,2,1:T(8,128)S(1)} %get-tuple-element.155), kind=kOutput, calls=%fused_computation.6 | convolution fusion | flops 2181820416 | bytes 70275072 | tf_op jit(solution)/shard_map/while/body/eval_jaxpr/fhe,lhe->hfl/dot_general | solution.py:99
  180.8 21.4 %fusion = f32[4,1024]{1,0:T(4,128)S(1)} fusion(f32[4,1024,4096]{2,1,0:T(8,128)} %get-tuple-element.214, f32[4,1024]{1,0:T(4,128)S(1)} %get-tuple-element.213, pred[4096]{0:T(1024)(128)(4,1)S(1)} %iota_compare_fusion), kind=kLoop, calls=%fused_computation.5 | loop fusion | flops 50327552 | bytes 67145728 | tf_op jit(solution)/shard_map/while/body/eval_jaxpr/reduce_sum | solution.py:110
  202.2 24.0 %fusion.33 = bf16[4,64,1024]{2,1,0:T(8,128)(2,1)S(1)} fusion(bf16[4096,4,64]{0,2,1:T(8,128)(2,1)S(1)} %bitcast.241, f32[4,1024,4096]{2,1,0:T(8,128)} %get-tuple-element.214, f32[4,1024]{1,0:T(4,128)S(1)} %fusion, f32[4,1024]{1,0:T(4,128)S(1)} %get-tuple-element.213, pred[4096]{0:T(1024)(128)(4,1)S(1)} %iota_compare_fusion), kind=kOutput, calls=%fused_computation.222 | convolution fusion | flops 2214854656 | bytes 69767168 | tf_op jit(solution)/shard_map/while/body/eval_jaxpr/hfl,lhe->fhe/dot_general | solution.py:112
  227.8 16.0 %all_gather.32 = bf16[512,2,256]{2,0,1:T(8,128)(2,1)S(1)} all-gather(bf16[128,2,256]{2,0,1:T(8,128)(2,1)S(1)} %copy.28), channel_id=1, replica_groups=mesh['fsdp'=4,'ctx'=4,'tp'=2] {'fsdp'}, dimensions={0}, use_global_device_ids=true | all-gather | bytes 655360 | tf_op jit(solution)/shard_map/all_gather | solution.py:163
  245.1 22.8 %all-reduce.22.cloned.1.call-done = bf16[1024,512]{1,0:T(8,128)(2,1)} async-done(((bf16[1024,512]{1,0:T(8,128)(2,1)}), bf16[1024,512]{1,0:T(8,128)(2,1)}) %all-reduce.22.cloned.1.call-update) | async-done | bytes 1048592 | tf_op jit(solution)/shard_map/psum | solution.py:53
  276.0 15.4 %all_gather.33 = bf16[512,256]{1,0:T(8,128)(2,1)} all-gather(bf16[128,256]{1,0:T(8,128)(2,1)S(1)} %copy-done.70), channel_id=1, replica_groups=mesh['fsdp'=4,'ctx'=4,'tp'=2] {'fsdp'}, dimensions={0}, use_global_device_ids=true | all-gather | bytes 327680 | tf_op jit(solution)/shard_map/all_gather | solution.py:164
  292.3 9.3 fusion.64
  301.6 32.1 %all-reduce.8 = (f32[256]{0:T(256)S(1)}, f32[]{:T(128)}, f32[256]{0:T(256)S(1)}) all-reduce(f32[256]{0:T(256)} %get-tuple-element.109, f32[]{:T(128)} %fusion.202, f32[256]{0:T(256)} %get-tuple-element.108), channel_id=1, replica_groups=mesh['fsdp'=4,'ctx'=4,'tp'=2] {'fsdp','ctx'}, use_global_device_ids=true, to_apply=%region_11.12 | all-reduce | flops 513 | bytes 4104 | tf_op jit(solution)/shard_map/psum | solution.py:213
  334.9 2.8 convolution_convert_fusion.8
  339.3 35.0 %all-reduce.24.cloned.1.call-done = bf16[1024,512]{1,0:T(8,128)(2,1)} async-done(((bf16[1024,512]{1,0:T(8,128)(2,1)}), bf16[1024,512]{1,0:T(8,128)(2,1)}) %all-reduce.24.cloned.1.call-update) | async-done | bytes 1048592 | tf_op jit(solution)/shard_map/psum | solution.py:53
  377.6 26.3 %all-gather.12.cloned.1.call-done = bf16[512,1024]{1,0:T(8,128)(2,1)} async-done(((bf16[128,1024]{1,0:T(8,128)(2,1)}), bf16[512,1024]{1,0:T(8,128)(2,1)}) %all-gather.12.cloned.1.call-update) | async-done | bytes 1048592 | tf_op jit(solution)/shard_map/all_gather | solution.py:165
  403.9 6.1 multiply_convert_fusion.1
  410.0 22.9 %all-gather.14.cloned.1.call-done = bf16[512,1024]{1,0:T(8,128)(2,1)} async-done(((bf16[128,1024]{1,0:T(8,128)(2,1)}), bf16[512,1024]{1,0:T(8,128)(2,1)}) %all-gather.14.cloned.1.call-update) | async-done | bytes 1048592 | tf_op jit(solution)/shard_map/all_gather | solution.py:166
  432.9 4.1 convolution_convert_fusion.7
  437.1 39.6 %all-reduce.26.cloned.1.call-done = bf16[1024,512]{1,0:T(8,128)(2,1)} async-done(((bf16[1024,512]{1,0:T(8,128)(2,1)}), bf16[1024,512]{1,0:T(8,128)(2,1)}) %all-reduce.26.cloned.1.call-update) | async-done | bytes 1048592 | tf_op jit(solution)/shard_map/psum | solution.py:53
  485.5 2.5 fusion.11
  492.2 39.8 %all-reduce.28.cloned.1.call-done = bf16[1024,512]{1,0:T(8,128)(2,1)} async-done(((bf16[1024,512]{1,0:T(8,128)(2,1)}), bf16[1024,512]{1,0:T(8,128)(2,1)}) %all-reduce.28.cloned.1.call-update) | async-done | bytes 1048592 | tf_op jit(solution)/shard_map/psum | solution.py:53
  532.0 2.6 fusion.26
  538.0 2.3 fusion.121
  542.2 33.7 %all-reduce.7 = (f32[256]{0:T(256)}, f32[256]{0:T(256)}) all-reduce(f32[256]{0:T(256)} %get-tuple-element.217, f32[256]{0:T(256)} %reduce_sum.647), channel_id=1, replica_groups=mesh['fsdp'=4,'ctx'=4,'tp'=2] {'fsdp','ctx'}, use_global_device_ids=true, to_apply=%region_30.31 | all-reduce | flops 512 | bytes 4096 | tf_op jit(solution)/shard_map/psum | solution.py:243
  577.5 5.4 fusion.115
  584.2 3.0 collective-permute-start.3
  588.1 9.3 fusion.67
  600.7 38.1 %all-reduce.30.cloned.1.call-done = bf16[1024,512]{1,0:T(8,128)(2,1)} async-done(((bf16[1024,512]{1,0:T(8,128)(2,1)}), bf16[1024,512]{1,0:T(8,128)(2,1)}) %all-reduce.30.cloned.1.call-update) | async-done | bytes 1048592 | tf_op jit(solution)/shard_map/psum | solution.py:53
  645.3 23.9 %fusion.6 = bf16[4,64,4096]{2,1,0:T(8,128)(2,1)S(1)} fusion(bf16[1024,4,64]{0,2,1:T(8,128)(2,1)S(1)} %bitcast.237, f32[4,1024,4096]{2,1,0:T(8,128)} %get-tuple-element.214, f32[4,1024]{1,0:T(4,128)S(1)} %log_add_fusion, pred[4096]{0:T(1024)(128)(4,1)S(1)} %iota_compare_fusion), kind=kOutput, calls=%fused_computation.45 | convolution fusion | flops 2198863872 | bytes 69750784 | tf_op jit(solution)/shard_map/while/body/eval_jaxpr/hfl,fhe->lhe/dot_general | solution.py:126
  669.2 45.1 %multiply_reduce_fusion = (f32[4,1024]{1,0:T(4,128)S(1)}, f32[4,1024,4096]{2,1,0:T(8,128)}) fusion(f32[4,1024,4096]{2,1,0:T(8,128)} %get-tuple-element.214, f32[4,1024]{1,0:T(4,128)S(1)} %log_add_fusion, pred[4096]{0:T(1024)(128)(4,1)S(1)} %iota_compare_fusion, bf16[1024,4,64]{0,2,1:T(8,128)(2,1)S(1)} %bitcast.238, bf16[4096,4,64]{0,2,1:T(8,128)(2,1)S(1)} %bitcast.242), kind=kOutput, calls=%fused_computation.1 | convolution fusion | flops 2214588416 | bytes 136876032 | tf_op jit(solution)/shard_map/while/body/eval_jaxpr/fhe,lhe->hfl/dot_general | solution.py:121
  714.2 2.5 copy.30
  716.8 52.7 %multiply_convert_fusion = bf16[4,1024,4096]{2,1,0:T(8,128)(2,1)} fusion(f32[4,1024,4096]{2,1,0:T(8,128)} %get-tuple-element.220, f32[4,1024,4096]{2,1,0:T(8,128)} %get-tuple-element.214, f32[4,1024]{1,0:T(4,128)S(1)} %get-tuple-element.219, f32[4,1024]{1,0:T(4,128)S(1)} %log_add_fusion, pred[4096]{0:T(1024)(128)(4,1)S(1)} %iota_compare_fusion), kind=kLoop, calls=%fused_computation | loop fusion | flops 83886080 | bytes 167809024 | tf_op jit(solution)/shard_map/while/body/eval_jaxpr/convert_element_type | solution.py:123
  769.5 13.8 %convolution_convert_fusion = bf16[4,64,4096]{2,1,0:T(8,128)(2,1)S(1)} fusion(bf16[4,1024,4096]{2,1,0:T(8,128)(2,1)} %multiply_convert_fusion, f32[1024,4,32]{0,2,1:T(8,128)S(1)} %copy-done.36, f32[1024,4,32]{0,2,1:T(8,128)S(1)} %copy-done.34), kind=kOutput, calls=%fused_computation.46 | convolution fusion | flops 2149318656 | bytes 36700160 | tf_op jit(solution)/shard_map/while/body/eval_jaxpr/hfl,fhe->lhe/dot_general | solution.py:125
  783.3 2.5 copy.29
  785.8 4.5 pad_maximum_fusion
  791.9 17.0 %fusion.32 = f32[1,1024,4,64]{1,3,2,0:T(8,128)S(1)} fusion(bf16[4096,4,64]{0,2,1:T(8,128)(2,1)S(1)} %bitcast.234, bf16[4,1024,4096]{2,1,0:T(8,128)(2,1)} %multiply_convert_fusion), kind=kOutput, calls=%fused_computation.188 | convolution fusion | flops 2147745792 | bytes 36700160 | tf_op jit(solution)/shard_map/while/body/eval_jaxpr/hfl,lhe->fhe/dot_general | solution.py:124
  808.9 26.1 %reduce-scatter.10.cloned.1.call-done = bf16[1,1024,512]{2,1,0:T(8,128)(2,1)} async-done(((bf16[1,4096,512]{2,1,0:T(8,128)(2,1)}), bf16[1,1024,512]{2,1,0:T(8,128)(2,1)}) %reduce-scatter.10.cloned.1.call-update) | async-done | bytes 1048592 | tf_op jit(solution)/shard_map/reduce_scatter | solution.py:285
  840.0 3.4 bitcast_convert_fusion
  843.4 40.2 %all-reduce.32.cloned.1.call-done = bf16[1024,512]{1,0:T(8,128)(2,1)} async-done(((bf16[1024,512]{1,0:T(8,128)(2,1)}), bf16[1024,512]{1,0:T(8,128)(2,1)}) %all-reduce.32.cloned.1.call-update) | async-done | bytes 1048592 | tf_op jit(solution)/shard_map/psum | solution.py:53
  894.0 2.3 convolution_convert_fusion.5
  896.5 3.1 convolution_convert_fusion.14
  899.8 4.0 convolution_convert_fusion.2
  903.9 4.7 convolution_convert_fusion.1
  908.9 3.4 convolution_convert_fusion.13
  912.5 3.0 convolution_convert_fusion.15
  915.6 3.3 convolution_convert_fusion.11
  919.0 4.7 convolution_convert_fusion.4
  923.9 4.0 convolution_convert_fusion.3
  933.1 3.5 all-reduce.34.cloned.1.call-done
  938.6 20.8 %reduce-scatter.22.cloned.1.call-done = bf16[128,256]{1,0:T(8,128)(2,1)} async-done(((bf16[512,256]{1,0:T(8,128)(2,1)}), bf16[128,256]{1,0:T(8,128)(2,1)}) %reduce-scatter.22.cloned.1.call-update) | async-done | bytes 65552 | tf_op jit(solution)/shard_map/reduce_scatter | solution.py:336
  959.3 27.7 %reduce-scatter.24.cloned.1.call-done = bf16[128,1024]{1,0:T(8,128)(2,1)} async-done(((bf16[512,1024]{1,0:T(8,128)(2,1)}), bf16[128,1024]{1,0:T(8,128)(2,1)}) %reduce-scatter.24.cloned.1.call-update) | async-done | bytes 262160 | tf_op jit(solution)/shard_map/reduce_scatter | solution.py:339
  987.0 27.9 %reduce-scatter.26.cloned.1.call-done = bf16[128,1024]{1,0:T(8,128)(2,1)} async-done(((bf16[512,1024]{1,0:T(8,128)(2,1)}), bf16[128,1024]{1,0:T(8,128)(2,1)}) %reduce-scatter.26.cloned.1.call-update) | async-done | bytes 262160 | tf_op jit(solution)/shard_map/reduce_scatter | solution.py:342
  1015.0 22.5 %reduce-scatter.20.cloned.1.call-done = bf16[128,2,256]{2,0,1:T(8,128)(2,1)} async-done(((bf16[512,2,256]{2,0,1:T(8,128)(2,1)}), bf16[128,2,256]{2,0,1:T(8,128)(2,1)}) %reduce-scatter.20.cloned.1.call-update) | async-done | bytes 131088 | tf_op jit(solution)/shard_map/reduce_scatter | solution.py:333
  1037.5 21.1 %reduce-scatter.18.cloned.1.call-done = bf16[128,256]{1,0:T(8,128)(2,1)} async-done(((bf16[512,256]{1,0:T(8,128)(2,1)}), bf16[128,256]{1,0:T(8,128)(2,1)}) %reduce-scatter.18.cloned.1.call-update) | async-done | bytes 65552 | tf_op jit(solution)/shard_map/reduce_scatter | solution.py:330
  1058.6 23.5 %reduce-scatter.16.cloned.1.call-done = bf16[128,3,256]{2,0,1:T(8,128)(2,1)} async-done(((bf16[512,3,256]{2,0,1:T(8,128)(2,1)}), bf16[128,3,256]{2,0,1:T(8,128)(2,1)}) %reduce-scatter.16.cloned.1.call-update) | async-done | bytes 196624 | tf_op jit(solution)/shard_map/reduce_scatter | solution.py:327
  1082.1 29.1 %reduce-scatter.12.cloned.1.call-done = bf16[128,1024]{1,0:T(8,128)(2,1)} async-done(((bf16[512,1024]{1,0:T(8,128)(2,1)}), bf16[128,1024]{1,0:T(8,128)(2,1)}) %reduce-scatter.12.cloned.1.call-update) | async-done | bytes 262160 | tf_op jit(solution)/shard_map/reduce_scatter | solution.py:321
  1111.3 28.1 %reduce-scatter.14.cloned.1.call-done = bf16[128,1024]{1,0:T(8,128)(2,1)} async-done(((bf16[512,1024]{1,0:T(8,128)(2,1)}), bf16[128,1024]{1,0:T(8,128)(2,1)}) %reduce-scatter.14.cloned.1.call-update) | async-done | bytes 262160 | tf_op jit(solution)/shard_map/reduce_scatter | solution.py:324
  1140.8 59.7 %all-reduce.6 = (f32[5,512]{1,0:T(8,128)}, f32[31,256]{1,0:T(8,128)}) all-reduce(f32[5,512]{1,0:T(8,128)S(1)} %stack.128, f32[31,256]{1,0:T(8,128)S(1)} %stack.160), channel_id=1, replica_groups=mesh['fsdp'=4,'ctx'=4,'tp'=2] {'fsdp','ctx'}, use_global_device_ids=true, to_apply=%region_47.48 | all-reduce | flops 10496 | bytes 83968 | tf_op jit(solution)/shard_map/psum | solution.py:309
  1200.5 3.3 add_bitcast_fusion
  (449 shorter events, 96.4 us)
Async XLA Ops:
  7.2 33.1 %all-gather.6.cloned.1.call-start = ((), (), s32[]{:S(2)}) async-start(), calls=%async_computation.9 | async-start | bytes 1310720 | tf_op jit(solution)/shard_map/all_gather | solution.py:159
  7.9 61.3 %all-gather.8.cloned.1.call-start = ((), (), s32[]{:S(2)}) async-start(), calls=%async_computation.10 | async-start | bytes 1310720 | tf_op jit(solution)/shard_map/all_gather | solution.py:160
  8.7 104.4 %all-reduce.20.cloned.1.call-start = ((), (), s32[]{:S(2)}) async-start(), calls=%async_computation.11 | async-start | bytes 2097152 | tf_op jit(solution)/shard_map/psum | solution.py:53
  10.6 34.8 %copy-start.65 = (f32[1024]{0:T(1024)}, f32[1024]{0:T(1024)S(1)}, u32[]{:S(2)}) copy-start(f32[1024]{0:T(1024)S(1)} %broadcast_multiply_fusion.4) | copy-start | bytes 12292
  11.0 34.4 %copy-start.83 = (f32[1024]{0:T(1024)}, f32[1024]{0:T(1024)S(1)}, u32[]{:S(2)}) copy-start(f32[1024]{0:T(1024)S(1)} %multiply_reduce_fusion.6) | copy-start | bytes 12292
  11.6 104.2 %copy-start.75 = (f32[1,512]{1,0:T(1,128)}, f32[1,512]{1,0:T(1,128)S(1)}, u32[]{:S(2)}) copy-start(f32[1,512]{1,0:T(1,128)S(1)} %get-tuple-element.202) | copy-start | bytes 6148
  11.6 631.2 %copy-start.77 = (f32[1,512]{1,0:T(1,128)}, f32[1,512]{1,0:T(1,128)S(1)}, u32[]{:S(2)}) copy-start(f32[1,512]{1,0:T(1,128)S(1)} %get-tuple-element.201) | copy-start | bytes 6148
  73.4 80.1 %all-gather.10.cloned.1.call-start = ((), (), s32[]{:S(2)}) async-start(), calls=%async_computation.12 | async-start | bytes 5242880 | tf_op jit(solution)/shard_map/all_gather | solution.py:192
  74.2 43.1 %copy-start.43 = (f32[1024,32]{0,1:T(8,128)}, f32[1024,32]{0,1:T(8,128)S(1)}, u32[]{:S(2)}) copy-start(f32[1024,32]{0,1:T(8,128)S(1)} %get-tuple-element.205) | copy-start | bytes 393220
  74.2 43.1 %copy-start.45 = (f32[1024,32]{0,1:T(8,128)}, f32[1024,32]{0,1:T(8,128)S(1)}, u32[]{:S(2)}) copy-start(f32[1024,32]{0,1:T(8,128)S(1)} %get-tuple-element.206) | copy-start | bytes 393220
  117.6 40.0 %copy-start.33 = (f32[1024,4,32]{0,2,1:T(8,128)}, f32[1024,4,32]{0,2,1:T(8,128)S(1)}, u32[]{:S(2)}) copy-start(f32[1024,4,32]{0,2,1:T(8,128)S(1)} %get-tuple-element.155) | copy-start | bytes 1572868
  117.6 40.0 %copy-start.35 = (f32[1024,4,32]{0,2,1:T(8,128)}, f32[1024,4,32]{0,2,1:T(8,128)S(1)}, u32[]{:S(2)}) copy-start(f32[1024,4,32]{0,2,1:T(8,128)S(1)} %get-tuple-element.156) | copy-start | bytes 1572868
  118.9 149.0 %all-reduce.22.cloned.1.call-start = ((), (), s32[]{:S(2)}) async-start(), calls=%async_computation.13 | async-start | bytes 2097152 | tf_op jit(solution)/shard_map/psum | solution.py:53
  226.2 43.9 %copy-start.41 = (bf16[4,64,1024]{2,1,0:T(8,128)(2,1)}, bf16[4,64,1024]{2,1,0:T(8,128)(2,1)S(1)}, u32[]{:S(2)}) copy-start(bf16[4,64,1024]{2,1,0:T(8,128)(2,1)S(1)} %fusion.33) | copy-start | bytes 1572868
  227.7 146.6 %all-reduce.24.cloned.1.call-start = ((), (), s32[]{:S(2)}) async-start(), calls=%async_computation.14 | async-start | bytes 2097152 | tf_op jit(solution)/shard_map/psum | solution.py:53
  244.4 331.5 %copy-start.95 = (f32[1,256]{1,0:T(1,128)}, f32[1,256]{1,0:T(1,128)S(1)}, u32[]{:S(2)}) copy-start(f32[1,256]{1,0:T(1,128)S(1)} %get-tuple-element.209) | copy-start | bytes 3076
  245.1 47.1 %copy-start.97 = (f32[1,256]{1,0:T(1,128)}, f32[1,256]{1,0:T(1,128)S(1)}, u32[]{:S(2)}) copy-start(f32[1,256]{1,0:T(1,128)S(1)} %get-tuple-element.170) | copy-start | bytes 3076
  245.1 47.1 %copy-start.99 = (f32[1,256]{1,0:T(1,128)}, f32[1,256]{1,0:T(1,128)S(1)}, u32[]{:S(2)}) copy-start(f32[1,256]{1,0:T(1,128)S(1)} %get-tuple-element.171) | copy-start | bytes 3076
  245.1 47.1 %copy-start.101 = (f32[1,256]{1,0:T(1,128)}, f32[1,256]{1,0:T(1,128)S(1)}, u32[]{:S(2)}) copy-start(f32[1,256]{1,0:T(1,128)S(1)} %get-tuple-element.172) | copy-start | bytes 3076
  245.1 47.1 %copy-start.103 = (f32[1,256]{1,0:T(1,128)}, f32[1,256]{1,0:T(1,128)S(1)}, u32[]{:S(2)}) copy-start(f32[1,256]{1,0:T(1,128)S(1)} %get-tuple-element.173) | copy-start | bytes 3076
  270.1 372.7 %copy-start = (f32[1024,512]{1,0:T(8,128)}, f32[1024,512]{1,0:T(8,128)S(1)}, u32[]{:S(2)}) copy-start(f32[1024,512]{1,0:T(8,128)S(1)} %get-tuple-element.143) | copy-start | bytes 6291460
  270.1 372.7 %copy-start.58 = (f32[1024]{0:T(1024)}, f32[1024]{0:T(1024)S(1)}, u32[]{:S(2)}) copy-start(f32[1024]{0:T(1024)S(1)} %broadcast_multiply_fusion.2) | copy-start | bytes 12292
  270.6 372.2 %copy-start.73 = (f32[1024]{0:T(1024)}, f32[1024]{0:T(1024)S(1)}, u32[]{:S(2)}) copy-start(f32[1024]{0:T(1024)S(1)} %fusion.199) | copy-start | bytes 12292
  273.1 304.4 %copy-start.14 = (bf16[1,1024,256]{2,1,0:T(8,128)(2,1)}, bf16[1,1024,256]{2,1,0:T(8,128)(2,1)S(1)}, u32[]{:S(2)}) copy-start(bf16[1,1024,256]{2,1,0:T(8,128)(2,1)S(1)} %fusion.127) | copy-start | bytes 1572868
  273.1 19.0 %collective-permute-start = (bf16[1,15,256]{2,1,0:T(8,128)(2,1)S(1)}, bf16[1,15,256]{2,1,0:T(8,128)(2,1)S(1)}, u32[]{:S(2)}, u32[]{:S(2)}) collective-permute-start(bf16[1,15,256]{2,1,0:T(8,128)(2,1)S(1)} %get-tuple-element.163), channel_id=1, source_target_pairs={{0,2},{2,4},{4,6},{1,3},{3,5},{5,7},{8,10},{10,12},{12,14},{9,11},... | collective-permute-start | bytes 23048 | tf_op jit(solution)/shard_map/ppermute | solution.py:22
  274.7 17.4 %collective-permute-start.1 = (bf16[1,15,256]{2,1,0:T(8,128)(2,1)S(1)}, bf16[1,15,256]{2,1,0:T(8,128)(2,1)S(1)}, u32[]{:S(2)}, u32[]{:S(2)}) collective-permute-start(bf16[1,15,256]{2,1,0:T(8,128)(2,1)S(1)} %get-tuple-element.164), channel_id=1, source_target_pairs={{2,0},{4,2},{6,4},{3,1},{5,3},{7,5},{10,8},{12,10},{14,12},{11,9},... | collective-permute-start | bytes 23048 | tf_op jit(solution)/shard_map/ppermute | solution.py:24
  292.1 45.6 %copy-start.62 = (bf16[1,15,256]{2,1,0:T(8,128)(2,1)}, bf16[1,15,256]{2,1,0:T(8,128)(2,1)S(1)}, u32[]{:S(2)}) copy-start(bf16[1,15,256]{2,1,0:T(8,128)(2,1)S(1)} %collective-permute-done) | copy-start | bytes 23044
  292.1 285.4 %copy-start.60 = (bf16[1,15,256]{2,1,0:T(8,128)(2,1)}, bf16[1,15,256]{2,1,0:T(8,128)(2,1)S(1)}, u32[]{:S(2)}) copy-start(bf16[1,15,256]{2,1,0:T(8,128)(2,1)S(1)} %collective-permute-done.1) | copy-start | bytes 23044
  337.8 66.2 %all-gather.12.cloned.1.call-start = ((), (), s32[]{:S(2)}) async-start(), calls=%async_computation.15 | async-start | bytes 1310720 | tf_op jit(solution)/shard_map/all_gather | solution.py:165
  338.5 94.4 %all-gather.14.cloned.1.call-start = ((), (), s32[]{:S(2)}) async-start(), calls=%async_computation.16 | async-start | bytes 1310720 | tf_op jit(solution)/shard_map/all_gather | solution.py:166
  339.3 137.4 %all-reduce.26.cloned.1.call-start = ((), (), s32[]{:S(2)}) async-start(), calls=%async_computation.17 | async-start | bytes 2097152 | tf_op jit(solution)/shard_map/psum | solution.py:53
  375.9 160.8 %copy-start.67 = (f32[1024]{0:T(1024)}, f32[1024]{0:T(1024)S(1)}, u32[]{:S(2)}) copy-start(f32[1024]{0:T(1024)S(1)} %broadcast_multiply_fusion.1) | copy-start | bytes 12292
  377.6 159.1 %copy-start.81 = (f32[1024]{0:T(1024)}, f32[1024]{0:T(1024)S(1)}, u32[]{:S(2)}) copy-start(f32[1024]{0:T(1024)S(1)} %fusion.200) | copy-start | bytes 12292
  437.0 95.0 %all-reduce.28.cloned.1.call-start = ((), (), s32[]{:S(2)}) async-start(), calls=%async_computation.18 | async-start | bytes 2097152 | tf_op jit(solution)/shard_map/psum | solution.py:53
  483.8 52.9 %copy-start.93 = (f32[1024]{0:T(1024)}, f32[1024]{0:T(1024)S(1)}, u32[]{:S(2)}) copy-start(f32[1024]{0:T(1024)S(1)} %negate_multiply_fusion.4) | copy-start | bytes 12292
  491.7 147.0 %all-reduce.30.cloned.1.call-start = ((), (), s32[]{:S(2)}) async-start(), calls=%async_computation.19 | async-start | bytes 2097152 | tf_op jit(solution)/shard_map/psum | solution.py:53
  540.2 47.8 %copy-start.98 = (f32[1,256]{1,0:T(1,128)S(1)}, f32[1,256]{1,0:T(1,128)}, u32[]{:S(2)}) copy-start(f32[1,256]{1,0:T(1,128)} %copy-done.97) | copy-start | bytes 3076
  540.2 47.8 %copy-start.100 = (f32[1,256]{1,0:T(1,128)S(1)}, f32[1,256]{1,0:T(1,128)}, u32[]{:S(2)}) copy-start(f32[1,256]{1,0:T(1,128)} %copy-done.99) | copy-start | bytes 3076
  540.2 47.8 %copy-start.102 = (f32[1,256]{1,0:T(1,128)S(1)}, f32[1,256]{1,0:T(1,128)}, u32[]{:S(2)}) copy-start(f32[1,256]{1,0:T(1,128)} %copy-done.101) | copy-start | bytes 3076
  540.3 47.8 %copy-start.104 = (f32[1,256]{1,0:T(1,128)S(1)}, f32[1,256]{1,0:T(1,128)}, u32[]{:S(2)}) copy-start(f32[1,256]{1,0:T(1,128)} %copy-done.103) | copy-start | bytes 3076
  540.3 47.8 %copy-start.106 = (f32[1,256]{1,0:T(1,128)S(1)}, f32[1,256]{1,0:T(1,128)}, u32[]{:S(2)}) copy-start(f32[1,256]{1,0:T(1,128)} %get-tuple-element.174) | copy-start | bytes 3076
  540.3 47.8 %copy-start.108 = (f32[1,256]{1,0:T(1,128)S(1)}, f32[1,256]{1,0:T(1,128)}, u32[]{:S(2)}) copy-start(f32[1,256]{1,0:T(1,128)} %get-tuple-element.175) | copy-start | bytes 3076
  582.9 4.3 collective-permute-start.2
  584.2 3.8 collective-permute-start.3
  600.6 234.4 %reduce-scatter.10.cloned.1.call-start = ((), (), s32[]{:S(2)}) async-start(), calls=%async_computation.20 | async-start | bytes 5242880 | tf_op jit(solution)/shard_map/reduce_scatter | solution.py:285
  716.8 52.7 %copy-start.34 = (f32[1024,4,32]{0,2,1:T(8,128)S(1)}, f32[1024,4,32]{0,2,1:T(8,128)}, u32[]{:S(2)}) copy-start(f32[1024,4,32]{0,2,1:T(8,128)} %copy-done.33) | copy-start | bytes 1572868
  716.8 52.7 %copy-start.36 = (f32[1024,4,32]{0,2,1:T(8,128)S(1)}, f32[1024,4,32]{0,2,1:T(8,128)}, u32[]{:S(2)}) copy-start(f32[1024,4,32]{0,2,1:T(8,128)} %copy-done.35) | copy-start | bytes 1572868
  790.3 93.3 %all-reduce.32.cloned.1.call-start = ((), (), s32[]{:S(2)}) async-start(), calls=%async_computation.21 | async-start | bytes 2097152 | tf_op jit(solution)/shard_map/psum | solution.py:53
  840.0 43.7 %copy-start.3 = (f32[1024,512]{1,0:T(8,128)S(1)}, f32[1024,512]{1,0:T(8,128)}, u32[]{:S(2)}) copy-start(f32[1024,512]{1,0:T(8,128)} %copy-done.2) | copy-start | bytes 6291460
  840.0 43.7 %copy-start.57 = (f32[1024]{0:T(1024)S(1)}, f32[1024]{0:T(1024)}, u32[]{:S(2)}) copy-start(f32[1024]{0:T(1024)} %copy-done.56) | copy-start | bytes 12292
  840.0 43.7 %copy-start.76 = (f32[1,512]{1,0:T(1,128)S(1)}, f32[1,512]{1,0:T(1,128)}, u32[]{:S(2)}) copy-start(f32[1,512]{1,0:T(1,128)} %copy-done.75) | copy-start | bytes 6148
  843.3 42.2 %copy-start.86 = (f32[1024]{0:T(1024)S(1)}, f32[1024]{0:T(1024)}, u32[]{:S(2)}) copy-start(f32[1024]{0:T(1024)} %copy-done.85) | copy-start | bytes 12292
  843.3 42.3 %copy-start.72 = (f32[1024]{0:T(1024)S(1)}, f32[1024]{0:T(1024)}, u32[]{:S(2)}) copy-start(f32[1024]{0:T(1024)} %copy-done.71) | copy-start | bytes 12292
  843.4 93.3 %all-reduce.34.cloned.1.call-start = ((), (), s32[]{:S(2)}) async-start(), calls=%async_computation.22 | async-start | bytes 2097152 | tf_op jit(solution)/shard_map/psum | solution.py:53
  896.4 62.9 %reduce-scatter.22.cloned.1.call-start = ((), (), s32[]{:S(2)}) async-start(), calls=%async_computation.28 | async-start | bytes 327680 | tf_op jit(solution)/shard_map/reduce_scatter | solution.py:336
  899.7 87.4 %reduce-scatter.24.cloned.1.call-start = ((), (), s32[]{:S(2)}) async-start(), calls=%async_computation.29 | async-start | bytes 1310720 | tf_op jit(solution)/shard_map/reduce_scatter | solution.py:339
  903.8 111.2 %reduce-scatter.26.cloned.1.call-start = ((), (), s32[]{:S(2)}) async-start(), calls=%async_computation.30 | async-start | bytes 1310720 | tf_op jit(solution)/shard_map/reduce_scatter | solution.py:342
  908.6 128.9 %reduce-scatter.20.cloned.1.call-start = ((), (), s32[]{:S(2)}) async-start(), calls=%async_computation.27 | async-start | bytes 655360 | tf_op jit(solution)/shard_map/reduce_scatter | solution.py:333
  912.4 146.1 %reduce-scatter.18.cloned.1.call-start = ((), (), s32[]{:S(2)}) async-start(), calls=%async_computation.26 | async-start | bytes 327680 | tf_op jit(solution)/shard_map/reduce_scatter | solution.py:330
  915.5 166.6 %reduce-scatter.16.cloned.1.call-start = ((), (), s32[]{:S(2)}) async-start(), calls=%async_computation.25 | async-start | bytes 983040 | tf_op jit(solution)/shard_map/reduce_scatter | solution.py:327
  918.9 192.3 %reduce-scatter.12.cloned.1.call-start = ((), (), s32[]{:S(2)}) async-start(), calls=%async_computation.23 | async-start | bytes 1310720 | tf_op jit(solution)/shard_map/reduce_scatter | solution.py:321
  923.8 215.6 %reduce-scatter.14.cloned.1.call-start = ((), (), s32[]{:S(2)}) async-start(), calls=%async_computation.24 | async-start | bytes 1310720 | tf_op jit(solution)/shard_map/reduce_scatter | solution.py:324
  928.0 275.7 %all-reduce.36.cloned.1.call-start = ((), (), s32[]{:S(2)}) async-start(), calls=%async_computation.31 | async-start | bytes 3014656 | tf_op jit(solution)/shard_map/psum | solution.py:351
  936.6 202.8 %copy-start.20 = (bf16[1024,512]{1,0:T(8,128)(2,1)S(1)}, bf16[1024,512]{1,0:T(8,128)(2,1)}, u32[]{:S(2)}) copy-start(bf16[1024,512]{1,0:T(8,128)(2,1)} %all-reduce.34.cloned.1.call-done) | copy-start | bytes 3145732
  (113 other events, 851.3 us)
Sparse Core Ops, SparseCore 0:
  9.6 30.6 all-gather.5
  41.9 27.3 all-gather.7
  73.6 39.5 all-reduce.19
  119.1 34.4 all-gather.9
  227.8 40.0 all-reduce.21
  337.9 36.4 all-reduce.23
  375.9 27.9 all-gather.11
  405.5 27.3 all-gather.13
  437.1 39.4 all-reduce.25
  491.8 40.0 all-reduce.27
  600.7 38.0 all-reduce.29
  790.4 44.5 reduce-scatter.9
  843.5 40.1 all-reduce.31
  896.5 40.0 all-reduce.33
  939.3 19.9 reduce-scatter.21
  961.5 25.5 reduce-scatter.23
  989.2 25.7 reduce-scatter.25
  1017.1 20.3 reduce-scatter.19
  1040.3 18.2 reduce-scatter.17
  1060.7 21.3 reduce-scatter.15
  1084.4 26.7 reduce-scatter.11
  1113.5 25.7 reduce-scatter.13
  1142.2 41.1 all-reduce.35
where the time goes:
time: 1230 us; the launch traced here: 1220 us
  waiting for transfers between devices  593 us (48%)
  matrix products  220 us (18%)
  blocking collectives  188 us (15%)
  other arithmetic  164 us (13%)
  local copies, waits for them, and re-layouts  30.3 us (2%)
  between operations  17.3 us (1%)
    psum x8, waiting for transfers between devices, tensor_total(): lax.psum(partial_value.astype(jnp.bfloat16), 'tp').astype(jnp.float32)  240 us
    psum x1, blocking collectives, per_device(): lax.psum((gain_terms, kernel_local), ('fsdp', 'ctx'))  59.7 us
    convert_element_type x1, other arithmetic, attend_back(): score_grad = (probs * (probs_grad - center)).astype(jnp.bfloat16)  52.7 us
    dot_general x1, matrix products, attend_back(): jnp.einsum('fhe,lhe->hfl', mixed_grad, values, preferred_element_type=jnp...  45.1 us
    psum x1, blocking collectives, per_device(): lax.psum((jnp.sum(shifted_grad, (0, 1)), jnp.sum(shifted_grad * unit, (0,...  33.7 us
    psum x1, blocking collectives, per_device(): lax.psum((jnp.sum(live_cube * filtered, (0, 1)), jnp.sum(live_cube * filt...  32.1 us
    reduce_scatter x1, waiting for transfers between devices, per_device(): lax.psum_scatter(weight_grads[0].astype(jnp.bfloat16), 'fsdp', scatter_di...  29.1 us
    all_gather x1, waiting for transfers between devices, per_device(): lax.all_gather(feed_up, 'fsdp', axis=0, tiled=True)  28.7 us
  transfers between devices with their start and end apart: 27, of which 23 were waited for; matrix products, arithmetic and copies ran while one was open for 6% of the time, Pallas kernels for 0%

commit v1 on v0

--- a/solution.py
+++ b/solution.py
@@ -1,14 +1,186 @@
 import jax
 import jax.numpy as jnp
 from jax import lax
+from jax.experimental import pallas as pl
+from jax.experimental.pallas import tpu as pltpu
 from jax.sharding import PartitionSpec as P
 
 HEAD = 64
+PAIR = 128
 KERNEL = 31
 
 
 norm_eps = 1e-05
 masked_score = -1000000000.0
+
+
+def split_heads(block, axis):
+    spot = lax.broadcasted_iota(jnp.int32, block.shape, axis)
+    zero = jnp.zeros_like(block)
+    return (jnp.where(spot < HEAD, block, zero), jnp.where(spot < HEAD, zero, block))
+
+
+def key_bias(length, chunk):
+    spot = pl.program_id(1) * chunk + lax.broadcasted_iota(jnp.int32, (chunk, 1), 0)
+    return jnp.where(spot < length, 0.0, masked_score)
+
+
+def attend_forward_kernel(length_ref, q_ref, k_ref, v_ref, o_ref, lse_ref, qt_s, top_s, sum_s):
+    chunk = k_ref.shape[0]
+    step = pl.program_id(1)
+
+    @pl.when(step == 0)
+    def _():
+        first, second = split_heads(q_ref[...].T, 0)
+        qt_s[0] = first
+        qt_s[1] = second
+        top_s[...] = jnp.full_like(top_s, -jnp.inf)
+        sum_s[...] = jnp.zeros_like(sum_s)
+        o_ref[...] = jnp.zeros_like(o_ref)
+
+    bias = key_bias(length_ref[0], chunk)
+    values = v_ref[...].T
+    for j in range(2):
+        scores = jnp.dot(k_ref[...], qt_s[j], preferred_element_type=jnp.float32) + bias
+        old = top_s[j]
+        top = jnp.maximum(old, jnp.max(scores, 0, keepdims=True))
+        fade = jnp.exp(old - top)
+        raised = jnp.exp(scores - top)
+        top_s[j] = top
+        sum_s[j] = sum_s[j] * fade + jnp.sum(raised, 0, keepdims=True)
+        rows = slice(j * HEAD, (j + 1) * HEAD)
+        o_ref[rows] = o_ref[rows] * fade + jnp.dot(
+            values[rows], raised.astype(jnp.bfloat16), preferred_element_type=jnp.float32
+        )
+
+    @pl.when(step == pl.num_programs(1) - 1)
+    def _():
+        for j in range(2):
+            rows = slice(j * HEAD, (j + 1) * HEAD)
+            o_ref[rows] = o_ref[rows] / sum_s[j]
+            lse_ref[j] = top_s[j] + jnp.log(sum_s[j])
+
+
+def attend_forward(query, joined, length, chunk=512):
+    frames, width = query.shape
+    keys = joined.shape[0]
+    pairs = width // PAIR
+    return pl.pallas_call(
+        attend_forward_kernel,
+        grid_spec=pltpu.PrefetchScalarGridSpec(
+            num_scalar_prefetch=1,
+            grid=(pairs, keys // chunk),
+            in_specs=[
+                pl.BlockSpec((frames, PAIR), lambda p, c, n: (0, p)),
+                pl.BlockSpec((chunk, PAIR), lambda p, c, n: (c, p)),
+                pl.BlockSpec((chunk, PAIR), lambda p, c, n: (c, pairs + p)),
+            ],
+            out_specs=[
+                pl.BlockSpec((PAIR, frames), lambda p, c, n: (p, 0)),
+                pl.BlockSpec((2, 1, frames), lambda p, c, n: (p, 0, 0)),
+            ],
+            scratch_shapes=[
+                pltpu.VMEM((2, PAIR, frames), jnp.bfloat16),
+                pltpu.VMEM((2, 1, frames), jnp.float32),
+                pltpu.VMEM((2, 1, frames), jnp.float32),
+            ],
+        ),
+        out_shape=[
+            jax.ShapeDtypeStruct((width, frames), jnp.float32),
+            jax.ShapeDtypeStruct((2 * pairs, 1, frames), jnp.float32),
+        ],
+        compiler_params=pltpu.CompilerParams(vmem_limit_bytes=50 * 1024 * 1024),
+        cost_estimate=pl.CostEstimate(
+            flops=4 * frames * keys * width,
+            bytes_accessed=4 * keys * width + 6 * frames * width,
+            transcendentals=2 * pairs * frames * keys,
+        ),
+        name="attend_forward",
+    )(length, query, joined, joined)
+
+
+def attend_backward_kernel(
+    length_ref, q_ref, g_ref, o_ref, lse_ref, k_ref, v_ref, dq_ref, dkv_ref,
+    qt_s, gt_s, q_s, g_s, delta_s,
+):
+    chunk = k_ref.shape[0]
+
+    @pl.when(pl.program_id(1) == 0)
+    def _():
+        query, grad = q_ref[...], g_ref[...]
+        for j, part in enumerate(split_heads(query, 1)):
+            q_s[j] = part
+        for j, part in enumerate(split_heads(grad, 1)):
+            g_s[j] = part
+        grad_t = grad.T
+        for j, part in enumerate(split_heads(query.T, 0)):
+            qt_s[j] = part
+        for j, part in enumerate(split_heads(grad_t, 0)):
+            gt_s[j] = part
+        product = grad_t.astype(jnp.float32) * o_ref[...]
+        for j in range(2):
+            delta_s[j] = jnp.sum(product[j * HEAD : (j + 1) * HEAD], 0, keepdims=True)
+        dq_ref[...] = jnp.zeros_like(dq_ref)
+
+    bias = key_bias(length_ref[0], chunk)
+    keys_t = k_ref[...].T
+    dk = dv = None
+    for j in range(2):
+        scores = jnp.dot(k_ref[...], qt_s[j], preferred_element_type=jnp.float32) + bias
+        probs = jnp.exp(scores - lse_ref[j])
+        dp = jnp.dot(v_ref[...], gt_s[j], preferred_element_type=jnp.float32)
+        ds = (probs * (dp - delta_s[j])).astype(jnp.bfloat16)
+        dv_j = jnp.dot(probs.astype(jnp.bfloat16), g_s[j], preferred_element_type=jnp.float32)
+        dk_j = jnp.dot(ds, q_s[j], preferred_element_type=jnp.float32)
+        dk = dk_j if dk is None else dk + dk_j
+        dv = dv_j if dv is None else dv + dv_j
+        rows = slice(j * HEAD, (j + 1) * HEAD)
+        dq_ref[rows] += jnp.dot(keys_t[rows], ds, preferred_element_type=jnp.float32)
+    dkv_ref[0] = dk.astype(jnp.bfloat16)
+    dkv_ref[1] = dv.astype(jnp.bfloat16)
+
+
+def attend_backward(query, joined, length, lse, mixed, grad, chunk=512):
+    frames, width = query.shape
+    keys = joined.shape[0]
+    pairs = width // PAIR
+    return pl.pallas_call(
+        attend_backward_kernel,
+        grid_spec=pltpu.PrefetchScalarGridSpec(
+            num_scalar_prefetch=1,
+            grid=(pairs, keys // chunk),
+            in_specs=[
+                pl.BlockSpec((frames, PAIR), lambda p, c, n: (0, p)),
+                pl.BlockSpec((frames, PAIR), lambda p, c, n: (0, p)),
+                pl.BlockSpec((PAIR, frames), lambda p, c, n: (p, 0)),
+                pl.BlockSpec((2, 1, frames), lambda p, c, n: (p, 0, 0)),
+                pl.BlockSpec((chunk, PAIR), lambda p, c, n: (c, p)),
+                pl.BlockSpec((chunk, PAIR), lambda p, c, n: (c, pairs + p)),
+            ],
+            out_specs=[
+                pl.BlockSpec((PAIR, frames), lambda p, c, n: (p, 0)),
+                pl.BlockSpec((2, chunk, PAIR), lambda p, c, n: (0, c, p)),
+            ],
+            scratch_shapes=[
+                pltpu.VMEM((2, PAIR, frames), jnp.bfloat16),
+                pltpu.VMEM((2, PAIR, frames), jnp.bfloat16),
+                pltpu.VMEM((2, frames, PAIR), jnp.bfloat16),
+                pltpu.VMEM((2, frames, PAIR), jnp.bfloat16),
+                pltpu.VMEM((2, 1, frames), jnp.float32),
+            ],
+        ),
+        out_shape=[
+            jax.ShapeDtypeStruct((width, frames), jnp.float32),
+            jax.ShapeDtypeStruct((2, keys, width), jnp.bfloat16),
+        ],
+        compiler_params=pltpu.CompilerParams(vmem_limit_bytes=50 * 1024 * 1024),
+        cost_estimate=pl.CostEstimate(
+            flops=10 * frames * keys * width,
+            bytes_accessed=8 * keys * width + 12 * frames * width,
+            transcendentals=2 * pairs * frames * keys,
+        ),
+        name="attend_backward",
+    )(length, query, grad, mixed, lse, joined, joined)
 
 
 def with_halo(cells, sides, width):
@@ -50,7 +222,88 @@
 
 
 def tensor_total(partial_value):
-    return lax.psum(partial_value.astype(jnp.bfloat16), "tp").astype(jnp.float32)
+    low = partial_value.astype(jnp.bfloat16)
+    if lax.axis_size("tp") != 2:
+        return lax.psum(low, "tp").astype(jnp.float32)
+    other = lax.ppermute(low, "tp", [(0, 1), (1, 0)])
+    return low.astype(jnp.float32) + other.astype(jnp.float32)
+
+
+def gather_weights(*shards):
+    rows = shards[0].shape[0]
+    flat = jnp.concatenate([shard.reshape(rows, -1) for shard in shards], 1)
+    part = rows // lax.axis_size("ctx")
+    mine = lax.dynamic_slice_in_dim(flat, lax.axis_index("ctx") * part, part, 0)
+    whole = lax.all_gather(mine, ("fsdp", "ctx"), axis=0, tiled=True)
+    pieces, start = [], 0
+    for shard in shards:
+        width = shard.size // rows
+        pieces.append(
+            lax.slice_in_dim(whole, start, start + width, axis=1).reshape(-1, *shard.shape[1:])
+        )
+        start += width
+    return pieces
+
+
+def pack_grads(*grads):
+    return jnp.concatenate(
+        [grad.astype(jnp.bfloat16).reshape(grad.shape[0], -1) for grad in grads], 1
+    )
+
+
+def reduce_grads(packed, *shapes):
+    part = lax.psum_scatter(packed, ("fsdp", "ctx"), scatter_dimension=0, tiled=True)
+    whole = lax.all_gather(part, "ctx", axis=0, tiled=True)
+    pieces, start = [], 0
+    for shape in shapes:
+        width = 1
+        for size in shape[1:]:
+            width *= size
+        pieces.append(
+            lax.slice_in_dim(whole, start, start + width, axis=1)
+            .astype(jnp.float32)
+            .reshape(-1, *shape[1:])
+        )
+        start += width
+    return pieces
+
+
+def attend_all(query_low, joined_all, lengths):
+    batch, frames, heads, _ = query_low.shape
+    if (heads * HEAD) % PAIR:
+        return lax.map(attend_one, (query_low, joined_all, lengths))
+    mixed, totals = [], []
+    for row in range(batch):
+        out, total = attend_forward(
+            query_low[row].reshape(frames, -1), joined_all[row], lengths[row : row + 1]
+        )
+        mixed.append(out)
+        totals.append(total)
+    return (jnp.stack(mixed), jnp.stack(totals))
+
+
+def attend_all_back(query_low, joined_all, lengths, log_total, mixed, mixed_grad):
+    batch, frames, heads, _ = query_low.shape
+    if (heads * HEAD) % PAIR:
+        query_grad, joined_grad = lax.map(
+            attend_back, (query_low, joined_all, lengths, log_total, mixed_grad)
+        )
+        width = heads * HEAD
+        low = joined_grad.astype(jnp.bfloat16)
+        return (query_grad, jnp.stack([low[..., :width], low[..., width:]], 1))
+    queries, others = [], []
+    for row in range(batch):
+        query_grad, joined_grad = attend_backward(
+            query_low[row].reshape(frames, -1),
+            joined_all[row],
+            lengths[row : row + 1],
+            log_total[row],
+            mixed[row],
+            mixed_grad[row].reshape(frames, -1),
+        )
+        queries.append(query_grad.T.reshape(frames, heads, HEAD))
+        others.append(joined_grad)
+    return (jnp.stack(queries), jnp.stack(others))
 
 
 def product_rows(left, right):
@@ -155,17 +408,11 @@
     live = (place[None, :] < lengths[:, None]).astype(jnp.float32)
     live_rows = live.reshape(rows, 1)
     live_cube = live[:, :, None]
-    gathered = (
-        lax.all_gather(feed_up, "fsdp", axis=0, tiled=True),
-        lax.all_gather(feed_down, "fsdp", axis=0, tiled=True),
-        lax.all_gather(attend_in, "fsdp", axis=0, tiled=True),
-        lax.all_gather(attend_out, "fsdp", axis=0, tiled=True),
-        lax.all_gather(mixer_in, "fsdp", axis=0, tiled=True),
-        lax.all_gather(mixer_out, "fsdp", axis=0, tiled=True),
-        lax.all_gather(final_up, "fsdp", axis=0, tiled=True),
-        lax.all_gather(final_down, "fsdp", axis=0, tiled=True),
-    )
-    up_one, down_one, proj_in, proj_out, conv_in, conv_out, up_two, down_two = gathered
+    up_one, down_one = gather_weights(feed_up, feed_down)
+    proj_in, proj_out, conv_in, conv_out = gather_weights(
+        attend_in, attend_out, mixer_in, mixer_out
+    )
+    up_two, down_two = gather_weights(final_up, final_down)
     stream = layer_input.reshape(rows, width)
     cotangent = out_grad.reshape(rows, width)
     branch_one, saved_one = feed_forward(stream, norm_gains[0], up_one, down_one)
@@ -190,8 +437,11 @@
         -1,
     )
     joined_all = lax.all_gather(joined, "ctx", axis=1, tiled=True)
-    mixed, log_total = lax.map(attend_one, (query_low, joined_all, lengths))
-    mixed_rows = mixed.reshape(rows, local_width)
+    mixed, log_total = attend_all(query_low, joined_all, lengths)
+    if local_width % PAIR:
+        mixed_rows = mixed.reshape(rows, local_width)
+    else:
+        mixed_rows = mixed.astype(jnp.bfloat16).transpose(0, 2, 1).reshape(rows, local_width)
     after_two = after_one + tensor_total(product_rows(mixed_rows, proj_out))
     normed, norm_back_three = jax.vjp(layer_norm, after_two, norm_gains[2])
     normed_three = normed.astype(jnp.bfloat16)
@@ -279,14 +529,19 @@
         .astype(jnp.bfloat16)
         .reshape(batch, frames, heads, HEAD)
     )
-    query_grad, joined_grad = lax.map(
-        attend_back, (query_low, joined_all, lengths, log_total, mixed_grad)
+    early = pack_grads(up_two_grad, down_two_grad, conv_in_grad, conv_out_grad, proj_out_grad)
+    early, mixed_grad = lax.optimization_barrier((early, mixed_grad))
+    up_two_grad, down_two_grad, conv_in_grad, conv_out_grad, proj_out_grad = reduce_grads(
+        early, final_up.shape, final_down.shape, mixer_in.shape, mixer_out.shape, attend_out.shape
+    )
+    query_grad, joined_grad = attend_all_back(
+        query_low, joined_all, lengths, log_total, mixed, mixed_grad
     )
     joined_local = lax.psum_scatter(
-        joined_grad.astype(jnp.bfloat16), "ctx", scatter_dimension=1, tiled=True
+        joined_grad, "ctx", scatter_dimension=2, tiled=True
     ).astype(jnp.float32)
-    key_grad = joined_local[..., :local_width].reshape(batch, frames, heads, HEAD)
-    value_grad = joined_local[..., local_width:].reshape(batch, frames, heads, HEAD)
+    key_grad = joined_local[:, 0].reshape(batch, frames, heads, HEAD)
+    value_grad = joined_local[:, 1].reshape(batch, frames, heads, HEAD)
     query_raw_grad, key_raw_grad = rotate_back((query_grad, key_grad))
     proj_grad = (
         jnp.stack([query_raw_grad, key_raw_grad, value_grad], 2)
@@ -307,66 +562,26 @@
     input_grad = grad_one + stream_grad
     gain_terms = jnp.stack([gain_one, gain_two, gain_three, gain_four, gain_five])
     gain_total, kernel_total = lax.psum((gain_terms, kernel_local), ("fsdp", "ctx"))
-    weight_grads = (
+    up_one_grad, down_one_grad, proj_in_grad = reduce_grads(
+        pack_grads(up_one_grad, down_one_grad, proj_in_grad),
+        feed_up.shape,
+        feed_down.shape,
+        attend_in.shape,
+    )
+    return (
+        result.reshape(batch, frames, width),
+        input_grad.reshape(batch, frames, width),
+        gain_total,
         up_one_grad,
         down_one_grad,
         proj_in_grad,
         proj_out_grad,
         conv_in_grad,
         conv_out_grad,
+        kernel_total,
+        jnp.stack([scale_sum, bias_sum]),
         up_two_grad,
         down_two_grad,
-    )
-    owned = (
-        lax.psum_scatter(
-            weight_grads[0].astype(jnp.bfloat16), "fsdp", scatter_dimension=0, tiled=True
-        ).astype(jnp.float32),
-        lax.psum_scatter(
-            weight_grads[1].astype(jnp.bfloat16), "fsdp", scatter_dimension=0, tiled=True
-        ).astype(jnp.float32),
-        lax.psum_scatter(
-            weight_grads[2].astype(jnp.bfloat16), "fsdp", scatter_dimension=0, tiled=True
-        ).astype(jnp.float32),
-        lax.psum_scatter(
-            weight_grads[3].astype(jnp.bfloat16), "fsdp", scatter_dimension=0, tiled=True
-        ).astype(jnp.float32),
-        lax.psum_scatter(
-            weight_grads[4].astype(jnp.bfloat16), "fsdp", scatter_dimension=0, tiled=True
-        ).astype(jnp.float32),
-        lax.psum_scatter(
-            weight_grads[5].astype(jnp.bfloat16), "fsdp", scatter_dimension=0, tiled=True
-        ).astype(jnp.float32),
-        lax.psum_scatter(
-            weight_grads[6].astype(jnp.bfloat16), "fsdp", scatter_dimension=0, tiled=True
-        ).astype(jnp.float32),
-        lax.psum_scatter(
-            weight_grads[7].astype(jnp.bfloat16), "fsdp", scatter_dimension=0, tiled=True
-        ).astype(jnp.float32),
-    )
-    owned = (
-        lax.psum(owned[0].astype(jnp.bfloat16), "ctx").astype(jnp.float32),
-        lax.psum(owned[1].astype(jnp.bfloat16), "ctx").astype(jnp.float32),
-        lax.psum(owned[2].astype(jnp.bfloat16), "ctx").astype(jnp.float32),
-        lax.psum(owned[3].astype(jnp.bfloat16), "ctx").astype(jnp.float32),
-        lax.psum(owned[4].astype(jnp.bfloat16), "ctx").astype(jnp.float32),
-        lax.psum(owned[5].astype(jnp.bfloat16), "ctx").astype(jnp.float32),
-        lax.psum(owned[6].astype(jnp.bfloat16), "ctx").astype(jnp.float32),
-        lax.psum(owned[7].astype(jnp.bfloat16), "ctx").astype(jnp.float32),
-    )
-    return (
-        result.reshape(batch, frames, width),
-        input_grad.reshape(batch, frames, width),
-        gain_total,
-        owned[0],
-        owned[1],
-        owned[2],
-        owned[3],
-        owned[4],
-        owned[5],
-        kernel_total,
-        jnp.stack([scale_sum, bias_sum]),
-        owned[6],
-        owned[7],
     )
 
 

time: 1230 us -> 723 us (0.59)
  waiting for transfers between devices: 593 us -> 266 us
  matrix products: 220 us -> 50.1 us
  Pallas kernels: 0 us -> 83.2 us
  other arithmetic: 164 us -> 83.5 us
  blocking collectives: 188 us -> 146 us
  local copies, waits for them, and re-layouts: 30.3 us -> 49.4 us
    psum x9 -> x0, waiting for transfers between devices: 240 us -> none  [the longest x8 240 us: tensor_total(): lax.psum(partial_value.astype(jnp.bfloat16), 'tp').astype(jnp.float32)]
    reduce_scatter x9 -> x3, waiting for transfers between devices: 227 us -> 57.1 us  [the longest x1 41.8 us: per_device(): lax.psum_scatter(joined_grad, 'ctx', scatter_dimension=2, tiled=True)]
    dot_general x6 -> x0, matrix products: 147 us -> none  [the longest x1 45.1 us: attend_back(): jnp.einsum('fhe,lhe->hfl', mixed_grad, values, preferred_element_type=jnp...]
    ppermute x0 -> x8, waiting for transfers between devices: none -> 107 us  [tensor_total(): other = lax.ppermute(low, 'tp', [(0, 1), (1, 0)])]
    pallas_call x0 -> x2, Pallas kernels: none -> 83.2 us  [the longest x1 48.5 us: attend_backward(): pl.pallas_call(attend_backward_kernel, grid_spec=pltpu.PrefetchScalarGrid...]
    convert_element_type x8 -> x5, other arithmetic: 61.8 us -> 5.43 us  [the longest x3 4.82 us: reduce_grads(): pieces.append(lax.slice_in_dim(whole, start, start + width, axis=1).astyp...]
    all_gather x4 -> x2, blocking collectives: 63 us -> 15.5 us  [reduce_grads(): whole = lax.all_gather(part, 'ctx', axis=0, tiled=True)]
    all_gather x4 -> x3, waiting for transfers between devices: 102 us -> 67.4 us  [gather_weights(): whole = lax.all_gather(mine, ('fsdp', 'ctx'), axis=0, tiled=True)]
  transfers between devices with their start and end apart: 27 -> 19, of which waited for: 23 -> 12; matrix products, arithmetic and copies ran while one was open for 6% -> 14% of each run, Pallas kernels for 0% -> 0%
where the time goes in v1:
time: 723 us; the launch traced here: 714 us
  waiting for transfers between devices  266 us (37%)
  blocking collectives  146 us (20%)
  other arithmetic  83.5 us (12%)
  Pallas kernels  83.2 us (12%)
  matrix products  50.1 us (7%)
  local copies, waits for them, and re-layouts  49.4 us (7%)
  starting transfers between devices  19.7 us (3%)
  between operations  16.6 us (2%)
    ppermute x8, waiting for transfers between devices, tensor_total(): other = lax.ppermute(low, 'tp', [(0, 1), (1, 0)])  107 us
    all_gather x3, waiting for transfers between devices, gather_weights(): whole = lax.all_gather(mine, ('fsdp', 'ctx'), axis=0, tiled=True)  67.4 us
    psum x1, blocking collectives, per_device(): lax.psum((gain_terms, kernel_local), ('fsdp', 'ctx'))  61.5 us
    pallas_call x1, Pallas kernels, attend_backward(): pl.pallas_call(attend_backward_kernel, grid_spec=pltpu.PrefetchScalarGrid...  48.5 us
    reduce_scatter x1, waiting for transfers between devices, per_device(): lax.psum_scatter(joined_grad, 'ctx', scatter_dimension=2, tiled=True)  41.8 us
    unnamed x196, local copies, waits for them, and re-layouts  37.2 us
    psum x1, blocking collectives, per_device(): lax.psum((jnp.sum(shifted_grad, (0, 1)), jnp.sum(shifted_grad * unit, (0,...  35.3 us
    pallas_call x1, Pallas kernels, attend_forward(): pl.pallas_call(attend_forward_kernel, grid_spec=pltpu.PrefetchScalarGridS...  34.7 us
  transfers between devices with their start and end apart: 19, of which 12 were waited for; matrix products, arithmetic and copies ran while one was open for 14% of the time, Pallas kernels for 0%

profile of v1, /device:TPU:0, one launch (start us, length us, event | category | flops | bytes accessed | tf_op | source)
XLA Modules:
  0.0 713.7 jit_solution(481179626745147303)
XLA Ops:
  14.0 1.9 copy.82
  16.0 2.6 reduce_sum.609
  20.0 34.9 %all-gather.5.cloned.1.call-done = bf16[512,2048]{1,0:T(8,128)(2,1)} async-done(((bf16[32,2048]{1,0:T(8,128)(2,1)}), bf16[512,2048]{1,0:T(8,128)(2,1)}) %all-gather.5.cloned.1.call-update) | async-done | bytes 2097168 | tf_op jit(solution)/shard_map/all_gather | solution.py:237
  54.9 5.2 multiply_convert_fusion.1
  60.1 2.3 convolution_convert_fusion.9
  64.5 32.5 %all-gather.7.cloned.1.call-done = bf16[512,1792]{1,0:T(8,128)(2,1)} async-done(((bf16[32,1792]{1,0:T(8,128)(2,1)}), bf16[512,1792]{1,0:T(8,128)(2,1)}) %all-gather.7.cloned.1.call-update) | async-done | bytes 1835024 | tf_op jit(solution)/shard_map/all_gather | solution.py:237
  99.3 2.1 fusion.228
  107.4 32.5 %all-gather.9.cloned.1.call-done = bf16[1,4096,512]{2,1,0:T(8,128)(2,1)} async-done(((bf16[1,1024,512]{2,1,0:T(8,128)(2,1)}), bf16[1,4096,512]{2,1,0:T(8,128)(2,1)}) %all-gather.9.cloned.1.call-update) | async-done | bytes 4194320 | tf_op jit(solution)/shard_map/all_gather | solution.py:439
  139.9 34.7 %attend_forward.1 = (f32[256,1024]{1,0:T(8,128)S(1)}, f32[4,1,1024]{2,1,0:T(1,128)S(1)}) custom-call(s32[1]{0:T(128)} %copy.138.length_ref, bf16[1024,256]{1,0:T(8,128)(2,1)S(1)} %copy.92.q_ref, bf16[4096,512]{1,0:T(8,128)(2,1)} %bitcast.365, bf16[4096,512]{1,0:T(8,128)(2,1)} %bitcast.366), custom_call_target="tpu_custom_call" | custom-call | flops 4294967296 | bytes 5767168 | tf_op jit(solution)/shard_map/attend_forward/pallas_call | solution.py:68
  175.1 1.5 collective-permute-start.1
  180.6 19.9 %collective-permute-done.1 = bf16[1024,512]{0,1:T(8,128)(2,1)} collective-permute-done((bf16[1024,512]{0,1:T(8,128)(2,1)S(1)}, bf16[1024,512]{0,1:T(8,128)(2,1)}, u32[]{:S(2)}, u32[]{:S(2)}) %collective-permute-start.1) | collective-permute-done | bytes 1048608 | tf_op jit(solution)/shard_map/ppermute | solution.py:228
  200.6 2.6 fusion.227
  211.6 8.0 %fusion.45 = (f32[256]{0:T(256)S(1)}, f32[256]{0:T(256)S(1)}, f32[1,1024,256]{2,1,0:T(8,128)S(1)}) fusion(f32[1024]{0:T(1024)S(1)} %fusion.194, bf16[1,15,256]{2,1,0:T(8,128)(2,1)S(1)} %collective-permute-done.3, bf16[1,1024,256]{2,1,0:T(8,128)(2,1)S(1)} %fusion.108, f32[256]{0:T(256)S(1)} %bitcast.282, f32[256]{0:T(256)S(1)} %bitcast.284, ...), kind=kLoop, calls=%fused_computation.236 | loop fusion | flops 48758272 | bytes 1626112 | tf_op jit(solution)/shard_map/reduce_sum | solution.py:466
  219.6 33.3 %all-reduce.8 = (f32[256]{0:T(256)S(1)}, f32[]{:T(128)}, f32[256]{0:T(256)S(1)}) all-reduce(f32[256]{0:T(256)S(1)} %get-tuple-element.105, f32[]{:T(128)} %fusion.200, f32[256]{0:T(256)S(1)} %get-tuple-element.104), channel_id=1, replica_groups=mesh['fsdp'=4,'ctx'=4,'tp'=2] {'fsdp','ctx'}, use_global_device_ids=true, to_apply=%region_7.0 | all-reduce | flops 513 | bytes 4104 | tf_op jit(solution)/shard_map/psum | solution.py:463
  253.5 1.7 convolution_convert_fusion.8
  255.2 1.5 collective-permute-start.4
  256.8 21.3 %collective-permute-done.4 = bf16[1024,512]{0,1:T(8,128)(2,1)S(1)} collective-permute-done((bf16[1024,512]{0,1:T(8,128)(2,1)S(1)}, bf16[1024,512]{0,1:T(8,128)(2,1)S(1)}, u32[]{:S(2)}, u32[]{:S(2)}) %collective-permute-start.4) | collective-permute-done | bytes 1048608 | tf_op jit(solution)/shard_map/ppermute | solution.py:228
  280.4 3.4 fusion.113
  283.8 2.4 convolution_convert_fusion.7
  287.7 3.3 copy.96
  291.0 17.4 %collective-permute-done.5 = bf16[1024,512]{0,1:T(8,128)(2,1)} collective-permute-done((bf16[1024,512]{0,1:T(8,128)(2,1)}, bf16[1024,512]{0,1:T(8,128)(2,1)}, u32[]{:S(2)}, u32[]{:S(2)}) %collective-permute-start.5) | collective-permute-done | bytes 1048608 | tf_op jit(solution)/shard_map/ppermute | solution.py:228
  308.4 2.7 fusion.224
  313.9 2.0 fusion.223
  316.0 2.3 copy-done.84
  318.3 2.4 fusion.2
  323.5 19.6 %collective-permute-done.6 = bf16[1024,512]{0,1:T(8,128)(2,1)S(1)} collective-permute-done((bf16[1024,512]{0,1:T(8,128)(2,1)S(1)}, bf16[1024,512]{0,1:T(8,128)(2,1)S(1)}, u32[]{:S(2)}, u32[]{:S(2)}) %collective-permute-start.6) | collective-permute-done | bytes 1048608 | tf_op jit(solution)/shard_map/ppermute | solution.py:228
  343.6 1.6 multiply_reduce_fusion
  346.7 1.8 fusion.102
  349.9 35.3 %all-reduce.7 = (f32[256]{0:T(256)S(1)}, f32[256]{0:T(256)S(1)}) all-reduce(f32[256]{0:T(256)S(1)} %get-tuple-element.207, f32[256]{0:T(256)S(1)} %reduce_sum.626), channel_id=1, replica_groups=mesh['fsdp'=4,'ctx'=4,'tp'=2] {'fsdp','ctx'}, use_global_device_ids=true, to_apply=%region_23.0 | all-reduce | flops 512 | bytes 4096 | tf_op jit(solution)/shard_map/psum | solution.py:493
  386.0 5.3 fusion.95
  392.6 3.3 collective-permute-start.8
  396.0 4.0 fusion.12
  400.0 8.5 %fusion.48 = (f32[1024,1,256]{2,0,1:T(8,128)S(1)}, f32[1024,1,256]{2,0,1:T(8,128)S(1)}) fusion(f32[1024,2,256]{2,0,1:T(8,128)S(1)} %copy-done.14, f32[1024]{0:T(1024)S(1)} %fusion.194, bf16[1,1024,256]{2,1,0:T(8,128)(2,1)S(1)} %get-tuple-element.117, bf16[1,15,256]{2,1,0:T(8,128)(2,1)S(1)} %collective-permute-done.8, f32[256]{0:T(256)S(1)} %bitcast.283, ...), kind=kLoop, calls=%fused_computation.239 | loop fusion | flops 49807360 | bytes 4769792 | tf_op jit(solution)/shard_map/transpose(jvp())/mul | solution.py:451
  409.6 1.7 bitcast_convert_fusion.1
  412.8 2.5 fusion.11
  415.2 1.7 convolution_convert_fusion.12
  419.1 3.1 fusion.14
  422.2 14.5 %collective-permute-done.9 = bf16[1024,512]{0,1:T(8,128)(2,1)} collective-permute-done((bf16[1024,512]{0,1:T(8,128)(2,1)}, bf16[1024,512]{0,1:T(8,128)(2,1)}, u32[]{:S(2)}, u32[]{:S(2)}) %collective-permute-start.9) | collective-permute-done | bytes 1048608 | tf_op jit(solution)/shard_map/ppermute | solution.py:228
  436.7 3.0 multiply_reduce_fusion.1
  439.7 2.5 fusion.221
  444.8 2.2 convolution_convert_fusion.11
  448.2 48.5 %attend_backward.1 = (f32[256,1024]{1,0:T(8,128)S(1)}, bf16[2,4096,256]{2,1,0:T(8,128)(2,1)}) custom-call(s32[1]{0:T(128)} %copy.138.length_ref, bf16[1024,256]{1,0:T(8,128)(2,1)S(1)} %copy.92.q_ref, bf16[1024,256]{1,0:T(8,128)(2,1)S(1)} %copy.104.g_ref, f32[256,1024]{1,0:T(8,128)S(1)} %get-tuple-element.19.o_ref, ...), custom_call_target="tpu_custom_call" | custom-call | flops 10737418240 | bytes 11534336 | tf_op jit(solution)/shard_map/attend_backward/pallas_call | solution.py:147
  496.9 41.8 %reduce-scatter.4.cloned.1.call-done = bf16[1,2,1024,256]{3,2,1,0:T(8,128)(2,1)} async-done(((bf16[1,2,4096,256]{3,2,1,0:T(8,128)(2,1)}), bf16[1,2,1024,256]{3,2,1,0:T(8,128)(2,1)}) %reduce-scatter.4.cloned.1.call-update) | async-done | bytes 1048592 | tf_op jit(solution)/shard_map/reduce_scatter | solution.py:540
  538.7 2.1 slice_convert_fusion.1
  543.8 1.5 collective-permute-start.10
  545.4 3.2 copy.113
  548.7 3.4 convolution_convert_fusion.10
  552.1 2.4 copy.111
  554.4 14.3 %collective-permute-done.10 = bf16[1024,512]{0,1:T(8,128)(2,1)} collective-permute-done((bf16[1024,512]{0,1:T(8,128)(2,1)S(1)}, bf16[1024,512]{0,1:T(8,128)(2,1)}, u32[]{:S(2)}, u32[]{:S(2)}) %collective-permute-start.10) | collective-permute-done | bytes 1048608 | tf_op jit(solution)/shard_map/ppermute | solution.py:228
  568.7 1.7 multiply_reduce_fusion.5
  570.5 2.4 multiply_reduce_fusion.2
  573.1 2.6 add_add_fusion.5
  579.3 2.5 fusion.5
  584.6 1.8 pad_maximum_fusion
  595.6 15.3 %reduce-scatter.8.cloned.1.call-done = bf16[32,3072]{1,0:T(8,128)(2,1)} async-done(((bf16[512,3072]{1,0:T(8,128)(2,1)}), bf16[32,3072]{1,0:T(8,128)(2,1)}) %reduce-scatter.8.cloned.1.call-update) | async-done | bytes 196624 | tf_op jit(solution)/shard_map/reduce_scatter | solution.py:255
  610.9 8.3 %all_gather.23 = bf16[128,3072]{1,0:T(8,128)(2,1)S(1)} all-gather(bf16[32,3072]{1,0:T(8,128)(2,1)} %reduce-scatter.8.cloned.1.call-done), channel_id=1, replica_groups=mesh['fsdp'=4,'ctx'=4,'tp'=2] {'ctx'}, dimensions={0}, use_global_device_ids=true | all-gather | bytes 983040 | tf_op jit(solution)/shard_map/all_gather | solution.py:256
  621.0 1.6 slice_convert_fusion.8
  622.6 2.1 slice_convert_fusion.2
  624.7 1.8 multiply_reduce_fusion.4
  626.5 2.4 multiply_reduce_fusion.3
  629.0 3.5 add_bitcast_fusion
  632.5 2.9 copy.114
  635.4 61.5 %all-reduce.6 = (f32[5,512]{1,0:T(8,128)}, f32[31,256]{1,0:T(8,128)}) all-reduce(f32[5,512]{1,0:T(8,128)S(1)} %stack.133, f32[31,256]{1,0:T(8,128)S(1)} %stack.165), channel_id=1, replica_groups=mesh['fsdp'=4,'ctx'=4,'tp'=2] {'fsdp','ctx'}, use_global_device_ids=true, to_apply=%region_36.0 | all-reduce | flops 10496 | bytes 83968 | tf_op jit(solution)/shard_map/psum | solution.py:564
  696.9 7.2 %all_gather.22 = bf16[128,2816]{1,0:T(8,128)(2,1)S(1)} all-gather(bf16[32,2816]{1,0:T(8,128)(2,1)} %reduce-scatter.6.cloned.1.call-done), channel_id=1, replica_groups=mesh['fsdp'=4,'ctx'=4,'tp'=2] {'ctx'}, dimensions={0}, use_global_device_ids=true | all-gather | bytes 901120 | tf_op jit(solution)/shard_map/all_gather | solution.py:256
  (313 shorter events, 77.2 us)
Async XLA Ops:
  7.2 47.8 %all-gather.5.cloned.1.call-start = ((), (), s32[]{:S(2)}) async-start(), calls=%async_computation.3 | async-start | bytes 2228224 | tf_op jit(solution)/shard_map/all_gather | solution.py:237
  8.8 88.2 %all-gather.7.cloned.1.call-start = ((), (), s32[]{:S(2)}) async-start(), calls=%async_computation.4 | async-start | bytes 1949696 | tf_op jit(solution)/shard_map/all_gather | solution.py:237
  14.0 125.9 %all-gather.9.cloned.1.call-start = ((), (), s32[]{:S(2)}) async-start(), calls=%async_computation.5 | async-start | bytes 5242880 | tf_op jit(solution)/shard_map/all_gather | solution.py:439
  15.9 83.4 %copy-start = (f32[1,1024,512]{1,2,0:T(8,128)}, f32[1,1024,512]{1,2,0:T(8,128)S(1)}, u32[]{:S(2)}) copy-start(f32[1,1024,512]{1,2,0:T(8,128)S(1)} %copy.82) | copy-start | bytes 6291460
  16.0 3.5 copy-start.66
  18.5 41.6 %copy-start.42 = (f32[1024]{0:T(1024)}, f32[1024]{0:T(1024)S(1)}, u32[]{:S(2)}) copy-start(f32[1024]{0:T(1024)S(1)} %broadcast_multiply_fusion.5) | copy-start | bytes 12292
  19.4 40.7 %copy-start.46 = (f32[1024]{0:T(1024)}, f32[1024]{0:T(1024)S(1)}, u32[]{:S(2)}) copy-start(f32[1024]{0:T(1024)S(1)} %fusion.195) | copy-start | bytes 12292
  20.0 40.1 %copy-start.56 = (f32[1,512]{1,0:T(1,128)}, f32[1,512]{1,0:T(1,128)S(1)}, u32[]{:S(2)}) copy-start(f32[1,512]{1,0:T(1,128)S(1)} %get-tuple-element.197) | copy-start | bytes 6148
  54.9 5.2 copy-start.78
  62.4 36.9 %collective-permute-start = (bf16[1024,512]{0,1:T(8,128)(2,1)}, bf16[1024,512]{0,1:T(8,128)(2,1)}, u32[]{:S(2)}, u32[]{:S(2)}) collective-permute-start(bf16[1024,512]{0,1:T(8,128)(2,1)} %convolution_convert_fusion.9), channel_id=1, source_target_pairs={{0,1},{1,0},{2,3},{3,2},{4,5},{5,4},{6,7},{7,6},{8,9},{9,8},{10,11... | collective-permute-start | bytes 3145736 | tf_op jit(solution)/shard_map/ppermute | solution.py:228
  64.4 40.1 %copy-start.33 = (f32[1024,32]{0,1:T(8,128)}, f32[1024,32]{0,1:T(8,128)S(1)}, u32[]{:S(2)}) copy-start(f32[1024,32]{0,1:T(8,128)S(1)} %get-tuple-element.200) | copy-start | bytes 393220
  106.4 174.0 %all-gather.11.cloned.1.call-start = ((), (), s32[]{:S(2)}) async-start(), calls=%async_computation.6 | async-start | bytes 2228224 | tf_op jit(solution)/shard_map/all_gather | solution.py:237
  139.9 34.8 %copy-start.28 = (bf16[512,1792]{1,0:T(8,128)(2,1)S(1)}, bf16[512,1792]{1,0:T(8,128)(2,1)}, u32[]{:S(2)}) copy-start(bf16[512,1792]{1,0:T(8,128)(2,1)} %all-gather.7.cloned.1.call-done) | copy-start | bytes 5505028
  174.6 5.0 slice-start.1
  175.1 25.5 %collective-permute-start.1 = (bf16[1024,512]{0,1:T(8,128)(2,1)S(1)}, bf16[1024,512]{0,1:T(8,128)(2,1)}, u32[]{:S(2)}, u32[]{:S(2)}) collective-permute-start(bf16[1024,512]{0,1:T(8,128)(2,1)S(1)} %convolution_convert_fusion), channel_id=1, source_target_pairs={{0,1},{1,0},{2,3},{3,2},{4,5},{5,4},{6,7},{7,6},{8,9},{9,8},{10,11... | collective-permute-start | bytes 3145736 | tf_op jit(solution)/shard_map/ppermute | solution.py:228
  177.3 361.4 %reduce-scatter.4.cloned.1.call-start = ((), (), s32[]{:S(2)}) async-start(), calls=%async_computation.7 | async-start | bytes 5242880 | tf_op jit(solution)/shard_map/reduce_scatter | solution.py:540
  205.6 3.9 copy-start.77
  206.9 179.1 %copy-start.11 = (bf16[1,1024,256]{2,1,0:T(8,128)(2,1)}, bf16[1,1024,256]{2,1,0:T(8,128)(2,1)S(1)}, u32[]{:S(2)}) copy-start(bf16[1,1024,256]{2,1,0:T(8,128)(2,1)S(1)} %fusion.108) | copy-start | bytes 1572868
  206.9 3.2 collective-permute-start.2
  208.2 3.4 collective-permute-start.3
  253.5 24.6 %copy-start.3 = (f32[1024,512]{0,1:T(8,128)S(1)}, f32[1024,512]{0,1:T(8,128)}, u32[]{:S(2)}) copy-start(f32[1024,512]{0,1:T(8,128)} %copy-done.2) | copy-start | bytes 6291460
  255.2 22.8 %collective-permute-start.4 = (bf16[1024,512]{0,1:T(8,128)(2,1)S(1)}, bf16[1024,512]{0,1:T(8,128)(2,1)S(1)}, u32[]{:S(2)}, u32[]{:S(2)}) collective-permute-start(bf16[1024,512]{0,1:T(8,128)(2,1)S(1)} %convolution_convert_fusion.8), channel_id=1, source_target_pairs={{0,1},{1,0},{2,3},{3,2},{4,5},{5,4},{6,7},{7,6},{8,9},{9,8},{10,11... | collective-permute-start | bytes 3145736 | tf_op jit(solution)/shard_map/ppermute | solution.py:228
  280.4 3.4 copy-start.81
  286.2 22.2 %collective-permute-start.5 = (bf16[1024,512]{0,1:T(8,128)(2,1)}, bf16[1024,512]{0,1:T(8,128)(2,1)}, u32[]{:S(2)}, u32[]{:S(2)}) collective-permute-start(bf16[1024,512]{0,1:T(8,128)(2,1)} %convolution_convert_fusion.7), channel_id=1, source_target_pairs={{0,1},{1,0},{2,3},{3,2},{4,5},{5,4},{6,7},{7,6},{8,9},{9,8},{10,11... | collective-permute-start | bytes 3145736 | tf_op jit(solution)/shard_map/ppermute | solution.py:228
  313.9 4.3 copy-start.84
  316.0 29.3 %copy-start.25 = (f32[1024,512]{0,1:T(8,128)}, f32[1024,512]{0,1:T(8,128)S(1)}, u32[]{:S(2)}) copy-start(f32[1024,512]{0,1:T(8,128)S(1)} %get-tuple-element.126) | copy-start | bytes 6291460
  320.6 22.4 %copy-start.9 = (f32[1024,512]{0,1:T(8,128)S(1)}, f32[1024,512]{0,1:T(8,128)}, u32[]{:S(2)}) copy-start(f32[1024,512]{0,1:T(8,128)} %copy-done.8) | copy-start | bytes 6291460
  322.0 21.1 %collective-permute-start.6 = (bf16[1024,512]{0,1:T(8,128)(2,1)S(1)}, bf16[1024,512]{0,1:T(8,128)(2,1)S(1)}, u32[]{:S(2)}, u32[]{:S(2)}) collective-permute-start(bf16[1024,512]{0,1:T(8,128)(2,1)S(1)} %convolution_convert_fusion.6), channel_id=1, source_target_pairs={{0,1},{1,0},{2,3},{3,2},{4,5},{5,4},{6,7},{7,6},{8,9},{9,8},{10,11... | collective-permute-start | bytes 3145736 | tf_op jit(solution)/shard_map/ppermute | solution.py:228
  385.2 6.1 copy-start.75
  385.2 14.8 %copy-start.73 = (f32[256]{0:T(256)}, f32[256]{0:T(256)S(1)}, u32[]{:S(2)}) copy-start(f32[256]{0:T(256)S(1)} %get-tuple-element.112) | copy-start | bytes 3076
  385.2 10.8 %copy-start.10 = (f32[1024,512]{0,1:T(8,128)S(1)}, f32[1024,512]{0,1:T(8,128)}, u32[]{:S(2)}) copy-start(f32[1024,512]{0,1:T(8,128)} %copy-done.8) | copy-start | bytes 6291460
  391.3 8.7 %copy-start.15 = (bf16[1,1024,256]{2,1,0:T(8,128)(2,1)}, bf16[1,1024,256]{2,1,0:T(8,128)(2,1)S(1)}, u32[]{:S(2)}) copy-start(bf16[1,1024,256]{2,1,0:T(8,128)(2,1)S(1)} %get-tuple-element.117) | copy-start | bytes 1572868
  391.3 8.6 %collective-permute-start.7 = (bf16[1,15,256]{2,1,0:T(8,128)(2,1)S(1)}, bf16[1,15,256]{2,1,0:T(8,128)(2,1)S(1)}, u32[]{:S(2)}, u32[]{:S(2)}) collective-permute-start(bf16[1,15,256]{2,1,0:T(8,128)(2,1)S(1)} %get-tuple-element.155), channel_id=1, source_target_pairs={{2,0},{4,2},{6,4},{3,1},{5,3},{7,5},{10,8},{12,10},{14,12},{11,9},... | collective-permute-start | bytes 23048 | tf_op jit(solution)/shard_map/ppermute | solution.py:196
  392.6 7.4 %copy-start.14 = (f32[1024,2,256]{2,0,1:T(8,128)S(1)}, f32[1024,2,256]{2,0,1:T(8,128)}, u32[]{:S(2)}) copy-start(f32[1024,2,256]{2,0,1:T(8,128)} %copy-done.13) | copy-start | bytes 6291460
  392.6 7.3 %collective-permute-start.8 = (bf16[1,15,256]{2,1,0:T(8,128)(2,1)S(1)}, bf16[1,15,256]{2,1,0:T(8,128)(2,1)S(1)}, u32[]{:S(2)}, u32[]{:S(2)}) collective-permute-start(bf16[1,15,256]{2,1,0:T(8,128)(2,1)S(1)} %get-tuple-element.156), channel_id=1, source_target_pairs={{0,2},{2,4},{4,6},{1,3},{3,5},{5,7},{8,10},{10,12},{12,14},{9,11},... | collective-permute-start | bytes 23048 | tf_op jit(solution)/shard_map/ppermute | solution.py:194
  408.5 4.3 copy-start.85
  408.8 4.0 copy-start.26
  411.3 3.9 copy-start.4
  411.3 25.4 %collective-permute-start.9 = (bf16[1024,512]{0,1:T(8,128)(2,1)}, bf16[1024,512]{0,1:T(8,128)(2,1)}, u32[]{:S(2)}, u32[]{:S(2)}) collective-permute-start(bf16[1024,512]{0,1:T(8,128)(2,1)} %bitcast_convert_fusion.1), channel_id=1, source_target_pairs={{0,1},{1,0},{2,3},{3,2},{4,5},{5,4},{6,7},{7,6},{8,9},{9,8},{10,11... | collective-permute-start | bytes 3145736 | tf_op jit(solution)/shard_map/ppermute | solution.py:228
  419.1 17.6 %copy-start.5 = (f32[1024,512]{0,1:T(8,128)S(1)}, f32[1024,512]{0,1:T(8,128)}, u32[]{:S(2)}) copy-start(f32[1024,512]{0,1:T(8,128)} %copy-done.2) | copy-start | bytes 6291460
  496.7 114.2 %reduce-scatter.8.cloned.1.call-start = ((), (), s32[]{:S(2)}) async-start(), calls=%async_computation.9 | async-start | bytes 3342336 | tf_op jit(solution)/shard_map/reduce_scatter | solution.py:255
  496.9 44.3 %copy-start.34 = (f32[1024,32]{0,1:T(8,128)S(1)}, f32[1024,32]{0,1:T(8,128)}, u32[]{:S(2)}) copy-start(f32[1024,32]{0,1:T(8,128)} %copy-done.33) | copy-start | bytes 393220
  543.8 24.9 %collective-permute-start.10 = (bf16[1024,512]{0,1:T(8,128)(2,1)S(1)}, bf16[1024,512]{0,1:T(8,128)(2,1)}, u32[]{:S(2)}, u32[]{:S(2)}) collective-permute-start(bf16[1024,512]{0,1:T(8,128)(2,1)S(1)} %bitcast_convert_fusion), channel_id=1, source_target_pairs={{0,1},{1,0},{2,3},{3,2},{4,5},{5,4},{6,7},{7,6},{8,9},{9,8},{10,11... | collective-permute-start | bytes 3145736 | tf_op jit(solution)/shard_map/ppermute | solution.py:228
  545.3 151.6 %reduce-scatter.6.cloned.1.call-start = ((), (), s32[]{:S(2)}) async-start(), calls=%async_computation.8 | async-start | bytes 3063808 | tf_op jit(solution)/shard_map/reduce_scatter | solution.py:255
  545.4 3.3 copy-start.7
  545.4 3.3 copy-start.45
  545.4 3.3 copy-start.49
  545.4 3.2 copy-start.61
  554.4 16.0 %copy-start.53 = (f32[1024]{0:T(1024)S(1)}, f32[1024]{0:T(1024)}, u32[]{:S(2)}) copy-start(f32[1024]{0:T(1024)} %copy-done.52) | copy-start | bytes 12292
  575.7 3.6 copy-start.91
  579.3 3.9 copy-start.1
  579.3 3.9 copy-start.43
  579.3 3.9 copy-start.47
  579.3 3.9 copy-start.57
  587.5 4.5 copy-start.80
  587.5 4.5 copy-start.90
  592.1 3.4 copy-start.67
  592.1 3.4 copy-start.68
  592.1 3.4 copy-start.69
  592.1 3.4 copy-start.70
  592.1 3.4 copy-start.71
  592.1 3.4 copy-start.72
  593.4 31.3 %collective-permute-start.11 = (bf16[1024,512]{0,1:T(8,128)(2,1)S(1)}, bf16[1024,512]{0,1:T(8,128)(2,1)}, u32[]{:S(2)}, u32[]{:S(2)}) collective-permute-start(bf16[1024,512]{0,1:T(8,128)(2,1)S(1)} %convolution_convert_fusion.3), channel_id=1, source_target_pairs={{0,1},{1,0},{2,3},{3,2},{4,5},{5,4},{6,7},{7,6},{8,9},{9,8},{10,11... | collective-permute-start | bytes 3145736 | tf_op jit(solution)/shard_map/ppermute | solution.py:228
  632.5 2.9 copy-start.65
  (49 other events, 91.5 us)
Sparse Core Ops, SparseCore 0:
  10.7 44.1 all-gather.4
  57.8 39.1 all-gather.6
  106.5 33.2 all-gather.8
  177.5 40.5 all-gather.10
  496.9 41.7 reduce-scatter.3
  545.5 65.3 reduce-scatter.7
  614.7 64.3 reduce-scatter.5

commit v2 on v1

--- a/solution.py
+++ b/solution.py
@@ -1,3 +1,5 @@
+import functools
+
 import jax
 import jax.numpy as jnp
 from jax import lax
@@ -229,6 +231,82 @@
     return low.astype(jnp.float32) + other.astype(jnp.float32)
 
 
+def group_sum_kernel(axes, sizes, x_ref, o_ref, slots, send_sem, recv_sem):
+    places = [lax.axis_index(axis) for axis in axes]
+    peers = []
+    mine = 0
+    for place, size in zip(places, sizes):
+        mine = mine * size + place
+    total = 1
+    for size in sizes:
+        total *= size
+    for offset in range(1, total):
+        rest, target = offset, {}
+        for axis, place, size in reversed(list(zip(axes, places, sizes))):
+            target[axis] = lax.rem(place + rest % size, size)
+            rest //= size
+        peers.append(target)
+    barrier = pltpu.get_barrier_semaphore()
+    for target in peers:
+        pl.semaphore_signal(
+            barrier, inc=1, device_id=target, device_id_type=pl.DeviceIdType.MESH
+        )
+    pl.semaphore_wait(barrier, total - 1)
+    copies = []
+    for number, target in enumerate(peers):
+        copy = pltpu.make_async_remote_copy(
+            src_ref=x_ref,
+            dst_ref=slots.at[mine],
+            send_sem=send_sem.at[number],
+            recv_sem=recv_sem.at[number],
+            device_id=target,
+            device_id_type=pl.DeviceIdType.MESH,
+        )
+        copy.start()
+        copies.append(copy)
+    slots[mine] = x_ref[...]
+    for copy in copies:
+        copy.wait()
+    result = slots[0]
+    for number in range(1, total):
+        result = result + slots[number]
+    o_ref[...] = result
+
+
+def group_sum(values, axes, number):
+    sizes = [lax.axis_size(axis) for axis in axes]
+    total = 1
+    for size in sizes:
+        total *= size
+    return pl.pallas_call(
+        functools.partial(group_sum_kernel, axes, sizes),
+        out_shape=jax.ShapeDtypeStruct(values.shape, jnp.float32),
+        in_specs=[pl.BlockSpec(memory_space=pltpu.VMEM)],
+        out_specs=pl.BlockSpec(memory_space=pltpu.VMEM),
+        scratch_shapes=[
+            pltpu.VMEM((total,) + values.shape, jnp.float32),
+            pltpu.SemaphoreType.DMA((total - 1,)),
+            pltpu.SemaphoreType.DMA((total - 1,)),
+        ],
+        compiler_params=pltpu.CompilerParams(collective_id=number, has_side_effects=True),
+        name="group_sum_" + str(number),
+    )(values)
+
+
+def flat_sum(arrays, stages):
+    flat = jnp.concatenate([array.reshape(-1) for array in arrays])
+    size = flat.shape[0]
+    flat = jnp.pad(flat, (0, -size % 1024)).reshape(-1, 128)
+    for axes, number in stages:
+        flat = group_sum(flat, axes, number)
+    flat = flat.reshape(-1)
+    pieces, start = [], 0
+    for array in arrays:
+        pieces.append(lax.slice_in_dim(flat, start, start + array.size).reshape(array.shape))
+        start += array.size
+    return pieces
+
+
 def gather_weights(*shards):
     rows = shards[0].shape[0]
     flat = jnp.concatenate([shard.reshape(rows, -1) for shard in shards], 1)
@@ -409,10 +487,8 @@
     live_rows = live.reshape(rows, 1)
     live_cube = live[:, :, None]
     up_one, down_one = gather_weights(feed_up, feed_down)
-    proj_in, proj_out, conv_in, conv_out = gather_weights(
-        attend_in, attend_out, mixer_in, mixer_out
-    )
-    up_two, down_two = gather_weights(final_up, final_down)
+    (proj_in,) = gather_weights(attend_in)
+    proj_out, conv_in, conv_out = gather_weights(attend_out, mixer_in, mixer_out)
     stream = layer_input.reshape(rows, width)
     cotangent = out_grad.reshape(rows, width)
     branch_one, saved_one = feed_forward(stream, norm_gains[0], up_one, down_one)
@@ -437,6 +513,8 @@
         -1,
     )
     joined_all = lax.all_gather(joined, "ctx", axis=1, tiled=True)
+    joined_all, late_up, late_down = lax.optimization_barrier((joined_all, final_up, final_down))
+    up_two, down_two = gather_weights(late_up, late_down)
     mixed, log_total = attend_all(query_low, joined_all, lengths)
     if local_width % PAIR:
         mixed_rows = mixed.reshape(rows, local_width)
@@ -460,13 +538,14 @@
         filtered = filtered + depth_kernel[offset] * padded[:, offset : offset + frames].astype(
             jnp.float32
         )
-    sums = lax.psum(
-        (
+    live_count = jnp.full((channels,), jnp.sum(live))
+    sums = flat_sum(
+        [
             jnp.sum(live_cube * filtered, (0, 1)),
             jnp.sum(live_cube * filtered * filtered, (0, 1)),
-            jnp.sum(live),
-        ),
-        ("fsdp", "ctx"),
+            live_count,
+        ],
+        [(("fsdp", "ctx"), 0)],
     )
     count = sums[2]
     mean = sums[0] / count
@@ -485,13 +564,18 @@
         0.5 * grad_four, saved_four, up_two, down_two
     )
     grad_three = grad_four + stream_grad
+    early, grad_three = lax.optimization_barrier(
+        (pack_grads(up_two_grad, down_two_grad), grad_three)
+    )
+    up_two_grad, down_two_grad = reduce_grads(early, final_up.shape, final_down.shape)
     branch_low = grad_three.astype(jnp.bfloat16)
     conv_out_grad = product_cols(branch_low, active_low)
     shifted_grad = active_back(jnp.dot(branch_low, conv_out, preferred_element_type=jnp.float32))[
         0
     ].reshape(batch, frames, channels)
-    bias_sum, scale_sum = lax.psum(
-        (jnp.sum(shifted_grad, (0, 1)), jnp.sum(shifted_grad * unit, (0, 1))), ("fsdp", "ctx")
+    bias_sum, scale_sum = flat_sum(
+        [jnp.sum(shifted_grad, (0, 1)), jnp.sum(shifted_grad * unit, (0, 1))],
+        [(("fsdp", "ctx"), 1)],
     )
     var_grad = -0.5 * rescale * rescale * batch_norm[0] * scale_sum
     first_grad = (-rescale * batch_norm[0] * bias_sum - 2.0 * mean * var_grad) / count
@@ -529,10 +613,10 @@
         .astype(jnp.bfloat16)
         .reshape(batch, frames, heads, HEAD)
     )
-    early = pack_grads(up_two_grad, down_two_grad, conv_in_grad, conv_out_grad, proj_out_grad)
+    early = pack_grads(conv_in_grad, conv_out_grad, proj_out_grad)
     early, mixed_grad = lax.optimization_barrier((early, mixed_grad))
-    up_two_grad, down_two_grad, conv_in_grad, conv_out_grad, proj_out_grad = reduce_grads(
-        early, final_up.shape, final_down.shape, mixer_in.shape, mixer_out.shape, attend_out.shape
+    conv_in_grad, conv_out_grad, proj_out_grad = reduce_grads(
+        early, mixer_in.shape, mixer_out.shape, attend_out.shape
     )
     query_grad, joined_grad = attend_all_back(
         query_low, joined_all, lengths, log_total, mixed, mixed_grad
@@ -561,7 +645,9 @@
     )
     input_grad = grad_one + stream_grad
     gain_terms = jnp.stack([gain_one, gain_two, gain_three, gain_four, gain_five])
-    gain_total, kernel_total = lax.psum((gain_terms, kernel_local), ("fsdp", "ctx"))
+    gain_total, kernel_total = flat_sum(
+        [gain_terms, kernel_local], [(("ctx",), 2), (("fsdp",), 3)]
+    )
     up_one_grad, down_one_grad, proj_in_grad = reduce_grads(
         pack_grads(up_one_grad, down_one_grad, proj_in_grad),
         feed_up.shape,

time: 723 us -> 728 us (level)
  blocking collectives: 146 us -> 42.2 us
  waiting for transfers between devices: 266 us -> 328 us
  Pallas kernels: 83.2 us -> 116 us
  other arithmetic: 83.5 us -> 97.8 us
    psum x3 -> x0, blocking collectives: 130 us -> none  [the longest x1 61.5 us: per_device(): lax.psum((gain_terms, kernel_local), ('fsdp', 'ctx'))]
    reduce_scatter x2 -> x3, waiting for transfers between devices: 15.3 us -> 87.3 us  [reduce_grads(): lax.psum_scatter(packed, ('fsdp', 'ctx'), scatter_dimension=0, tiled=True)]
    pallas_call x0 -> x4, Pallas kernels: none -> 33.1 us  [group_sum(): pl.pallas_call(functools.partial(group_sum_kernel, axes, sizes), out_shap...]
    all_gather x0 -> x1, blocking collectives: none -> 21.3 us  [gather_weights(): whole = lax.all_gather(mine, ('fsdp', 'ctx'), axis=0, tiled=True)]
    all_gather x3, waiting for transfers between devices: 67.4 us -> 47.3 us  [gather_weights(): whole = lax.all_gather(mine, ('fsdp', 'ctx'), axis=0, tiled=True)]
    unnamed x196 -> x214, local copies, waits for them, and re-layouts: 37.2 us -> 26 us
    ppermute x8, waiting for transfers between devices: 107 us -> 115 us  [tensor_total(): other = lax.ppermute(low, 'tp', [(0, 1), (1, 0)])]
    all_gather x2 -> x3, blocking collectives: 15.5 us -> 20.9 us  [reduce_grads(): whole = lax.all_gather(part, 'ctx', axis=0, tiled=True)]
  transfers between devices with their start and end apart: 19 -> 20, of which waited for: 12 -> 16; matrix products, arithmetic and copies ran while one was open for 14% -> 14% of each run, Pallas kernels for 0% -> 8%
where the time goes in v2:
time: 728 us; the launch traced here: 718 us
  waiting for transfers between devices  328 us (45%)
  Pallas kernels  116 us (16%)
  other arithmetic  97.8 us (13%)
  matrix products  53.3 us (7%)
  local copies, waits for them, and re-layouts  44.1 us (6%)
  blocking collectives  42.2 us (6%)
  starting transfers between devices  19.7 us (3%)
  between operations  16.9 us (2%)
    ppermute x8, waiting for transfers between devices, tensor_total(): other = lax.ppermute(low, 'tp', [(0, 1), (1, 0)])  115 us
    reduce_scatter x3, waiting for transfers between devices, reduce_grads(): lax.psum_scatter(packed, ('fsdp', 'ctx'), scatter_dimension=0, tiled=True)  87.3 us
    pallas_call x1, Pallas kernels, attend_backward(): pl.pallas_call(attend_backward_kernel, grid_spec=pltpu.PrefetchScalarGrid...  48.5 us
    all_gather x3, waiting for transfers between devices, gather_weights(): whole = lax.all_gather(mine, ('fsdp', 'ctx'), axis=0, tiled=True)  47.3 us
    reduce_scatter x1, waiting for transfers between devices, per_device(): lax.psum_scatter(joined_grad, 'ctx', scatter_dimension=2, tiled=True)  43.9 us
    pallas_call x1, Pallas kernels, attend_forward(): pl.pallas_call(attend_forward_kernel, grid_spec=pltpu.PrefetchScalarGridS...  34.6 us
    pallas_call x4, Pallas kernels, group_sum(): pl.pallas_call(functools.partial(group_sum_kernel, axes, sizes), out_shap...  33.1 us
    all_gather x1, waiting for transfers between devices, per_device(): joined_all = lax.all_gather(joined, 'ctx', axis=1, tiled=True)  31.6 us
  transfers between devices with their start and end apart: 20, of which 16 were waited for; matrix products, arithmetic and copies ran while one was open for 14% of the time, Pallas kernels for 8%

profile of v2, /device:TPU:0, one launch (start us, length us, event | category | flops | bytes accessed | tf_op | source)
XLA Modules:
  0.0 718.3 jit_solution(8939311304606318136)
XLA Ops:
  8.8 1.9 copy.82
  10.8 2.6 reduce_sum.609
  13.7 41.2 %all-gather.5.cloned.1.call-done = bf16[512,2048]{1,0:T(8,128)(2,1)} async-done(((bf16[32,2048]{1,0:T(8,128)(2,1)}), bf16[512,2048]{1,0:T(8,128)(2,1)}) %all-gather.5.cloned.1.call-update) | async-done | bytes 2097168 | tf_op jit(solution)/shard_map/all_gather | solution.py:315
  54.9 5.2 multiply_convert_fusion.1
  60.1 2.3 convolution_convert_fusion.9
  64.3 21.3 %all_gather.25 = bf16[512,768]{1,0:T(8,128)(2,1)S(1)} all-gather(bf16[32,768]{1,0:T(8,128)(2,1)S(1)} %copy.84), channel_id=1, replica_groups=mesh['fsdp'=4,'ctx'=4,'tp'=2] {'fsdp','ctx'}, dimensions={0}, use_global_device_ids=true | all-gather | bytes 835584 | tf_op jit(solution)/shard_map/all_gather | solution.py:315
  88.0 2.1 fusion.233
  96.9 31.6 %all-gather.7.cloned.1.call-done = bf16[1,4096,512]{2,1,0:T(8,128)(2,1)} async-done(((bf16[1,1024,512]{2,1,0:T(8,128)(2,1)}), bf16[1,4096,512]{2,1,0:T(8,128)(2,1)}) %all-gather.7.cloned.1.call-update) | async-done | bytes 4194320 | tf_op jit(solution)/shard_map/all_gather | solution.py:515
  128.4 34.6 %attend_forward.1 = (f32[256,1024]{1,0:T(8,128)S(1)}, f32[4,1,1024]{2,1,0:T(1,128)S(1)}) custom-call(s32[1]{0:T(128)} %copy.128.length_ref, bf16[1024,256]{1,0:T(8,128)(2,1)S(1)} %copy.89.q_ref, bf16[4096,512]{1,0:T(8,128)(2,1)} %bitcast.408, bf16[4096,512]{1,0:T(8,128)(2,1)} %bitcast.409), custom_call_target="tpu_custom_call" | custom-call | flops 4294967296 | bytes 5767168 | tf_op jit(solution)/shard_map/attend_forward/pallas_call | solution.py:70
  163.1 6.1 all-gather.9.cloned.1.call-done
  177.0 19.1 %collective-permute-done.1 = bf16[1024,512]{0,1:T(8,128)(2,1)} collective-permute-done((bf16[1024,512]{0,1:T(8,128)(2,1)S(1)}, bf16[1024,512]{0,1:T(8,128)(2,1)}, u32[]{:S(2)}, u32[]{:S(2)}) %collective-permute-start.1) | collective-permute-done | bytes 1048608 | tf_op jit(solution)/shard_map/ppermute | solution.py:230
  196.1 2.4 fusion.232
  206.4 8.0 %multiply_reduce_fusion.14 = (f32[256]{0:T(256)S(1)}, f32[256]{0:T(256)S(1)}, f32[1,1024,256]{2,1,0:T(8,128)S(1)}) fusion(f32[1024]{0:T(1024)S(1)} %fusion.195, bf16[1,15,256]{2,1,0:T(8,128)(2,1)S(1)} %collective-permute-done.3, bf16[1,1024,256]{2,1,0:T(8,128)(2,1)S(1)} %fusion.104, f32[256]{0:T(256)S(1)} %bitcast.325, f32[256]{0:T(256)S(1)} %bitcast.327, ...), kind=kLoop, calls=%fused_computation.156 | loop fusion | flops 48758272 | bytes 1626112 | tf_op jit(solution)/shard_map/reduce_sum | solution.py:544
  215.8 10.3 %group_sum_0.1 = f32[8,128]{1,0:T(8,128)} custom-call(f32[8,128]{1,0:T(8,128)} %fusion.192.x_ref), custom_call_target="tpu_custom_call" | custom-call | tf_op jit(solution)/shard_map/group_sum_0/pallas_call | solution.py:281
  230.8 23.7 %collective-permute-done.4 = bf16[1024,512]{0,1:T(8,128)(2,1)S(1)} collective-permute-done((bf16[1024,512]{0,1:T(8,128)(2,1)S(1)}, bf16[1024,512]{0,1:T(8,128)(2,1)S(1)}, u32[]{:S(2)}, u32[]{:S(2)}) %collective-permute-start.4) | collective-permute-done | bytes 1048608 | tf_op jit(solution)/shard_map/ppermute | solution.py:230
  256.8 5.9 multiply_convert_fusion
  265.5 3.3 copy.93
  268.7 19.7 %collective-permute-done.5 = bf16[1024,512]{0,1:T(8,128)(2,1)} collective-permute-done((bf16[1024,512]{0,1:T(8,128)(2,1)S(1)}, bf16[1024,512]{0,1:T(8,128)(2,1)}, u32[]{:S(2)}, u32[]{:S(2)}) %collective-permute-start.5) | collective-permute-done | bytes 1048608 | tf_op jit(solution)/shard_map/ppermute | solution.py:230
  288.4 2.4 fusion.229
  293.6 2.0 fusion.228
  295.6 2.3 copy-done.102
  297.9 2.4 fusion.2
  307.3 17.9 %collective-permute-done.6 = bf16[1024,512]{0,1:T(8,128)(2,1)} collective-permute-done((bf16[1024,512]{0,1:T(8,128)(2,1)S(1)}, bf16[1024,512]{0,1:T(8,128)(2,1)}, u32[]{:S(2)}, u32[]{:S(2)}) %collective-permute-start.6) | collective-permute-done | bytes 1048608 | tf_op jit(solution)/shard_map/ppermute | solution.py:230
  325.2 2.4 multiply_reduce_fusion.7
  327.7 3.0 multiply_reduce_fusion
  330.7 2.3 add_add_fusion.7
  333.1 3.6 fusion.98
  336.8 2.0 reduce_sum.626
  340.0 8.0 %group_sum_1.1 = f32[8,128]{1,0:T(8,128)} custom-call(f32[8,128]{1,0:T(8,128)} %fusion.191.x_ref), custom_call_target="tpu_custom_call" | custom-call | tf_op jit(solution)/shard_map/group_sum_1/pallas_call | solution.py:281
  348.9 5.5 fusion.91
  355.7 3.0 collective-permute-start.8
  359.5 9.4 %fusion.44 = (f32[1024,1,256]{2,0,1:T(8,128)S(1)}, f32[1024,1,256]{2,0,1:T(8,128)S(1)}) fusion(f32[1024,2,256]{2,0,1:T(8,128)S(1)} %copy-done.13, f32[1024]{0:T(1024)S(1)} %fusion.195, bf16[1,1024,256]{2,1,0:T(8,128)(2,1)S(1)} %get-tuple-element.120, bf16[1,15,256]{2,1,0:T(8,128)(2,1)S(1)} %collective-permute-done.8, f32[256]{0:T(256)S(1)} %bitcast.326, ...), kind=kLoop, calls=%fused_computation.236 | loop fusion | flops 49807360 | bytes 4769792 | tf_op jit(solution)/shard_map/transpose(jvp())/mul | solution.py:529
  370.4 1.9 bitcast_convert_fusion.1
  375.2 3.0 convolution_convert_fusion.12
  378.5 19.8 %collective-permute-done.9 = bf16[1024,512]{0,1:T(8,128)(2,1)} collective-permute-done((bf16[1024,512]{0,1:T(8,128)(2,1)}, bf16[1024,512]{0,1:T(8,128)(2,1)}, u32[]{:S(2)}, u32[]{:S(2)}) %collective-permute-start.9) | collective-permute-done | bytes 1048608 | tf_op jit(solution)/shard_map/ppermute | solution.py:230
  398.2 3.1 multiply_reduce_fusion.1
  401.3 2.5 fusion.226
  406.4 1.8 copy.99
  408.1 2.1 pad_maximum_fusion.4
  410.3 2.2 convolution_convert_fusion.11
  413.8 48.5 %attend_backward.1 = (f32[256,1024]{1,0:T(8,128)S(1)}, bf16[2,4096,256]{2,1,0:T(8,128)(2,1)}) custom-call(s32[1]{0:T(128)} %copy.128.length_ref, bf16[1024,256]{1,0:T(8,128)(2,1)S(1)} %copy.89.q_ref, bf16[1024,256]{1,0:T(8,128)(2,1)S(1)} %copy.101.g_ref, f32[256,1024]{1,0:T(8,128)S(1)} %get-tuple-element.25.o_ref, ...), custom_call_target="tpu_custom_call" | custom-call | flops 10737418240 | bytes 11534336 | tf_op jit(solution)/shard_map/attend_backward/pallas_call | solution.py:149
  463.2 43.9 %reduce-scatter.5.cloned.1.call-done = bf16[1,2,1024,256]{3,2,1,0:T(8,128)(2,1)} async-done(((bf16[1,2,4096,256]{3,2,1,0:T(8,128)(2,1)}), bf16[1,2,1024,256]{3,2,1,0:T(8,128)(2,1)}) %reduce-scatter.5.cloned.1.call-update) | async-done | bytes 1048592 | tf_op jit(solution)/shard_map/reduce_scatter | solution.py:624
  507.1 2.1 slice_convert_fusion.1
  512.1 3.3 bitcast_convert_fusion
  516.9 1.8 copy.110
  520.4 3.4 convolution_convert_fusion.10
  523.7 2.3 copy.108
  526.1 14.4 %collective-permute-done.10 = bf16[1024,512]{0,1:T(8,128)(2,1)} collective-permute-done((bf16[1024,512]{0,1:T(8,128)(2,1)}, bf16[1024,512]{0,1:T(8,128)(2,1)}, u32[]{:S(2)}, u32[]{:S(2)}) %collective-permute-start.10) | collective-permute-done | bytes 1048608 | tf_op jit(solution)/shard_map/ppermute | solution.py:230
  540.5 2.1 multiply_reduce_fusion.5
  542.6 2.7 multiply_reduce_fusion.2
  545.4 2.9 add_add_fusion.5
  552.0 2.5 fusion.5
  562.5 2.9 convolution_convert_fusion.3
  568.2 6.0 all_gather.30
  574.9 1.8 reshape.858
  577.5 55.4 %reduce-scatter.11.cloned.1.call-done = bf16[32,2048]{1,0:T(8,128)(2,1)} async-done(((bf16[512,2048]{1,0:T(8,128)(2,1)}), bf16[32,2048]{1,0:T(8,128)(2,1)}) %reduce-scatter.11.cloned.1.call-update) | async-done | bytes 131088 | tf_op jit(solution)/shard_map/reduce_scatter | solution.py:333
  632.9 6.9 all_gather.31
  642.7 2.3 multiply_reduce_fusion.3
  645.7 5.9 group_sum_2.1.x_ref
  651.6 8.9 %group_sum_3.1 = f32[88,128]{1,0:T(8,128)} custom-call(f32[88,128]{1,0:T(8,128)} %group_sum_2.1.x_ref), custom_call_target="tpu_custom_call" | custom-call | tf_op jit(solution)/shard_map/group_sum_3/pallas_call | solution.py:281
  661.3 4.1 add_bitcast_fusion
  665.4 2.9 copy.111
  669.5 31.3 %reduce-scatter.7.cloned.1.call-done = bf16[32,2816]{1,0:T(8,128)(2,1)} async-done(((bf16[512,2816]{1,0:T(8,128)(2,1)}), bf16[32,2816]{1,0:T(8,128)(2,1)}) %reduce-scatter.7.cloned.1.call-update) | async-done | bytes 180240 | tf_op jit(solution)/shard_map/reduce_scatter | solution.py:333
  700.9 8.0 %all_gather.29 = bf16[128,2816]{1,0:T(8,128)(2,1)S(1)} all-gather(bf16[32,2816]{1,0:T(8,128)(2,1)} %reduce-scatter.7.cloned.1.call-done), channel_id=1, replica_groups=mesh['fsdp'=4,'ctx'=4,'tp'=2] {'ctx'}, dimensions={0}, use_global_device_ids=true | all-gather | bytes 901120 | tf_op jit(solution)/shard_map/all_gather | solution.py:334
  (352 shorter events, 91.4 us)
Async XLA Ops:
  7.2 47.8 %all-gather.5.cloned.1.call-start = ((), (), s32[]{:S(2)}) async-start(), calls=%async_computation.4 | async-start | bytes 2228224 | tf_op jit(solution)/shard_map/all_gather | solution.py:315
  8.8 119.6 %all-gather.7.cloned.1.call-start = ((), (), s32[]{:S(2)}) async-start(), calls=%async_computation.5 | async-start | bytes 5242880 | tf_op jit(solution)/shard_map/all_gather | solution.py:515
  10.8 77.2 %copy-start = (f32[1,1024,512]{1,2,0:T(8,128)}, f32[1,1024,512]{1,2,0:T(8,128)S(1)}, u32[]{:S(2)}) copy-start(f32[1,1024,512]{1,2,0:T(8,128)S(1)} %copy.82) | copy-start | bytes 6291460
  13.7 46.4 %copy-start.43 = (f32[1024]{0:T(1024)}, f32[1024]{0:T(1024)S(1)}, u32[]{:S(2)}) copy-start(f32[1024]{0:T(1024)S(1)} %multiply_reduce_fusion.13) | copy-start | bytes 12292
  54.9 5.2 copy-start.91
  62.4 25.6 %collective-permute-start = (bf16[1024,512]{0,1:T(8,128)(2,1)}, bf16[1024,512]{0,1:T(8,128)(2,1)}, u32[]{:S(2)}, u32[]{:S(2)}) collective-permute-start(bf16[1024,512]{0,1:T(8,128)(2,1)} %convolution_convert_fusion.9), channel_id=1, source_target_pairs={{0,1},{1,0},{2,3},{3,2},{4,5},{5,4},{6,7},{7,6},{8,9},{9,8},{10,11... | collective-permute-start | bytes 3145736 | tf_op jit(solution)/shard_map/ppermute | solution.py:230
  95.1 74.0 %all-gather.9.cloned.1.call-start = ((), (), s32[]{:S(2)}) async-start(), calls=%async_computation.6 | async-start | bytes 1114112 | tf_op jit(solution)/shard_map/all_gather | solution.py:315
  95.9 160.8 %all-gather.11.cloned.1.call-start = ((), (), s32[]{:S(2)}) async-start(), calls=%async_computation.7 | async-start | bytes 2228224 | tf_op jit(solution)/shard_map/all_gather | solution.py:315
  163.1 9.1 %copy-start.45 = (f32[31,256]{1,0:T(8,128)S(1)}, f32[31,256]{1,0:T(8,128)}, u32[]{:S(2)}) copy-start(f32[31,256]{1,0:T(8,128)} %param.24) | copy-start | bytes 95236
  170.6 25.5 %collective-permute-start.1 = (bf16[1024,512]{0,1:T(8,128)(2,1)S(1)}, bf16[1024,512]{0,1:T(8,128)(2,1)}, u32[]{:S(2)}, u32[]{:S(2)}) collective-permute-start(bf16[1024,512]{0,1:T(8,128)(2,1)S(1)} %convolution_convert_fusion), channel_id=1, source_target_pairs={{0,1},{1,0},{2,3},{3,2},{4,5},{5,4},{6,7},{7,6},{8,9},{9,8},{10,11... | collective-permute-start | bytes 3145736 | tf_op jit(solution)/shard_map/ppermute | solution.py:230
  172.2 34.1 %copy-start.47 = (f32[1,256]{1,0:T(1,128)}, f32[1,256]{1,0:T(1,128)S(1)}, u32[]{:S(2)}) copy-start(f32[1,256]{1,0:T(1,128)S(1)} %get-tuple-element.195) | copy-start | bytes 3076
  172.2 34.1 %copy-start.49 = (f32[1,256]{1,0:T(1,128)}, f32[1,256]{1,0:T(1,128)S(1)}, u32[]{:S(2)}) copy-start(f32[1,256]{1,0:T(1,128)S(1)} %get-tuple-element.196) | copy-start | bytes 3076
  175.0 23.8 %copy-start.31 = (bf16[512,512]{0,1:T(8,128)(2,1)}, bf16[512,512]{0,1:T(8,128)(2,1)S(1)}, u32[]{:S(2)}) copy-start(bf16[512,512]{0,1:T(8,128)(2,1)S(1)} %copy.126) | copy-start | bytes 1572868
  176.7 330.4 %reduce-scatter.5.cloned.1.call-start = ((), (), s32[]{:S(2)}) async-start(), calls=%async_computation.8 | async-start | bytes 5242880 | tf_op jit(solution)/shard_map/reduce_scatter | solution.py:624
  199.8 6.5 copy-start.51
  199.8 6.5 copy-start.53
  199.8 6.5 copy-start.55
  199.8 6.5 copy-start.57
  199.8 6.5 copy-start.58
  199.8 6.5 copy-start.59
  199.8 6.5 copy-start.60
  199.9 6.5 copy-start.61
  199.9 6.5 copy-start.62
  199.9 6.5 copy-start.63
  199.9 6.5 copy-start.64
  199.9 6.5 copy-start.65
  199.9 6.5 copy-start.66
  199.9 6.5 copy-start.67
  199.9 6.5 copy-start.68
  199.9 6.5 copy-start.69
  199.9 6.5 copy-start.70
  200.0 6.5 copy-start.71
  200.0 6.5 copy-start.72
  201.2 147.7 %copy-start.10 = (bf16[1,1024,256]{2,1,0:T(8,128)(2,1)}, bf16[1,1024,256]{2,1,0:T(8,128)(2,1)S(1)}, u32[]{:S(2)}) copy-start(bf16[1,1024,256]{2,1,0:T(8,128)(2,1)S(1)} %fusion.104) | copy-start | bytes 1572868
  201.2 3.8 collective-permute-start.2
  202.5 3.8 collective-permute-start.3
  214.5 14.7 %copy-start.27 = (f32[1,1024,256]{2,1,0:T(8,128)}, f32[1,1024,256]{2,1,0:T(8,128)S(1)}, u32[]{:S(2)}) copy-start(f32[1,1024,256]{2,1,0:T(8,128)S(1)} %get-tuple-element.134) | copy-start | bytes 3145732
  227.4 27.0 %copy-start.3 = (f32[1024,512]{0,1:T(8,128)S(1)}, f32[1024,512]{0,1:T(8,128)}, u32[]{:S(2)}) copy-start(f32[1024,512]{0,1:T(8,128)} %copy-done.2) | copy-start | bytes 6291460
  229.2 25.2 %collective-permute-start.4 = (bf16[1024,512]{0,1:T(8,128)(2,1)S(1)}, bf16[1024,512]{0,1:T(8,128)(2,1)S(1)}, u32[]{:S(2)}, u32[]{:S(2)}) collective-permute-start(bf16[1024,512]{0,1:T(8,128)(2,1)S(1)} %convolution_convert_fusion.8), channel_id=1, source_target_pairs={{0,1},{1,0},{2,3},{3,2},{4,5},{5,4},{6,7},{7,6},{8,9},{9,8},{10,11... | collective-permute-start | bytes 3145736 | tf_op jit(solution)/shard_map/ppermute | solution.py:230
  256.7 5.9 copy-start.94
  264.0 24.4 %collective-permute-start.5 = (bf16[1024,512]{0,1:T(8,128)(2,1)S(1)}, bf16[1024,512]{0,1:T(8,128)(2,1)}, u32[]{:S(2)}, u32[]{:S(2)}) collective-permute-start(bf16[1024,512]{0,1:T(8,128)(2,1)S(1)} %convolution_convert_fusion.7), channel_id=1, source_target_pairs={{0,1},{1,0},{2,3},{3,2},{4,5},{5,4},{6,7},{7,6},{8,9},{9,8},{10,11... | collective-permute-start | bytes 3145736 | tf_op jit(solution)/shard_map/ppermute | solution.py:230
  295.6 7.6 %copy-start.25 = (f32[1024,512]{0,1:T(8,128)}, f32[1024,512]{0,1:T(8,128)S(1)}, u32[]{:S(2)}) copy-start(f32[1024,512]{0,1:T(8,128)S(1)} %get-tuple-element.129) | copy-start | bytes 6291460
  301.6 23.6 %collective-permute-start.6 = (bf16[1024,512]{0,1:T(8,128)(2,1)S(1)}, bf16[1024,512]{0,1:T(8,128)(2,1)}, u32[]{:S(2)}, u32[]{:S(2)}) collective-permute-start(bf16[1024,512]{0,1:T(8,128)(2,1)S(1)} %convolution_convert_fusion.4), channel_id=1, source_target_pairs={{0,1},{1,0},{2,3},{3,2},{4,5},{5,4},{6,7},{7,6},{8,9},{9,8},{10,11... | collective-permute-start | bytes 3145736 | tf_op jit(solution)/shard_map/ppermute | solution.py:230
  307.3 20.4 %copy-start.9 = (f32[1024,512]{0,1:T(8,128)S(1)}, f32[1024,512]{0,1:T(8,128)}, u32[]{:S(2)}) copy-start(f32[1024,512]{0,1:T(8,128)} %copy-done.7) | copy-start | bytes 6291460
  333.1 15.8 %copy-start.29 = (f32[1,1024,256]{2,1,0:T(8,128)S(1)}, f32[1,1024,256]{2,1,0:T(8,128)}, u32[]{:S(2)}) copy-start(f32[1,1024,256]{2,1,0:T(8,128)} %copy-done.27) | copy-start | bytes 3145732
  336.7 22.8 %copy-start.48 = (f32[1,256]{1,0:T(1,128)S(1)}, f32[1,256]{1,0:T(1,128)}, u32[]{:S(2)}) copy-start(f32[1,256]{1,0:T(1,128)} %copy-done.47) | copy-start | bytes 3076
  336.7 22.8 %copy-start.50 = (f32[1,256]{1,0:T(1,128)S(1)}, f32[1,256]{1,0:T(1,128)}, u32[]{:S(2)}) copy-start(f32[1,256]{1,0:T(1,128)} %copy-done.49) | copy-start | bytes 3076
  336.8 22.8 %copy-start.52 = (f32[1,256]{1,0:T(1,128)S(1)}, f32[1,256]{1,0:T(1,128)}, u32[]{:S(2)}) copy-start(f32[1,256]{1,0:T(1,128)} %get-tuple-element.166) | copy-start | bytes 3076
  336.8 22.8 %copy-start.54 = (f32[1,256]{1,0:T(1,128)S(1)}, f32[1,256]{1,0:T(1,128)}, u32[]{:S(2)}) copy-start(f32[1,256]{1,0:T(1,128)} %get-tuple-element.167) | copy-start | bytes 3076
  336.8 22.8 %copy-start.56 = (f32[1,256]{1,0:T(1,128)S(1)}, f32[1,256]{1,0:T(1,128)}, u32[]{:S(2)}) copy-start(f32[1,256]{1,0:T(1,128)} %get-tuple-element.168) | copy-start | bytes 3076
  348.0 11.5 %copy-start.13 = (f32[1024,2,256]{2,0,1:T(8,128)S(1)}, f32[1024,2,256]{2,0,1:T(8,128)}, u32[]{:S(2)}) copy-start(f32[1024,2,256]{2,0,1:T(8,128)} %copy-done.12) | copy-start | bytes 6291460
  354.4 14.6 %copy-start.14 = (bf16[1,1024,256]{2,1,0:T(8,128)(2,1)}, bf16[1,1024,256]{2,1,0:T(8,128)(2,1)S(1)}, u32[]{:S(2)}) copy-start(bf16[1,1024,256]{2,1,0:T(8,128)(2,1)S(1)} %get-tuple-element.120) | copy-start | bytes 1572868
  354.4 4.3 collective-permute-start.7
  355.7 3.8 collective-permute-start.8
  372.2 26.0 %collective-permute-start.9 = (bf16[1024,512]{0,1:T(8,128)(2,1)}, bf16[1024,512]{0,1:T(8,128)(2,1)}, u32[]{:S(2)}, u32[]{:S(2)}) collective-permute-start(bf16[1024,512]{0,1:T(8,128)(2,1)} %bitcast_convert_fusion.1), channel_id=1, source_target_pairs={{0,1},{1,0},{2,3},{3,2},{4,5},{5,4},{6,7},{7,6},{8,9},{9,8},{10,11... | collective-permute-start | bytes 3145736 | tf_op jit(solution)/shard_map/ppermute | solution.py:230
  378.5 22.8 %copy-start.4 = (f32[1024,512]{0,1:T(8,128)S(1)}, f32[1024,512]{0,1:T(8,128)}, u32[]{:S(2)}) copy-start(f32[1024,512]{0,1:T(8,128)} %copy-done.2) | copy-start | bytes 6291460
  462.3 105.9 %reduce-scatter.9.cloned.1.call-start = ((), (), s32[]{:S(2)}) async-start(), calls=%async_computation.10 | async-start | bytes 1114112 | tf_op jit(solution)/shard_map/reduce_scatter | solution.py:333
  462.9 170.0 %reduce-scatter.11.cloned.1.call-start = ((), (), s32[]{:S(2)}) async-start(), calls=%async_computation.11 | async-start | bytes 2228224 | tf_op jit(solution)/shard_map/reduce_scatter | solution.py:333
  515.4 25.0 %collective-permute-start.10 = (bf16[1024,512]{0,1:T(8,128)(2,1)}, bf16[1024,512]{0,1:T(8,128)(2,1)}, u32[]{:S(2)}, u32[]{:S(2)}) collective-permute-start(bf16[1024,512]{0,1:T(8,128)(2,1)} %bitcast_convert_fusion), channel_id=1, source_target_pairs={{0,1},{1,0},{2,3},{3,2},{4,5},{5,4},{6,7},{7,6},{8,9},{9,8},{10,11... | collective-permute-start | bytes 3145736 | tf_op jit(solution)/shard_map/ppermute | solution.py:230
  518.8 182.1 %reduce-scatter.7.cloned.1.call-start = ((), (), s32[]{:S(2)}) async-start(), calls=%async_computation.9 | async-start | bytes 3063808 | tf_op jit(solution)/shard_map/reduce_scatter | solution.py:333
  562.4 5.1 copy-start.76
  562.4 5.1 copy-start.77
  562.4 5.1 copy-start.78
  565.4 75.5 %collective-permute-start.11 = (bf16[1024,512]{0,1:T(8,128)(2,1)S(1)}, bf16[1024,512]{0,1:T(8,128)(2,1)}, u32[]{:S(2)}, u32[]{:S(2)}) collective-permute-start(bf16[1024,512]{0,1:T(8,128)(2,1)S(1)} %convolution_convert_fusion.3), channel_id=1, source_target_pairs={{0,1},{1,0},{2,3},{3,2},{4,5},{5,4},{6,7},{7,6},{8,9},{9,8},{10,11... | collective-permute-start | bytes 3145736 | tf_op jit(solution)/shard_map/ppermute | solution.py:230
  (60 other events, 162.4 us)
Sparse Core Ops, SparseCore 0:
  10.7 44.1 all-gather.4
  95.2 33.1 all-gather.6
  131.2 37.9 all-gather.8
  176.8 39.5 all-gather.10
  462.4 44.6 reduce-scatter.4
  510.6 57.5 reduce-scatter.8
  572.0 60.8 reduce-scatter.10
  636.7 64.1 reduce-scatter.6

commit v3 on v2

--- a/solution.py
+++ b/solution.py
@@ -22,14 +22,15 @@
     return (jnp.where(spot < HEAD, block, zero), jnp.where(spot < HEAD, zero, block))
 
 
-def key_bias(length, chunk):
-    spot = pl.program_id(1) * chunk + lax.broadcasted_iota(jnp.int32, (chunk, 1), 0)
-    return jnp.where(spot < length, 0.0, masked_score)
-
-
-def attend_forward_kernel(length_ref, q_ref, k_ref, v_ref, o_ref, lse_ref, qt_s, top_s, sum_s):
+def key_bias(meta_ref, chunk):
+    start = meta_ref[1 + pl.program_id(0)]
+    spot = start + lax.broadcasted_iota(jnp.int32, (chunk, 1), 0)
+    return jnp.where(spot < meta_ref[0], 0.0, masked_score)
+
+
+def attend_forward_kernel(meta_ref, q_ref, k_ref, v_ref, o_ref, lse_ref, qt_s, top_s, sum_s):
     chunk = k_ref.shape[0]
-    step = pl.program_id(1)
+    step = pl.program_id(0)
 
     @pl.when(step == 0)
     def _():
@@ -40,7 +41,7 @@
         sum_s[...] = jnp.zeros_like(sum_s)
         o_ref[...] = jnp.zeros_like(o_ref)
 
-    bias = key_bias(length_ref[0], chunk)
+    bias = key_bias(meta_ref, chunk)
     values = v_ref[...].T
     for j in range(2):
         scores = jnp.dot(k_ref[...], qt_s[j], preferred_element_type=jnp.float32) + bias
@@ -55,7 +56,7 @@
             values[rows], raised.astype(jnp.bfloat16), preferred_element_type=jnp.float32
         )
 
-    @pl.when(step == pl.num_programs(1) - 1)
+    @pl.when(step == pl.num_programs(0) - 1)
     def _():
         for j in range(2):
             rows = slice(j * HEAD, (j + 1) * HEAD)
@@ -63,23 +64,22 @@
             lse_ref[j] = top_s[j] + jnp.log(sum_s[j])
 
 
-def attend_forward(query, joined, length, chunk=512):
-    frames, width = query.shape
+def attend_forward(query, pair, joined, meta, chunk):
+    frames = query.shape[0]
     keys = joined.shape[0]
-    pairs = width // PAIR
     return pl.pallas_call(
         attend_forward_kernel,
         grid_spec=pltpu.PrefetchScalarGridSpec(
             num_scalar_prefetch=1,
-            grid=(pairs, keys // chunk),
+            grid=(keys // chunk,),
             in_specs=[
-                pl.BlockSpec((frames, PAIR), lambda p, c, n: (0, p)),
-                pl.BlockSpec((chunk, PAIR), lambda p, c, n: (c, p)),
-                pl.BlockSpec((chunk, PAIR), lambda p, c, n: (c, pairs + p)),
+                pl.BlockSpec((frames, PAIR), lambda c, n: (0, pair)),
+                pl.BlockSpec((chunk, PAIR), lambda c, n: (c, 0)),
+                pl.BlockSpec((chunk, PAIR), lambda c, n: (c, 1)),
             ],
             out_specs=[
-                pl.BlockSpec((PAIR, frames), lambda p, c, n: (p, 0)),
-                pl.BlockSpec((2, 1, frames), lambda p, c, n: (p, 0, 0)),
+                pl.BlockSpec((PAIR, frames), lambda c, n: (0, 0)),
+                pl.BlockSpec((2, 1, frames), lambda c, n: (0, 0, 0)),
             ],
             scratch_shapes=[
                 pltpu.VMEM((2, PAIR, frames), jnp.bfloat16),
@@ -88,26 +88,26 @@
             ],
         ),
         out_shape=[
-            jax.ShapeDtypeStruct((width, frames), jnp.float32),
-            jax.ShapeDtypeStruct((2 * pairs, 1, frames), jnp.float32),
+            jax.ShapeDtypeStruct((PAIR, frames), jnp.float32),
+            jax.ShapeDtypeStruct((2, 1, frames), jnp.float32),
         ],
         compiler_params=pltpu.CompilerParams(vmem_limit_bytes=50 * 1024 * 1024),
         cost_estimate=pl.CostEstimate(
-            flops=4 * frames * keys * width,
-            bytes_accessed=4 * keys * width + 6 * frames * width,
-            transcendentals=2 * pairs * frames * keys,
+            flops=4 * frames * keys * PAIR,
+            bytes_accessed=4 * keys * PAIR + 6 * frames * PAIR,
+            transcendentals=2 * frames * keys,
         ),
         name="attend_forward",
-    )(length, query, joined, joined)
+    )(meta, query, joined, joined)
 
 
 def attend_backward_kernel(
-    length_ref, q_ref, g_ref, o_ref, lse_ref, k_ref, v_ref, dq_ref, dkv_ref,
+    meta_ref, q_ref, g_ref, o_ref, lse_ref, k_ref, v_ref, dq_ref, dkv_ref,
     qt_s, gt_s, q_s, g_s, delta_s,
 ):
     chunk = k_ref.shape[0]
 
-    @pl.when(pl.program_id(1) == 0)
+    @pl.when(pl.program_id(0) == 0)
     def _():
         query, grad = q_ref[...], g_ref[...]
         for j, part in enumerate(split_heads(query, 1)):
@@ -124,7 +124,7 @@
             delta_s[j] = jnp.sum(product[j * HEAD : (j + 1) * HEAD], 0, keepdims=True)
         dq_ref[...] = jnp.zeros_like(dq_ref)
 
-    bias = key_bias(length_ref[0], chunk)
+    bias = key_bias(meta_ref, chunk)
     keys_t = k_ref[...].T
     dk = dv = None
     for j in range(2):
@@ -138,30 +138,29 @@
         dv = dv_j if dv is None else dv + dv_j
         rows = slice(j * HEAD, (j + 1) * HEAD)
         dq_ref[rows] += jnp.dot(keys_t[rows], ds, preferred_element_type=jnp.float32)
-    dkv_ref[0] = dk.astype(jnp.bfloat16)
-    dkv_ref[1] = dv.astype(jnp.bfloat16)
-
-
-def attend_backward(query, joined, length, lse, mixed, grad, chunk=512):
-    frames, width = query.shape
+    dkv_ref[:, :PAIR] = dk.astype(jnp.bfloat16)
+    dkv_ref[:, PAIR:] = dv.astype(jnp.bfloat16)
+
+
+def attend_backward(query, grad, pair, joined, meta, lse, mixed, chunk):
+    frames = query.shape[0]
     keys = joined.shape[0]
-    pairs = width // PAIR
     return pl.pallas_call(
         attend_backward_kernel,
         grid_spec=pltpu.PrefetchScalarGridSpec(
             num_scalar_prefetch=1,
-            grid=(pairs, keys // chunk),
+            grid=(keys // chunk,),
             in_specs=[
-                pl.BlockSpec((frames, PAIR), lambda p, c, n: (0, p)),
-                pl.BlockSpec((frames, PAIR), lambda p, c, n: (0, p)),
-                pl.BlockSpec((PAIR, frames), lambda p, c, n: (p, 0)),
-                pl.BlockSpec((2, 1, frames), lambda p, c, n: (p, 0, 0)),
-                pl.BlockSpec((chunk, PAIR), lambda p, c, n: (c, p)),
-                pl.BlockSpec((chunk, PAIR), lambda p, c, n: (c, pairs + p)),
+                pl.BlockSpec((frames, PAIR), lambda c, n: (0, pair)),
+                pl.BlockSpec((frames, PAIR), lambda c, n: (0, pair)),
+                pl.BlockSpec((PAIR, frames), lambda c, n: (0, 0)),
+                pl.BlockSpec((2, 1, frames), lambda c, n: (0, 0, 0)),
+                pl.BlockSpec((chunk, PAIR), lambda c, n: (c, 0)),
+                pl.BlockSpec((chunk, PAIR), lambda c, n: (c, 1)),
             ],
             out_specs=[
-                pl.BlockSpec((PAIR, frames), lambda p, c, n: (p, 0)),
-                pl.BlockSpec((2, chunk, PAIR), lambda p, c, n: (0, c, p)),
+                pl.BlockSpec((PAIR, frames), lambda c, n: (0, 0)),
+                pl.BlockSpec((chunk, 2 * PAIR), lambda c, n: (c, 0)),
             ],
             scratch_shapes=[
                 pltpu.VMEM((2, PAIR, frames), jnp.bfloat16),
@@ -172,17 +171,17 @@
             ],
         ),
         out_shape=[
-            jax.ShapeDtypeStruct((width, frames), jnp.float32),
-            jax.ShapeDtypeStruct((2, keys, width), jnp.bfloat16),
+            jax.ShapeDtypeStruct((PAIR, frames), jnp.float32),
+            jax.ShapeDtypeStruct((keys, 2 * PAIR), jnp.bfloat16),
         ],
         compiler_params=pltpu.CompilerParams(vmem_limit_bytes=50 * 1024 * 1024),
         cost_estimate=pl.CostEstimate(
-            flops=10 * frames * keys * width,
-            bytes_accessed=8 * keys * width + 12 * frames * width,
-            transcendentals=2 * pairs * frames * keys,
+            flops=10 * frames * keys * PAIR,
+            bytes_accessed=8 * keys * PAIR + 12 * frames * PAIR,
+            transcendentals=2 * frames * keys,
         ),
         name="attend_backward",
-    )(length, query, grad, mixed, lse, joined, joined)
+    )(meta, query, grad, mixed, lse, joined, joined)
 
 
 def with_halo(cells, sides, width):
@@ -346,42 +345,60 @@
     return pieces
 
 
-def attend_all(query_low, joined_all, lengths):
-    batch, frames, heads, _ = query_low.shape
-    if (heads * HEAD) % PAIR:
-        return lax.map(attend_one, (query_low, joined_all, lengths))
-    mixed, totals = [], []
-    for row in range(batch):
-        out, total = attend_forward(
-            query_low[row].reshape(frames, -1), joined_all[row], lengths[row : row + 1]
-        )
-        mixed.append(out)
-        totals.append(total)
-    return (jnp.stack(mixed), jnp.stack(totals))
-
-
-def attend_all_back(query_low, joined_all, lengths, log_total, mixed, mixed_grad):
-    batch, frames, heads, _ = query_low.shape
-    if (heads * HEAD) % PAIR:
-        query_grad, joined_grad = lax.map(
-            attend_back, (query_low, joined_all, lengths, log_total, mixed_grad)
-        )
-        width = heads * HEAD
-        low = joined_grad.astype(jnp.bfloat16)
-        return (query_grad, jnp.stack([low[..., :width], low[..., width:]], 1))
-    queries, others = [], []
-    for row in range(batch):
-        query_grad, joined_grad = attend_backward(
-            query_low[row].reshape(frames, -1),
-            joined_all[row],
-            lengths[row : row + 1],
-            log_total[row],
-            mixed[row],
-            mixed_grad[row].reshape(frames, -1),
-        )
-        queries.append(query_grad.T.reshape(frames, heads, HEAD))
-        others.append(joined_grad)
-    return (jnp.stack(queries), jnp.stack(others))
+def swap(values, axis, bit):
+    return lax.ppermute(values, axis, [(i, i ^ bit) for i in range(lax.axis_size(axis))])
+
+
+def halve(values, axis, bit, dim):
+    own = lax.axis_index(axis) // bit % 2
+    keep = lax.dynamic_index_in_dim(values, own, dim, keepdims=False)
+    send = lax.dynamic_index_in_dim(values, 1 - own, dim, keepdims=False)
+    other = swap(send, axis, bit)
+    return (keep.astype(jnp.float32) + other.astype(jnp.float32)).astype(jnp.bfloat16)
+
+
+def double(values, axis, bit, dim):
+    own = lax.axis_index(axis) // bit % 2
+    other = swap(values, axis, bit)
+    return jnp.where(
+        own == 0, jnp.stack([values, other], dim), jnp.stack([other, values], dim)
+    )
+
+
+def reduce_by_swaps(grad):
+    if lax.axis_size("fsdp") != 4 or lax.axis_size("ctx") != 4:
+        return reduce_grads(pack_grads(grad), (grad.shape[0],) + grad.shape[1:])[0]
+    low = grad.astype(jnp.bfloat16).reshape(grad.shape[0], -1)
+    total = low.reshape(2, 2, 2, 2, -1, low.shape[1])
+    total = halve(total, "ctx", 1, 3)
+    total = halve(total, "ctx", 2, 2)
+    total = halve(total, "fsdp", 1, 1)
+    total = halve(total, "fsdp", 2, 0)
+    total = double(total, "ctx", 2, 0)
+    total = double(total, "ctx", 1, 1)
+    return total.astype(jnp.float32).reshape(-1, *grad.shape[1:])
+
+
+def attend_plan(lengths, frames, chunk):
+    me = lax.axis_index("ctx")
+    starts = [
+        (me ^ block) * frames + start for block in (0, 2, 1, 3) for start in range(0, frames, chunk)
+    ]
+    return jnp.stack([lengths[0]] + starts).astype(jnp.int32)
+
+
+def keys_everywhere(own):
+    far = swap(own, "ctx", 2)
+    near = swap(own, "ctx", 1)
+    return jnp.concatenate([own, far, near, swap(far, "ctx", 1)], 0)
+
+
+def keys_home(grads):
+    half = grads.shape[0] // 2
+    near = swap(grads[half:], "ctx", 1)
+    both = grads[:half].astype(jnp.float32) + near.astype(jnp.float32)
+    far = swap(both[half // 2 :].astype(jnp.bfloat16), "ctx", 2)
+    return both[: half // 2] + far.astype(jnp.float32)
 
 
 def product_rows(left, right):
@@ -512,14 +529,29 @@
         ],
         -1,
     )
-    joined_all = lax.all_gather(joined, "ctx", axis=1, tiled=True)
-    joined_all, late_up, late_down = lax.optimization_barrier((joined_all, final_up, final_down))
+    paired = local_width % PAIR == 0 and batch == 1 and lax.axis_size("ctx") == 4
+    pairs = local_width // PAIR
+    chunk = min(frames, 512)
+    if paired:
+        plan = attend_plan(lengths, frames, chunk)
+        query_rows = query_low.reshape(rows, local_width)
+        pair_keys, pair_out, pair_lse = [], [], []
+        for pair in range(pairs):
+            own = [
+                joined[0, :, side * local_width + pair * PAIR :][:, :PAIR] for side in range(2)
+            ]
+            pair_keys.append(keys_everywhere(jnp.concatenate(own, 1)))
+        for pair in range(pairs):
+            out, lse = attend_forward(query_rows, pair, pair_keys[pair], plan, chunk)
+            pair_out.append(out)
+            pair_lse.append(lse)
+        mixed_rows = jnp.concatenate([out.astype(jnp.bfloat16).T for out in pair_out], 1)
+    else:
+        joined_all = lax.all_gather(joined, "ctx", axis=1, tiled=True)
+        mixed, log_total = lax.map(attend_one, (query_low, joined_all, lengths))
+        mixed_rows = mixed.reshape(rows, local_width)
+    mixed_rows, late_up, late_down = lax.optimization_barrier((mixed_rows, final_up, final_down))
     up_two, down_two = gather_weights(late_up, late_down)
-    mixed, log_total = attend_all(query_low, joined_all, lengths)
-    if local_width % PAIR:
-        mixed_rows = mixed.reshape(rows, local_width)
-    else:
-        mixed_rows = mixed.astype(jnp.bfloat16).transpose(0, 2, 1).reshape(rows, local_width)
     after_two = after_one + tensor_total(product_rows(mixed_rows, proj_out))
     normed, norm_back_three = jax.vjp(layer_norm, after_two, norm_gains[2])
     normed_three = normed.astype(jnp.bfloat16)
@@ -618,14 +650,38 @@
     conv_in_grad, conv_out_grad, proj_out_grad = reduce_grads(
         early, mixer_in.shape, mixer_out.shape, attend_out.shape
     )
-    query_grad, joined_grad = attend_all_back(
-        query_low, joined_all, lengths, log_total, mixed, mixed_grad
-    )
-    joined_local = lax.psum_scatter(
-        joined_grad, "ctx", scatter_dimension=2, tiled=True
-    ).astype(jnp.float32)
-    key_grad = joined_local[:, 0].reshape(batch, frames, heads, HEAD)
-    value_grad = joined_local[:, 1].reshape(batch, frames, heads, HEAD)
+    if paired:
+        grad_rows = mixed_grad.reshape(rows, local_width)
+        home, queries = [], []
+        for pair in range(pairs):
+            query_part, keys_part = attend_backward(
+                query_rows,
+                grad_rows,
+                pair,
+                pair_keys[pair],
+                plan,
+                pair_lse[pair],
+                pair_out[pair],
+                chunk,
+            )
+            queries.append(query_part.T)
+            home.append(keys_home(keys_part))
+        query_grad = jnp.concatenate(queries, 1).reshape(batch, frames, heads, HEAD)
+        key_grad, value_grad = (
+            jnp.concatenate([part[:, side * PAIR :][:, :PAIR] for part in home], 1).reshape(
+                batch, frames, heads, HEAD
+            )
+            for side in range(2)
+        )
+    else:
+        query_grad, joined_grad = lax.map(
+            attend_back, (query_low, joined_all, lengths, log_total, mixed_grad)
+        )
+        joined_local = lax.psum_scatter(
+            joined_grad.astype(jnp.bfloat16), "ctx", scatter_dimension=1, tiled=True
+        ).astype(jnp.float32)
+        key_grad = joined_local[..., :local_width].reshape(batch, frames, heads, HEAD)
+        value_grad = joined_local[..., local_width:].reshape(batch, frames, heads, HEAD)
     query_raw_grad, key_raw_grad = rotate_back((query_grad, key_grad))
     proj_grad = (
         jnp.stack([query_raw_grad, key_raw_grad, value_grad], 2)
@@ -648,12 +704,9 @@
     gain_total, kernel_total = flat_sum(
         [gain_terms, kernel_local], [(("ctx",), 2), (("fsdp",), 3)]
     )
-    up_one_grad, down_one_grad, proj_in_grad = reduce_grads(
-        pack_grads(up_one_grad, down_one_grad, proj_in_grad),
-        feed_up.shape,
-        feed_down.shape,
-        attend_in.shape,
-    )
+    proj_in_grad = reduce_by_swaps(proj_in_grad)
+    down_one_grad = reduce_by_swaps(down_one_grad)
+    up_one_grad = reduce_by_swaps(up_one_grad)
     return (
         result.reshape(batch, frames, width),
         input_grad.reshape(batch, frames, width),

time: 728 us -> 660 us (0.907)
  waiting for transfers between devices: 328 us -> 212 us
  other arithmetic: 97.8 us -> 117 us
  starting transfers between devices: 19.7 us -> 38.8 us
  local copies, waits for them, and re-layouts: 44.1 us -> 60.8 us
  blocking collectives: 42.2 us -> 34.4 us
    reduce_scatter x3 -> x2, waiting for transfers between devices: 87.3 us -> 0.01 us  [reduce_grads(): lax.psum_scatter(packed, ('fsdp', 'ctx'), scatter_dimension=0, tiled=True)]
    ppermute x0 -> x28, waiting for transfers between devices: none -> 71.1 us  [swap(): lax.ppermute(values, axis, [(i, i ^ bit) for i in range(lax.axis_size(axi...]
    reduce_scatter x1 -> x0, waiting for transfers between devices: 43.9 us -> none  [per_device(): lax.psum_scatter(joined_grad, 'ctx', scatter_dimension=2, tiled=True)]
    all_gather x1 -> x0, waiting for transfers between devices: 31.6 us -> none  [per_device(): joined_all = lax.all_gather(joined, 'ctx', axis=1, tiled=True)]
    ppermute x0 -> x28, starting transfers between devices: none -> 19 us  [swap(): lax.ppermute(values, axis, [(i, i ^ bit) for i in range(lax.axis_size(axi...]
    ppermute x8, waiting for transfers between devices: 115 us -> 99.6 us  [tensor_total(): other = lax.ppermute(low, 'tp', [(0, 1), (1, 0)])]
    mul x2, other arithmetic: 9.65 us -> 22 us  [gate_linear(): return values[:, 0] * jax.nn.sigmoid(values[:, 1]) * live_rows]
    concatenate x1 -> x6, other arithmetic: 1.05 us -> 8.99 us  [the longest x2 6.18 us: keys_everywhere(): return jnp.concatenate([own, far, near, swap(far, 'ctx', 1)], 0)]
  transfers between devices with their start and end apart: 20 -> 45, of which waited for: 16 -> 23; matrix products, arithmetic and copies ran while one was open for 14% -> 17% of each run, Pallas kernels for 8% -> 17%
where the time goes in v3:
time: 660 us; the launch traced here: 651 us
  waiting for transfers between devices  212 us (32%)
  Pallas kernels  119 us (18%)
  other arithmetic  117 us (18%)
  local copies, waits for them, and re-layouts  60.8 us (9%)
  matrix products  52.1 us (8%)
  starting transfers between devices  38.8 us (6%)
  blocking collectives  34.4 us (5%)
  between operations  17.3 us (3%)
    ppermute x8, waiting for transfers between devices, tensor_total(): other = lax.ppermute(low, 'tp', [(0, 1), (1, 0)])  99.6 us
    ppermute x28, waiting for transfers between devices, swap(): lax.ppermute(values, axis, [(i, i ^ bit) for i in range(lax.axis_size(axi...  71.1 us
    pallas_call x2, Pallas kernels, attend_backward(): pl.pallas_call(attend_backward_kernel, grid_spec=pltpu.PrefetchScalarGrid...  50.5 us
    all_gather x3, waiting for transfers between devices, gather_weights(): whole = lax.all_gather(mine, ('fsdp', 'ctx'), axis=0, tiled=True)  40.7 us
    pallas_call x2, Pallas kernels, attend_forward(): pl.pallas_call(attend_forward_kernel, grid_spec=pltpu.PrefetchScalarGridS...  35.2 us
    pallas_call x4, Pallas kernels, group_sum(): pl.pallas_call(functools.partial(group_sum_kernel, axes, sizes), out_shap...  33 us
    unnamed x287, local copies, waits for them, and re-layouts  27.1 us
    mul x2, other arithmetic, gate_linear(): return values[:, 0] * jax.nn.sigmoid(values[:, 1]) * live_rows  22 us
  transfers between devices with their start and end apart: 45, of which 23 were waited for; matrix products, arithmetic and copies ran while one was open for 17% of the time, Pallas kernels for 17%

profile of v3, /device:TPU:0, one launch (start us, length us, event | category | flops | bytes accessed | tf_op | source)
XLA Modules:
  0.0 650.9 jit_solution(3683985663864077268)
XLA Ops:
  10.8 2.6 reduce_sum.609
  14.3 40.6 %all-gather.4.cloned.1.call-done = bf16[512,2048]{1,0:T(8,128)(2,1)} async-done(((bf16[32,2048]{1,0:T(8,128)(2,1)}), bf16[512,2048]{1,0:T(8,128)(2,1)}) %all-gather.4.cloned.1.call-update) | async-done | bytes 2097168 | tf_op jit(solution)/shard_map/all_gather | solution.py:314
  54.9 5.2 multiply_convert_fusion.1
  60.2 2.3 convolution_convert_fusion.9
  64.3 21.3 %all_gather.19 = bf16[512,768]{1,0:T(8,128)(2,1)S(1)} all-gather(bf16[32,768]{1,0:T(8,128)(2,1)S(1)} %copy.96), channel_id=1, replica_groups=mesh['fsdp'=4,'ctx'=4,'tp'=2] {'fsdp','ctx'}, dimensions={0}, use_global_device_ids=true | all-gather | bytes 835584 | tf_op jit(solution)/shard_map/all_gather | solution.py:314
  88.0 2.1 fusion.248
  99.9 12.1 %collective-permute-done.1 = bf16[1024,256]{1,0:T(8,128)(2,1)} collective-permute-done((bf16[1024,256]{1,0:T(8,128)(2,1)}, bf16[1024,256]{1,0:T(8,128)(2,1)}, u32[]{:S(2)}, u32[]{:S(2)}) %collective-permute-start.1) | collective-permute-done | bytes 524320 | tf_op jit(solution)/shard_map/ppermute | solution.py:349
  114.6 7.4 %collective-permute-done.4 = bf16[1024,256]{1,0:T(8,128)(2,1)} collective-permute-done((bf16[1024,256]{1,0:T(8,128)(2,1)}, bf16[1024,256]{1,0:T(8,128)(2,1)}, u32[]{:S(2)}, u32[]{:S(2)}) %collective-permute-start.4) | collective-permute-done | bytes 524320 | tf_op jit(solution)/shard_map/ppermute | solution.py:349
  122.0 3.1 pad_maximum_fusion.k_ref.v_ref
  125.1 17.6 %attend_forward.2 = (f32[128,1024]{1,0:T(8,128)S(1)}, f32[2,1,1024]{2,1,0:T(1,128)S(1)}) custom-call(s32[9]{0:T(128)S(1)} %stack.261.meta_ref, bf16[1024,256]{1,0:T(8,128)(2,1)S(1)} %copy.102.q_ref, bf16[4096,256]{1,0:T(8,128)(2,1)S(1)} %pad_maximum_fusion.k_ref.v_ref, bf16[4096,256]{1,0:T(8,128)(2,1)S(1)} %pad_maximum_fusion.k_ref.v_ref), custom_call_target="tpu_custom_call" | custom-call | flops 2147483648 | bytes 2883584 | tf_op jit(solution)/shard_map/attend_forward/pallas_call | solution.py:70
  142.8 3.1 pad_maximum_fusion.1.k_ref.v_ref
  145.9 17.6 %attend_forward.3 = (f32[128,1024]{1,0:T(8,128)S(1)}, f32[2,1,1024]{2,1,0:T(1,128)S(1)}) custom-call(s32[9]{0:T(128)S(1)} %stack.261.meta_ref, bf16[1024,256]{1,0:T(8,128)(2,1)S(1)} %copy-done.3, bf16[4096,256]{1,0:T(8,128)(2,1)S(1)} %pad_maximum_fusion.1.k_ref.v_ref, bf16[4096,256]{1,0:T(8,128)(2,1)S(1)} %pad_maximum_fusion.1.k_ref.v_ref), custom_call_target="tpu_custom_call" | custom-call | flops 2147483648 | bytes 2883584 | tf_op jit(solution)/shard_map/attend_forward/pallas_call | solution.py:70
  170.4 20.6 %collective-permute-done.7 = bf16[1024,512]{0,1:T(8,128)(2,1)} collective-permute-done((bf16[1024,512]{0,1:T(8,128)(2,1)S(1)}, bf16[1024,512]{0,1:T(8,128)(2,1)}, u32[]{:S(2)}, u32[]{:S(2)}) %collective-permute-start.7) | collective-permute-done | bytes 1048608 | tf_op jit(solution)/shard_map/ppermute | solution.py:229
  191.0 2.7 fusion.247
  202.8 8.7 %multiply_reduce_fusion.14 = (f32[256]{0:T(256)S(1)}, f32[256]{0:T(256)S(1)}, f32[1,1024,256]{2,1,0:T(8,128)}) fusion(f32[1024]{0:T(1024)S(1)} %fusion.210, bf16[1,15,256]{2,1,0:T(8,128)(2,1)S(1)} %collective-permute-done.9, bf16[1,1024,256]{2,1,0:T(8,128)(2,1)S(1)} %fusion.107, f32[256]{0:T(256)S(1)} %bitcast.446, f32[256]{0:T(256)S(1)} %bitcast.448, ...), kind=kLoop, calls=%fused_computation.159 | loop fusion | flops 48758272 | bytes 1626112 | tf_op jit(solution)/shard_map/reduce_sum | solution.py:576
  212.8 10.4 %group_sum_0.1 = f32[8,128]{1,0:T(8,128)} custom-call(f32[8,128]{1,0:T(8,128)} %fusion.207.x_ref), custom_call_target="tpu_custom_call" | custom-call | tf_op jit(solution)/shard_map/group_sum_0/pallas_call | solution.py:280
  228.0 23.8 %collective-permute-done.10 = bf16[1024,512]{0,1:T(8,128)(2,1)S(1)} collective-permute-done((bf16[1024,512]{0,1:T(8,128)(2,1)S(1)}, bf16[1024,512]{0,1:T(8,128)(2,1)S(1)}, u32[]{:S(2)}, u32[]{:S(2)}) %collective-permute-start.10) | collective-permute-done | bytes 1048608 | tf_op jit(solution)/shard_map/ppermute | solution.py:229
  254.0 5.9 multiply_convert_fusion
  260.0 2.3 convolution_convert_fusion.7
  263.6 2.9 copy.108
  266.5 20.3 %collective-permute-done.11 = bf16[1024,512]{0,1:T(8,128)(2,1)} collective-permute-done((bf16[1024,512]{0,1:T(8,128)(2,1)}, bf16[1024,512]{0,1:T(8,128)(2,1)}, u32[]{:S(2)}, u32[]{:S(2)}) %collective-permute-start.11) | collective-permute-done | bytes 1048608 | tf_op jit(solution)/shard_map/ppermute | solution.py:229
  286.9 2.7 fusion.244
  292.4 2.0 fusion.243
  294.4 2.3 copy-done.138
  296.7 2.4 fusion.2
  299.2 2.3 convolution_convert_fusion.4
  302.8 3.0 copy.131
  305.9 3.6 convolution_convert_fusion.5
  312.4 12.8 %collective-permute-done.12 = bf16[1024,512]{0,1:T(8,128)(2,1)} collective-permute-done((bf16[1024,512]{0,1:T(8,128)(2,1)}, bf16[1024,512]{0,1:T(8,128)(2,1)}, u32[]{:S(2)}, u32[]{:S(2)}) %collective-permute-start.12) | collective-permute-done | bytes 1048608 | tf_op jit(solution)/shard_map/ppermute | solution.py:229
  325.2 2.8 multiply_reduce_fusion.7
  328.0 3.3 multiply_reduce_fusion
  331.3 2.7 add_add_fusion.7
  337.8 8.0 %group_sum_1.1 = f32[8,128]{1,0:T(8,128)} custom-call(f32[8,128]{1,0:T(8,128)} %fusion.206.x_ref), custom_call_target="tpu_custom_call" | custom-call | tf_op jit(solution)/shard_map/group_sum_1/pallas_call | solution.py:280
  346.7 7.2 %fusion.92 = (f32[256]{0:T(256)}, f32[256]{0:T(256)}, f32[256]{0:T(256)}, f32[256]{0:T(256)}, f32[256]{0:T(256)}, /*index=5*/f32[256]{0:T(256)}, bf16[1,1024,256]{2,1,0:T(8,128)(2,1)S(1)}) fusion(bf16[1,15,256]{2,1,0:T(8,128)(2,1)S(1)} %collective-permute-done.9, bf16[1,1024,256]{2,1,0:T(8,128)(2,1)} %copy-done.12, f32[1,1024,256]{2,1,0:T(8,128)} %get-tuple-element.142, ...), kind=kLoop, calls=%fused_computation.290 | loop fusion | flops 11270656 | bytes 3166720 | tf_op jit(solution)/shard_map/reduce_sum | solution.py:629
  356.7 3.6 collective-permute-start.14
  360.3 2.0 convolution_convert_fusion.14
  364.3 21.7 %fusion.45 = (f32[1024,1,256]{2,0,1:T(8,128)S(1)}, f32[1024,1,256]{2,0,1:T(8,128)S(1)}) fusion(f32[1024,2,256]{2,0,1:T(8,128)} %copy-done.15, f32[1024]{0:T(1024)S(1)} %fusion.210, bf16[1,1024,256]{2,1,0:T(8,128)(2,1)} %copy-done.17, bf16[1,15,256]{2,1,0:T(8,128)(2,1)} %collective-permute-done.14, f32[256]{0:T(256)S(1)} %bitcast.447, f32[256]{0:T(256)S(1)} %bitcast.449, ...), kind=kLoop, calls=%fused_computation.243 | loop fusion | flops 49807360 | bytes 4769792 | tf_op jit(solution)/shard_map/transpose(jvp())/mul | solution.py:561
  394.8 2.1 copy.112
  396.8 18.1 %collective-permute-done.15 = bf16[1024,512]{0,1:T(8,128)(2,1)} collective-permute-done((bf16[1024,512]{0,1:T(8,128)(2,1)}, bf16[1024,512]{0,1:T(8,128)(2,1)}, u32[]{:S(2)}, u32[]{:S(2)}) %collective-permute-start.15) | collective-permute-done | bytes 1048608 | tf_op jit(solution)/shard_map/ppermute | solution.py:229
  414.9 3.0 multiply_reduce_fusion.1
  418.0 2.5 fusion.241
  425.4 2.6 convolution_convert_fusion.11
  430.8 25.3 %attend_backward.2 = (f32[128,1024]{1,0:T(8,128)S(1)}, bf16[4096,256]{1,0:T(8,128)(2,1)}) custom-call(s32[9]{0:T(128)S(1)} %stack.261.meta_ref, bf16[1024,256]{1,0:T(8,128)(2,1)S(1)} %copy-done.4, bf16[1024,256]{1,0:T(8,128)(2,1)S(1)} %copy.116.g_ref, f32[128,1024]{1,0:T(8,128)S(1)} %get-tuple-element.28.o_ref, f32[2,1,1024]{2,1,0:T(1,128)S(1)} %get-tuple-element.35.lse_ref, ...), custom_call_target="tpu_custom_call" | custom-call | flops 5368709120 | bytes 5767168 | tf_op jit(solution)/shard_map/attend_backward/pallas_call | solution.py:148
  456.1 2.3 slice.720
  458.4 25.2 %attend_backward.3 = (f32[128,1024]{1,0:T(8,128)S(1)}, bf16[4096,256]{1,0:T(8,128)(2,1)}) custom-call(s32[9]{0:T(128)S(1)} %stack.261.meta_ref, bf16[1024,256]{1,0:T(8,128)(2,1)S(1)} %copy-done.4, bf16[1024,256]{1,0:T(8,128)(2,1)S(1)} %copy.116.g_ref, f32[128,1024]{1,0:T(8,128)S(1)} %get-tuple-element.29.o_ref, f32[2,1,1024]{2,1,0:T(1,128)S(1)} %get-tuple-element.37.lse_ref, ...), custom_call_target="tpu_custom_call" | custom-call | flops 5368709120 | bytes 5767168 | tf_op jit(solution)/shard_map/attend_backward/pallas_call | solution.py:148
  491.2 1.9 collective-permute-start.19
  493.8 10.5 %collective-permute-done.17 = bf16[1024,256]{1,0:T(8,128)(2,1)S(1)} collective-permute-done((bf16[1024,256]{1,0:T(8,128)(2,1)S(1)}, bf16[1024,256]{1,0:T(8,128)(2,1)S(1)}, u32[]{:S(2)}, u32[]{:S(2)}) %collective-permute-start.17) | collective-permute-done | bytes 524320 | tf_op jit(solution)/shard_map/ppermute | solution.py:349
  504.4 10.2 %collective-permute-done.19 = bf16[1024,256]{1,0:T(8,128)(2,1)S(1)} collective-permute-done((bf16[1024,256]{1,0:T(8,128)(2,1)S(1)}, bf16[1024,256]{1,0:T(8,128)(2,1)S(1)}, u32[]{:S(2)}, u32[]{:S(2)}) %collective-permute-start.19) | collective-permute-done | bytes 524320 | tf_op jit(solution)/shard_map/ppermute | solution.py:349
  529.6 6.2 all_gather.22
  535.8 2.7 bitcast_convert_fusion
  539.2 6.8 %collective-permute-done.35 = bf16[2,2,32,768]{3,2,1,0:T(8,128)(2,1)S(1)} collective-permute-done((bf16[2,2,32,768]{3,2,1,0:T(8,128)(2,1)S(1)}, bf16[2,2,32,768]{3,2,1,0:T(8,128)(2,1)S(1)}, u32[]{:S(2)}, u32[]{:S(2)}) %collective-permute-start.35) | collective-permute-done | bytes 196640 | tf_op jit(solution)/shard_map/ppermute | solution.py:349
  553.4 6.9 %all_gather.23 = bf16[128,2048]{1,0:T(8,128)(2,1)S(1)} all-gather(bf16[32,2048]{1,0:T(8,128)(2,1)} %reduce-scatter.5.cloned.1.call-done), channel_id=1, replica_groups=mesh['fsdp'=4,'ctx'=4,'tp'=2] {'ctx'}, dimensions={0}, use_global_device_ids=true | all-gather | bytes 655360 | tf_op jit(solution)/shard_map/all_gather | solution.py:333
  568.8 3.3 collective-permute-done.20
  573.9 2.4 multiply_reduce_fusion.2
  576.4 2.6 add_add_fusion.5
  582.1 2.5 fusion.5
  591.5 6.8 %collective-permute-done.29 = bf16[2,2,32,1024]{3,2,0,1:T(8,128)(2,1)S(1)} collective-permute-done((bf16[2,2,32,1024]{3,2,0,1:T(8,128)(2,1)S(1)}, bf16[2,2,32,1024]{3,2,0,1:T(8,128)(2,1)S(1)}, u32[]{:S(2)}, u32[]{:S(2)}) %collective-permute-start.29) | collective-permute-done | bytes 262176 | tf_op jit(solution)/shard_map/ppermute | solution.py:349
  599.8 3.4 collective-permute-done.23
  606.3 2.8 collective-permute-done.24
  609.1 2.3 collective-permute-start.25
  611.9 3.2 collective-permute-done.25
  616.5 2.9 collective-permute-done.26
  623.2 6.0 group_sum_2.1.x_ref
  629.2 8.7 %group_sum_3.1 = f32[88,128]{1,0:T(8,128)} custom-call(f32[88,128]{1,0:T(8,128)} %group_sum_2.1.x_ref), custom_call_target="tpu_custom_call" | custom-call | tf_op jit(solution)/shard_map/group_sum_3/pallas_call | solution.py:280
  (534 shorter events, 145.6 us)
Async XLA Ops:
  7.2 47.8 %all-gather.4.cloned.1.call-start = ((), (), s32[]{:S(2)}) async-start(), calls=%async_computation.2 | async-start | bytes 2228224 | tf_op jit(solution)/shard_map/all_gather | solution.py:314
  8.8 154.9 %all-gather.6.cloned.1.call-start = ((), (), s32[]{:S(2)}) async-start(), calls=%async_computation.3 | async-start | bytes 1114112 | tf_op jit(solution)/shard_map/all_gather | solution.py:314
  10.8 77.3 %copy-start.5 = (f32[1,1024,512]{1,2,0:T(8,128)}, f32[1,1024,512]{1,2,0:T(8,128)S(1)}, u32[]{:S(2)}) copy-start(f32[1,1024,512]{1,2,0:T(8,128)S(1)} %copy.94) | copy-start | bytes 6291460
  13.7 46.5 %copy-start.55 = (f32[1024]{0:T(1024)}, f32[1024]{0:T(1024)S(1)}, u32[]{:S(2)}) copy-start(f32[1024]{0:T(1024)S(1)} %multiply_reduce_fusion.13) | copy-start | bytes 12292
  14.3 45.9 %copy-start.61 = (f32[1,512]{1,0:T(1,128)}, f32[1,512]{1,0:T(1,128)S(1)}, u32[]{:S(2)}) copy-start(f32[1,512]{1,0:T(1,128)S(1)} %get-tuple-element.206) | copy-start | bytes 6148
  14.3 510.1 %copy-start.63 = (f32[1,512]{1,0:T(1,128)}, f32[1,512]{1,0:T(1,128)S(1)}, u32[]{:S(2)}) copy-start(f32[1,512]{1,0:T(1,128)S(1)} %get-tuple-element.205) | copy-start | bytes 6148
  62.4 25.6 %collective-permute-start = (bf16[1024,512]{0,1:T(8,128)(2,1)}, bf16[1024,512]{0,1:T(8,128)(2,1)}, u32[]{:S(2)}, u32[]{:S(2)}) collective-permute-start(bf16[1024,512]{0,1:T(8,128)(2,1)} %convolution_convert_fusion.9), channel_id=1, source_target_pairs={{0,1},{1,0},{2,3},{3,2},{4,5},{5,4},{6,7},{7,6},{8,9},{9,8},{10,11... | collective-permute-start | bytes 3145736 | tf_op jit(solution)/shard_map/ppermute | solution.py:229
  96.9 15.1 %copy-start.51 = (bf16[128,2,256]{2,1,0:T(2,128)(2,1)S(1)}, bf16[128,2,256]{2,1,0:T(2,128)(2,1)}, u32[]{:S(2)}) copy-start(bf16[128,2,256]{2,1,0:T(2,128)(2,1)} %param.22) | copy-start | bytes 393220
  96.9 15.1 %copy-start.53 = (bf16[128,256]{1,0:T(8,128)(2,1)S(1)}, bf16[128,256]{1,0:T(8,128)(2,1)}, u32[]{:S(2)}) copy-start(bf16[128,256]{1,0:T(8,128)(2,1)} %param.21) | copy-start | bytes 196612
  96.9 15.2 %copy-start.54 = (bf16[128,256]{1,0:T(8,128)(2,1)S(1)}, bf16[128,256]{1,0:T(8,128)(2,1)}, u32[]{:S(2)}) copy-start(bf16[128,256]{1,0:T(8,128)(2,1)} %param.23) | copy-start | bytes 196612
  96.9 15.1 %collective-permute-start.1 = (bf16[1024,256]{1,0:T(8,128)(2,1)}, bf16[1024,256]{1,0:T(8,128)(2,1)}, u32[]{:S(2)}, u32[]{:S(2)}) collective-permute-start(bf16[1024,256]{1,0:T(8,128)(2,1)} %pad_maximum_fusion.14), channel_id=1, source_target_pairs={{0,4},{2,6},{4,0},{6,2},{1,5},{3,7},{5,1},{7,3},{8,12},{10,14},{12... | collective-permute-start | bytes 1572872 | tf_op jit(solution)/shard_map/ppermute | solution.py:349
  98.5 23.5 %collective-permute-start.4 = (bf16[1024,256]{1,0:T(8,128)(2,1)}, bf16[1024,256]{1,0:T(8,128)(2,1)}, u32[]{:S(2)}, u32[]{:S(2)}) collective-permute-start(bf16[1024,256]{1,0:T(8,128)(2,1)} %pad_maximum_fusion.15), channel_id=1, source_target_pairs={{0,4},{2,6},{4,0},{6,2},{1,5},{3,7},{5,1},{7,3},{8,12},{10,14},{12... | collective-permute-start | bytes 1572872 | tf_op jit(solution)/shard_map/ppermute | solution.py:349
  99.9 22.0 %collective-permute-start.2 = (bf16[1024,256]{1,0:T(8,128)(2,1)}, bf16[1024,256]{1,0:T(8,128)(2,1)}, u32[]{:S(2)}, u32[]{:S(2)}) collective-permute-start(bf16[1024,256]{1,0:T(8,128)(2,1)} %pad_maximum_fusion.14), channel_id=1, source_target_pairs={{0,2},{2,0},{4,6},{6,4},{1,3},{3,1},{5,7},{7,5},{8,10},{10,8},{12,... | collective-permute-start | bytes 1572872 | tf_op jit(solution)/shard_map/ppermute | solution.py:349
  112.0 10.0 %collective-permute-start.3 = (bf16[1024,256]{1,0:T(8,128)(2,1)}, bf16[1024,256]{1,0:T(8,128)(2,1)}, u32[]{:S(2)}, u32[]{:S(2)}) collective-permute-start(bf16[1024,256]{1,0:T(8,128)(2,1)} %collective-permute-done.1), channel_id=1, source_target_pairs={{0,2},{2,0},{4,6},{6,4},{1,3},{3,1},{5,7},{7,5},{8,10},{10,8},{12,... | collective-permute-start | bytes 1572872 | tf_op jit(solution)/shard_map/ppermute | solution.py:349
  112.7 141.3 %all-gather.8.cloned.1.call-start = ((), (), s32[]{:S(2)}) async-start(), calls=%async_computation.4 | async-start | bytes 2228224 | tf_op jit(solution)/shard_map/all_gather | solution.py:314
  113.7 29.0 %collective-permute-start.5 = (bf16[1024,256]{1,0:T(8,128)(2,1)}, bf16[1024,256]{1,0:T(8,128)(2,1)}, u32[]{:S(2)}, u32[]{:S(2)}) collective-permute-start(bf16[1024,256]{1,0:T(8,128)(2,1)} %pad_maximum_fusion.15), channel_id=1, source_target_pairs={{0,2},{2,0},{4,6},{6,4},{1,3},{3,1},{5,7},{7,5},{8,10},{10,8},{12,... | collective-permute-start | bytes 1572872 | tf_op jit(solution)/shard_map/ppermute | solution.py:349
  122.0 20.8 %collective-permute-start.6 = (bf16[1024,256]{1,0:T(8,128)(2,1)}, bf16[1024,256]{1,0:T(8,128)(2,1)S(1)}, u32[]{:S(2)}, u32[]{:S(2)}) collective-permute-start(bf16[1024,256]{1,0:T(8,128)(2,1)} %collective-permute-done.4), channel_id=1, source_target_pairs={{0,2},{2,0},{4,6},{6,4},{1,3},{3,1},{5,7},{7,5},{8,10},{10,8},{12,... | collective-permute-start | bytes 1572872 | tf_op jit(solution)/shard_map/ppermute | solution.py:349
  125.1 17.6 %copy-start = (bf16[4096,256]{1,0:T(8,128)(2,1)}, bf16[4096,256]{1,0:T(8,128)(2,1)S(1)}, u32[]{:S(2)}) copy-start(bf16[4096,256]{1,0:T(8,128)(2,1)S(1)} %pad_maximum_fusion.k_ref.v_ref) | copy-start | bytes 6291460
  145.9 17.6 %copy-start.1 = (bf16[4096,256]{1,0:T(8,128)(2,1)}, bf16[4096,256]{1,0:T(8,128)(2,1)S(1)}, u32[]{:S(2)}) copy-start(bf16[4096,256]{1,0:T(8,128)(2,1)S(1)} %pad_maximum_fusion.1.k_ref.v_ref) | copy-start | bytes 6291460
  165.3 25.7 %collective-permute-start.7 = (bf16[1024,512]{0,1:T(8,128)(2,1)S(1)}, bf16[1024,512]{0,1:T(8,128)(2,1)}, u32[]{:S(2)}, u32[]{:S(2)}) collective-permute-start(bf16[1024,512]{0,1:T(8,128)(2,1)S(1)} %convolution_convert_fusion), channel_id=1, source_target_pairs={{0,1},{1,0},{2,3},{3,2},{4,5},{5,4},{6,7},{7,6},{8,9},{9,8},{10,11... | collective-permute-start | bytes 3145736 | tf_op jit(solution)/shard_map/ppermute | solution.py:229
  167.1 35.4 %copy-start.68 = (f32[1,256]{1,0:T(1,128)}, f32[1,256]{1,0:T(1,128)S(1)}, u32[]{:S(2)}) copy-start(f32[1,256]{1,0:T(1,128)S(1)} %get-tuple-element.191) | copy-start | bytes 3076
  167.1 35.4 %copy-start.70 = (f32[1,256]{1,0:T(1,128)}, f32[1,256]{1,0:T(1,128)S(1)}, u32[]{:S(2)}) copy-start(f32[1,256]{1,0:T(1,128)S(1)} %get-tuple-element.192) | copy-start | bytes 3076
  167.1 35.4 %copy-start.72 = (f32[1,256]{1,0:T(1,128)}, f32[1,256]{1,0:T(1,128)S(1)}, u32[]{:S(2)}) copy-start(f32[1,256]{1,0:T(1,128)S(1)} %get-tuple-element.193) | copy-start | bytes 3076
  167.1 35.4 %copy-start.74 = (f32[1,256]{1,0:T(1,128)}, f32[1,256]{1,0:T(1,128)S(1)}, u32[]{:S(2)}) copy-start(f32[1,256]{1,0:T(1,128)S(1)} %get-tuple-element.194) | copy-start | bytes 3076
  167.1 35.4 %copy-start.76 = (f32[1,256]{1,0:T(1,128)}, f32[1,256]{1,0:T(1,128)S(1)}, u32[]{:S(2)}) copy-start(f32[1,256]{1,0:T(1,128)S(1)} %get-tuple-element.195) | copy-start | bytes 3076
  167.1 35.4 %copy-start.78 = (f32[1,256]{1,0:T(1,128)}, f32[1,256]{1,0:T(1,128)S(1)}, u32[]{:S(2)}) copy-start(f32[1,256]{1,0:T(1,128)S(1)} %get-tuple-element.196) | copy-start | bytes 3076
  167.1 35.4 %copy-start.80 = (f32[1,256]{1,0:T(1,128)}, f32[1,256]{1,0:T(1,128)S(1)}, u32[]{:S(2)}) copy-start(f32[1,256]{1,0:T(1,128)S(1)} %get-tuple-element.197) | copy-start | bytes 3076
  170.4 359.3 %reduce-scatter.3.cloned.1.call-start = ((), (), s32[]{:S(2)}) async-start(), calls=%async_computation.5 | async-start | bytes 1114112 | tf_op jit(solution)/shard_map/reduce_scatter | solution.py:332
  197.6 4.5 collective-permute-start.8
  199.1 3.4 collective-permute-start.9
  226.5 25.2 %collective-permute-start.10 = (bf16[1024,512]{0,1:T(8,128)(2,1)S(1)}, bf16[1024,512]{0,1:T(8,128)(2,1)S(1)}, u32[]{:S(2)}, u32[]{:S(2)}) collective-permute-start(bf16[1024,512]{0,1:T(8,128)(2,1)S(1)} %convolution_convert_fusion.8), channel_id=1, source_target_pairs={{0,1},{1,0},{2,3},{3,2},{4,5},{5,4},{6,7},{7,6},{8,9},{9,8},{10,11... | collective-permute-start | bytes 3145736 | tf_op jit(solution)/shard_map/ppermute | solution.py:229
  262.2 24.6 %collective-permute-start.11 = (bf16[1024,512]{0,1:T(8,128)(2,1)}, bf16[1024,512]{0,1:T(8,128)(2,1)}, u32[]{:S(2)}, u32[]{:S(2)}) collective-permute-start(bf16[1024,512]{0,1:T(8,128)(2,1)} %convolution_convert_fusion.7), channel_id=1, source_target_pairs={{0,1},{1,0},{2,3},{3,2},{4,5},{5,4},{6,7},{7,6},{8,9},{9,8},{10,11... | collective-permute-start | bytes 3145736 | tf_op jit(solution)/shard_map/ppermute | solution.py:229
  301.4 23.8 %collective-permute-start.12 = (bf16[1024,512]{0,1:T(8,128)(2,1)}, bf16[1024,512]{0,1:T(8,128)(2,1)}, u32[]{:S(2)}, u32[]{:S(2)}) collective-permute-start(bf16[1024,512]{0,1:T(8,128)(2,1)} %convolution_convert_fusion.4), channel_id=1, source_target_pairs={{0,1},{1,0},{2,3},{3,2},{4,5},{5,4},{6,7},{7,6},{8,9},{9,8},{10,11... | collective-permute-start | bytes 3145736 | tf_op jit(solution)/shard_map/ppermute | solution.py:229
  312.4 15.6 %copy-start.11 = (f32[1024,512]{0,1:T(8,128)S(1)}, f32[1024,512]{0,1:T(8,128)}, u32[]{:S(2)}) copy-start(f32[1024,512]{0,1:T(8,128)} %copy-done.9) | copy-start | bytes 6291460
  345.8 14.5 %copy-start.25 = (f32[1024,512]{0,1:T(8,128)S(1)}, f32[1024,512]{0,1:T(8,128)}, u32[]{:S(2)}) copy-start(f32[1024,512]{0,1:T(8,128)} %copy-done.24) | copy-start | bytes 6291460
  355.3 8.9 %collective-permute-start.13 = (bf16[1,15,256]{2,1,0:T(8,128)(2,1)}, bf16[1,15,256]{2,1,0:T(8,128)(2,1)}, u32[]{:S(2)}, u32[]{:S(2)}) collective-permute-start(bf16[1,15,256]{2,1,0:T(8,128)(2,1)} %get-tuple-element.162), channel_id=1, source_target_pairs={{2,0},{4,2},{6,4},{3,1},{5,3},{7,5},{10,8},{12,10},{14,12},{11,9},... | collective-permute-start | bytes 23048 | tf_op jit(solution)/shard_map/ppermute | solution.py:197
  356.7 7.5 %collective-permute-start.14 = (bf16[1,15,256]{2,1,0:T(8,128)(2,1)}, bf16[1,15,256]{2,1,0:T(8,128)(2,1)}, u32[]{:S(2)}, u32[]{:S(2)}) collective-permute-start(bf16[1,15,256]{2,1,0:T(8,128)(2,1)} %get-tuple-element.163), channel_id=1, source_target_pairs={{0,2},{2,4},{4,6},{1,3},{3,5},{5,7},{8,10},{10,12},{12,14},{9,11},... | collective-permute-start | bytes 23048 | tf_op jit(solution)/shard_map/ppermute | solution.py:195
  364.1 21.8 %copy-start.16 = (f32[1024,2,256]{2,0,1:T(8,128)S(1)}, f32[1024,2,256]{2,0,1:T(8,128)}, u32[]{:S(2)}) copy-start(f32[1024,2,256]{2,0,1:T(8,128)} %copy-done.15) | copy-start | bytes 6291460
  388.8 26.2 %collective-permute-start.15 = (bf16[1024,512]{0,1:T(8,128)(2,1)}, bf16[1024,512]{0,1:T(8,128)(2,1)}, u32[]{:S(2)}, u32[]{:S(2)}) collective-permute-start(bf16[1024,512]{0,1:T(8,128)(2,1)} %bitcast_convert_fusion.1), channel_id=1, source_target_pairs={{0,1},{1,0},{2,3},{3,2},{4,5},{5,4},{6,7},{7,6},{8,9},{9,8},{10,11... | collective-permute-start | bytes 3145736 | tf_op jit(solution)/shard_map/ppermute | solution.py:229
  428.0 125.4 %reduce-scatter.5.cloned.1.call-start = ((), (), s32[]{:S(2)}) async-start(), calls=%async_computation.6 | async-start | bytes 2228224 | tf_op jit(solution)/shard_map/reduce_scatter | solution.py:332
  458.4 29.0 %collective-permute-start.16 = (bf16[2048,256]{1,0:T(8,128)(2,1)}, bf16[2048,256]{1,0:T(8,128)(2,1)}, u32[]{:S(2)}, u32[]{:S(2)}) collective-permute-start(bf16[2048,256]{1,0:T(8,128)(2,1)} %slice.720), channel_id=1, source_target_pairs={{0,2},{2,0},{4,6},{6,4},{1,3},{3,1},{5,7},{7,5},{8,10},{10,8},{12,... | collective-permute-start | bytes 3145736 | tf_op jit(solution)/shard_map/ppermute | solution.py:349
  485.0 4.4 collective-permute-start.18
  489.4 14.9 %collective-permute-start.17 = (bf16[1024,256]{1,0:T(8,128)(2,1)S(1)}, bf16[1024,256]{1,0:T(8,128)(2,1)S(1)}, u32[]{:S(2)}, u32[]{:S(2)}) collective-permute-start(bf16[1024,256]{1,0:T(8,128)(2,1)S(1)} %slice.1509), channel_id=1, source_target_pairs={{0,4},{2,6},{4,0},{6,2},{1,5},{3,7},{5,1},{7,3},{8,12},{10,14},{12... | collective-permute-start | bytes 1572872 | tf_op jit(solution)/shard_map/ppermute | solution.py:349
  491.2 23.4 %collective-permute-start.19 = (bf16[1024,256]{1,0:T(8,128)(2,1)S(1)}, bf16[1024,256]{1,0:T(8,128)(2,1)S(1)}, u32[]{:S(2)}, u32[]{:S(2)}) collective-permute-start(bf16[1024,256]{1,0:T(8,128)(2,1)S(1)} %slice.1508), channel_id=1, source_target_pairs={{0,4},{2,6},{4,0},{6,2},{1,5},{3,7},{5,1},{7,3},{8,12},{10,14},{12... | collective-permute-start | bytes 1572872 | tf_op jit(solution)/shard_map/ppermute | solution.py:349
  529.6 9.0 %collective-permute-start.34 = (bf16[2,2,2,32,768]{4,3,2,1,0:T(8,128)(2,1)}, bf16[2,2,2,32,768]{4,3,2,1,0:T(8,128)(2,1)S(1)}, u32[]{:S(2)}, u32[]{:S(2)}) collective-permute-start(bf16[2,2,2,32,768]{4,3,2,1,0:T(8,128)(2,1)} %dynamic-slice_bitcast_fusion.1), channel_id=1, source_target_pairs={{0,2},{2,0},{4,6},{6,4},{1,3},{3,1},{5,7},{7,5},{8,10},{10,8},{12,... | collective-permute-start | bytes 1179656 | tf_op jit(solution)/shard_map/ppermute | solution.py:349
  538.8 7.2 %collective-permute-start.35 = (bf16[2,2,32,768]{3,2,1,0:T(8,128)(2,1)S(1)}, bf16[2,2,32,768]{3,2,1,0:T(8,128)(2,1)S(1)}, u32[]{:S(2)}, u32[]{:S(2)}) collective-permute-start(bf16[2,2,32,768]{3,2,1,0:T(8,128)(2,1)S(1)} %dynamic-slice_bitcast_fusion.4), channel_id=1, source_target_pairs={{0,4},{2,6},{4,0},{6,2},{1,5},{3,7},{5,1},{7,3},{8,12},{10,14},{12... | collective-permute-start | bytes 589832 | tf_op jit(solution)/shard_map/ppermute | solution.py:349
  546.1 4.8 collective-permute-start.36
  547.6 24.5 %collective-permute-start.20 = (bf16[1024,512]{0,1:T(8,128)(2,1)S(1)}, bf16[1024,512]{0,1:T(8,128)(2,1)}, u32[]{:S(2)}, u32[]{:S(2)}) collective-permute-start(bf16[1024,512]{0,1:T(8,128)(2,1)S(1)} %bitcast_convert_fusion), channel_id=1, source_target_pairs={{0,1},{1,0},{2,3},{3,2},{4,5},{5,4},{6,7},{7,6},{8,9},{9,8},{10,11... | collective-permute-start | bytes 3145736 | tf_op jit(solution)/shard_map/ppermute | solution.py:229
  551.8 8.4 %collective-permute-start.37 = (bf16[32,768]{1,0:T(8,128)(2,1)S(1)}, bf16[32,768]{1,0:T(8,128)(2,1)S(1)}, u32[]{:S(2)}, u32[]{:S(2)}) collective-permute-start(bf16[32,768]{1,0:T(8,128)(2,1)S(1)} %dynamic-slice_bitcast_fusion.10), channel_id=1, source_target_pairs={{0,16},{8,24},{16,0},{24,8},{1,17},{9,25},{17,1},{25,9},{2,18},{10... | collective-permute-start | bytes 147464 | tf_op jit(solution)/shard_map/ppermute | solution.py:349
  560.3 4.2 collective-permute-start.38
  564.5 1.4 collective-permute-start.39
  580.4 8.5 %collective-permute-start.28 = (bf16[2,2,2,32,1024]{4,3,0,1,2:T(8,128)(2,1)S(1)}, bf16[2,2,2,32,1024]{4,3,0,1,2:T(8,128)(2,1)S(1)}, u32[]{:S(2)}, u32[]{:S(2)}) collective-permute-start(bf16[2,2,2,32,1024]{4,3,0,1,2:T(8,128)(2,1)S(1)} %bitcast.386), channel_id=1, source_target_pairs={{0,2},{2,0},{4,6},{6,4},{1,3},{3,1},{5,7},{7,5},{8,10},{10,8},{12,... | collective-permute-start | bytes 1572872 | tf_op jit(solution)/shard_map/ppermute | solution.py:349
  586.0 3.5 collective-permute-start.22
  587.4 32.2 %collective-permute-start.21 = (bf16[1024,512]{0,1:T(8,128)(2,1)S(1)}, bf16[1024,512]{0,1:T(8,128)(2,1)S(1)}, u32[]{:S(2)}, u32[]{:S(2)}) collective-permute-start(bf16[1024,512]{0,1:T(8,128)(2,1)S(1)} %convolution_convert_fusion.3), channel_id=1, source_target_pairs={{0,1},{1,0},{2,3},{3,2},{4,5},{5,4},{6,7},{7,6},{8,9},{9,8},{10,11... | collective-permute-start | bytes 3145736 | tf_op jit(solution)/shard_map/ppermute | solution.py:229
  589.1 9.2 %collective-permute-start.29 = (bf16[2,2,32,1024]{3,2,0,1:T(8,128)(2,1)S(1)}, bf16[2,2,32,1024]{3,2,0,1:T(8,128)(2,1)S(1)}, u32[]{:S(2)}, u32[]{:S(2)}) collective-permute-start(bf16[2,2,32,1024]{3,2,0,1:T(8,128)(2,1)S(1)} %dynamic-slice_bitcast_fusion.2), channel_id=1, source_target_pairs={{0,4},{2,6},{4,0},{6,2},{1,5},{3,7},{5,1},{7,3},{8,12},{10,14},{12... | collective-permute-start | bytes 786440 | tf_op jit(solution)/shard_map/ppermute | solution.py:349
  589.8 13.5 %collective-permute-start.23 = (bf16[2,2,32,1024]{3,2,1,0:T(8,128)(2,1)S(1)}, bf16[2,2,32,1024]{3,2,1,0:T(8,128)(2,1)S(1)}, u32[]{:S(2)}, u32[]{:S(2)}) collective-permute-start(bf16[2,2,32,1024]{3,2,1,0:T(8,128)(2,1)S(1)} %dynamic-slice_bitcast_fusion.3), channel_id=1, source_target_pairs={{0,4},{2,6},{4,0},{6,2},{1,5},{3,7},{5,1},{7,3},{8,12},{10,14},{12... | collective-permute-start | bytes 786440 | tf_op jit(solution)/shard_map/ppermute | solution.py:349
  598.5 6.2 collective-permute-start.30
  603.3 5.7 collective-permute-start.24
  604.7 6.7 %collective-permute-start.31 = (bf16[32,1024]{1,0:T(8,128)(2,1)S(1)}, bf16[32,1024]{1,0:T(8,128)(2,1)S(1)}, u32[]{:S(2)}, u32[]{:S(2)}) collective-permute-start(bf16[32,1024]{1,0:T(8,128)(2,1)S(1)} %dynamic-slice_bitcast_fusion.8), channel_id=1, source_target_pairs={{0,16},{8,24},{16,0},{24,8},{1,17},{9,25},{17,1},{25,9},{2,18},{10... | collective-permute-start | bytes 196616 | tf_op jit(solution)/shard_map/ppermute | solution.py:349
  609.1 5.9 collective-permute-start.25
  611.4 5.0 collective-permute-start.32
  615.1 4.3 collective-permute-start.26
  616.4 26.0 %collective-permute-start.33 = (bf16[2,32,1024]{2,1,0:T(8,128)(2,1)S(1)}, bf16[2,32,1024]{2,1,0:T(8,128)(2,1)S(1)}, u32[]{:S(2)}, u32[]{:S(2)}) collective-permute-start(bf16[2,32,1024]{2,1,0:T(8,128)(2,1)S(1)} %maximum_select_fusion.5), channel_id=1, source_target_pairs={{0,2},{2,0},{4,6},{6,4},{1,3},{3,1},{5,7},{7,5},{8,10},{10,8},{12,... | collective-permute-start | bytes 393224 | tf_op jit(solution)/shard_map/ppermute | solution.py:349
  619.4 23.8 %collective-permute-start.27 = (bf16[2,32,1024]{2,1,0:T(8,128)(2,1)S(1)}, bf16[2,32,1024]{2,1,0:T(8,128)(2,1)S(1)}, u32[]{:S(2)}, u32[]{:S(2)}) collective-permute-start(bf16[2,32,1024]{2,1,0:T(8,128)(2,1)S(1)} %maximum_select_fusion.4), channel_id=1, source_target_pairs={{0,2},{2,0},{4,6},{6,4},{1,3},{3,1},{5,7},{7,5},{8,10},{10,8},{12,... | collective-permute-start | bytes 393224 | tf_op jit(solution)/shard_map/ppermute | solution.py:349
  (121 other events, 473.1 us)
Sparse Core Ops, SparseCore 0:
  10.7 44.1 all-gather.3
  112.8 36.7 all-gather.5
  170.5 39.3 all-gather.7
  428.2 56.8 reduce-scatter.2
  488.7 60.9 reduce-scatter.4

commit v4 on v3

--- a/solution.py
+++ b/solution.py
@@ -28,7 +28,11 @@
     return jnp.where(spot < meta_ref[0], 0.0, masked_score)
 
 
-def attend_forward_kernel(meta_ref, q_ref, k_ref, v_ref, o_ref, lse_ref, qt_s, top_s, sum_s):
+def attend_forward_kernel(last, meta_ref, q_ref, k_ref, v_ref, *refs):
+    if last:
+        o_in, top_in, sum_in, o_ref, lse_ref, qt_s, top_s, sum_s = refs
+    else:
+        o_ref, top_s, sum_s, qt_s = refs
     chunk = k_ref.shape[0]
     step = pl.program_id(0)
 
@@ -37,9 +41,14 @@
         first, second = split_heads(q_ref[...].T, 0)
         qt_s[0] = first
         qt_s[1] = second
-        top_s[...] = jnp.full_like(top_s, -jnp.inf)
-        sum_s[...] = jnp.zeros_like(sum_s)
-        o_ref[...] = jnp.zeros_like(o_ref)
+        if last:
+            top_s[...] = top_in[...]
+            sum_s[...] = sum_in[...]
+            o_ref[...] = o_in[...]
+        else:
+            top_s[...] = jnp.full_like(top_s, -jnp.inf)
+            sum_s[...] = jnp.zeros_like(sum_s)
+            o_ref[...] = jnp.zeros_like(o_ref)
 
     bias = key_bias(meta_ref, chunk)
     values = v_ref[...].T
@@ -56,19 +65,26 @@
             values[rows], raised.astype(jnp.bfloat16), preferred_element_type=jnp.float32
         )
 
-    @pl.when(step == pl.num_programs(0) - 1)
-    def _():
-        for j in range(2):
-            rows = slice(j * HEAD, (j + 1) * HEAD)
-            o_ref[rows] = o_ref[rows] / sum_s[j]
-            lse_ref[j] = top_s[j] + jnp.log(sum_s[j])
-
-
-def attend_forward(query, pair, joined, meta, chunk):
+    if last:
+
+        @pl.when(step == pl.num_programs(0) - 1)
+        def _():
+            for j in range(2):
+                rows = slice(j * HEAD, (j + 1) * HEAD)
+                o_ref[rows] = o_ref[rows] / sum_s[j]
+                lse_ref[j] = top_s[j] + jnp.log(sum_s[j])
+
+
+def attend_forward(query, pair, joined, meta, chunk, state):
     frames = query.shape[0]
     keys = joined.shape[0]
+    last = len(state) > 0
+    wide = pl.BlockSpec((PAIR, frames), lambda c, n: (0, 0))
+    row = pl.BlockSpec((2, 1, frames), lambda c, n: (0, 0, 0))
+    row_scratch = pltpu.VMEM((2, 1, frames), jnp.float32)
+    row_shape = jax.ShapeDtypeStruct((2, 1, frames), jnp.float32)
     return pl.pallas_call(
-        attend_forward_kernel,
+        functools.partial(attend_forward_kernel, last),
         grid_spec=pltpu.PrefetchScalarGridSpec(
             num_scalar_prefetch=1,
             grid=(keys // chunk,),
@@ -76,29 +92,22 @@
                 pl.BlockSpec((frames, PAIR), lambda c, n: (0, pair)),
                 pl.BlockSpec((chunk, PAIR), lambda c, n: (c, 0)),
                 pl.BlockSpec((chunk, PAIR), lambda c, n: (c, 1)),
-            ],
-            out_specs=[
-                pl.BlockSpec((PAIR, frames), lambda c, n: (0, 0)),
-                pl.BlockSpec((2, 1, frames), lambda c, n: (0, 0, 0)),
-            ],
-            scratch_shapes=[
-                pltpu.VMEM((2, PAIR, frames), jnp.bfloat16),
-                pltpu.VMEM((2, 1, frames), jnp.float32),
-                pltpu.VMEM((2, 1, frames), jnp.float32),
-            ],
+            ]
+            + ([wide, row, row] if last else []),
+            out_specs=[wide, row] if last else [wide, row, row],
+            scratch_shapes=[pltpu.VMEM((2, PAIR, frames), jnp.bfloat16)]
+            + ([row_scratch, row_scratch] if last else []),
         ),
-        out_shape=[
-            jax.ShapeDtypeStruct((PAIR, frames), jnp.float32),
-            jax.ShapeDtypeStruct((2, 1, frames), jnp.float32),
-        ],
+        out_shape=[jax.ShapeDtypeStruct((PAIR, frames), jnp.float32), row_shape]
+        + ([] if last else [row_shape]),
         compiler_params=pltpu.CompilerParams(vmem_limit_bytes=50 * 1024 * 1024),
         cost_estimate=pl.CostEstimate(
-            flops=4 * frames * keys * PAIR,
+            flops=16 * frames * keys * PAIR,
             bytes_accessed=4 * keys * PAIR + 6 * frames * PAIR,
             transcendentals=2 * frames * keys,
         ),
         name="attend_forward",
-    )(meta, query, joined, joined)
+    )(meta, query, joined, joined, *state)
 
 
 def attend_backward_kernel(
@@ -176,7 +185,7 @@
         ],
         compiler_params=pltpu.CompilerParams(vmem_limit_bytes=50 * 1024 * 1024),
         cost_estimate=pl.CostEstimate(
-            flops=10 * frames * keys * PAIR,
+            flops=30 * frames * keys * PAIR,
             bytes_accessed=8 * keys * PAIR + 12 * frames * PAIR,
             transcendentals=2 * frames * keys,
         ),
@@ -330,7 +339,10 @@
 
 def reduce_grads(packed, *shapes):
     part = lax.psum_scatter(packed, ("fsdp", "ctx"), scatter_dimension=0, tiled=True)
-    whole = lax.all_gather(part, "ctx", axis=0, tiled=True)
+    if lax.axis_size("ctx") == 4:
+        whole = double(double(part, "ctx", 2, 0), "ctx", 1, 1).reshape(-1, part.shape[1])
+    else:
+        whole = lax.all_gather(part, "ctx", axis=0, tiled=True)
     pieces, start = [], 0
     for shape in shapes:
         width = 1
@@ -379,26 +391,36 @@
     return total.astype(jnp.float32).reshape(-1, *grad.shape[1:])
 
 
-def attend_plan(lengths, frames, chunk):
+def attend_plans(lengths, frames, chunk):
     me = lax.axis_index("ctx")
-    starts = [
-        (me ^ block) * frames + start for block in (0, 2, 1, 3) for start in range(0, frames, chunk)
+    return [
+        jnp.stack(
+            [lengths[0]]
+            + [
+                (me ^ block) * frames + start
+                for block in blocks
+                for start in range(0, frames, chunk)
+            ]
+        ).astype(jnp.int32)
+        for blocks in ((0, 1), (2, 3))
     ]
-    return jnp.stack([lengths[0]] + starts).astype(jnp.int32)
-
-
-def keys_everywhere(own):
-    far = swap(own, "ctx", 2)
-    near = swap(own, "ctx", 1)
-    return jnp.concatenate([own, far, near, swap(far, "ctx", 1)], 0)
-
-
-def keys_home(grads):
-    half = grads.shape[0] // 2
-    near = swap(grads[half:], "ctx", 1)
-    both = grads[:half].astype(jnp.float32) + near.astype(jnp.float32)
-    far = swap(both[half // 2 :].astype(jnp.bfloat16), "ctx", 2)
-    return both[: half // 2] + far.astype(jnp.float32)
+
+
+def sum_by_swaps(arrays, axes):
+    flat = jnp.concatenate([array.reshape(-1) for array in arrays])
+    size = flat.shape[0]
+    flat = jnp.pad(flat, (0, -size % 1024)).reshape(-1, 128)
+    for axis in axes:
+        bit = 1
+        while bit < lax.axis_size(axis):
+            flat = flat + swap(flat, axis, bit)
+            bit *= 2
+    flat = flat.reshape(-1)
+    pieces, start = [], 0
+    for array in arrays:
+        pieces.append(lax.slice_in_dim(flat, start, start + array.size).reshape(array.shape))
+        start += array.size
+    return pieces
 
 
 def product_rows(left, right):
@@ -423,7 +445,7 @@
     return (branch, (norm_back, normed_low, active_back, active_low))
 
 
-def feed_backward(branch_grad, saved, weight_up, weight_down):
+def feed_backward(branch_grad, saved, weight_up, weight_down, gain_early):
     norm_back, normed_low, active_back, active_low = saved
     grad_low = branch_grad.astype(jnp.bfloat16)
     down_grad = product_cols(grad_low, active_low)
@@ -431,9 +453,13 @@
         0
     ].astype(jnp.bfloat16)
     up_grad = product_cols(normed_low, hidden_grad)
-    normed_grad = tensor_total(product_rows(hidden_grad, weight_up))
-    stream_grad, gain_grad = norm_back(normed_grad)
-    return (stream_grad, gain_grad, up_grad, down_grad)
+    normed_part = product_rows(hidden_grad, weight_up)
+    _, gain_part = norm_back(normed_part)
+    normed_low_grad = normed_part.astype(jnp.bfloat16)
+    if gain_early:
+        gain_part, normed_low_grad = lax.optimization_barrier((gain_part, normed_low_grad))
+    stream_grad, _ = norm_back(tensor_total(normed_low_grad))
+    return (stream_grad, gain_part, up_grad, down_grad)
 
 
 def split_joined(joined, heads):
@@ -533,16 +559,33 @@
     pairs = local_width // PAIR
     chunk = min(frames, 512)
     if paired:
-        plan = attend_plan(lengths, frames, chunk)
+        near_plan, far_plan = attend_plans(lengths, frames, chunk)
         query_rows = query_low.reshape(rows, local_width)
-        pair_keys, pair_out, pair_lse = [], [], []
+        owns = [
+            jnp.concatenate(
+                [joined[0, :, side * local_width + pair * PAIR :][:, :PAIR] for side in range(2)],
+                1,
+            )
+            for pair in range(pairs)
+        ]
+        cores = [swap(own, "ctx", 1) for own in owns]
+        chips = [swap(own, "ctx", 2) for own in owns]
+        near_keys = [jnp.concatenate([own, core], 0) for own, core in zip(owns, cores)]
+        far_keys, states, pair_out, pair_lse = [], [], [], []
         for pair in range(pairs):
-            own = [
-                joined[0, :, side * local_width + pair * PAIR :][:, :PAIR] for side in range(2)
-            ]
-            pair_keys.append(keys_everywhere(jnp.concatenate(own, 1)))
+            state = attend_forward(query_rows, pair, near_keys[pair], near_plan, chunk, ())
+            near_plan, far_plan, chip, *state = lax.optimization_barrier(
+                (near_plan, far_plan, chips[pair], *state)
+            )
+            states.append(state)
+            far_keys.append(jnp.concatenate([chip, swap(chip, "ctx", 1)], 0))
         for pair in range(pairs):
-            out, lse = attend_forward(query_rows, pair, pair_keys[pair], plan, chunk)
+            out, lse = attend_forward(
+                query_rows, pair, far_keys[pair], far_plan, chunk, tuple(states[pair])
+            )
+            near_plan, far_plan, out, lse = lax.optimization_barrier(
+                (near_plan, far_plan, out, lse)
+            )
             pair_out.append(out)
             pair_lse.append(lse)
         mixed_rows = jnp.concatenate([out.astype(jnp.bfloat16).T for out in pair_out], 1)
@@ -593,7 +636,7 @@
     result, final_back = jax.vjp(layer_norm, after_four, norm_gains[4])
     grad_four, gain_five = final_back(cotangent)
     stream_grad, gain_four, up_two_grad, down_two_grad = feed_backward(
-        0.5 * grad_four, saved_four, up_two, down_two
+        0.5 * grad_four, saved_four, up_two, down_two, False
     )
     grad_three = grad_four + stream_grad
     early, grad_three = lax.optimization_barrier(
@@ -630,6 +673,7 @@
         )
     kernel_local = jnp.stack(kernel_terms)
     gates_grad = gate_back(gated_grad.reshape(rows, channels))[0].astype(jnp.bfloat16)
+    (kernel_total,) = sum_by_swaps([kernel_local], ("ctx", "fsdp"))
     conv_in_grad = jnp.einsum(
         "nd,nke->dke", normed_three, gates_grad, preferred_element_type=jnp.float32
     )
@@ -637,6 +681,10 @@
         jnp.einsum("nke,dke->nd", gates_grad, conv_in, preferred_element_type=jnp.float32)
     )
     stream_grad, gain_three = norm_back_three(normed_grad)
+    share = 1.0 / lax.axis_size("tp")
+    gain_three, gain_four, gain_five = sum_by_swaps(
+        [gain_three * share, gain_four, gain_five * share], ("ctx", "fsdp", "tp")
+    )
     grad_two = grad_three + stream_grad
     branch_low = grad_two.astype(jnp.bfloat16)
     proj_out_grad = product_cols(branch_low, mixed_rows)
@@ -652,20 +700,36 @@
     )
     if paired:
         grad_rows = mixed_grad.reshape(rows, local_width)
-        home, queries = [], []
+        half = frames
+        far_grads, far_parts, home, queries = [], [], [], []
         for pair in range(pairs):
-            query_part, keys_part = attend_backward(
-                query_rows,
-                grad_rows,
-                pair,
-                pair_keys[pair],
-                plan,
-                pair_lse[pair],
-                pair_out[pair],
-                chunk,
+            query_far, keys_far = attend_backward(
+                query_rows, grad_rows, pair, far_keys[pair], far_plan,
+                pair_lse[pair], pair_out[pair], chunk,
             )
-            queries.append(query_part.T)
-            home.append(keys_home(keys_part))
+            near_plan, far_plan, query_far, keys_far = lax.optimization_barrier(
+                (near_plan, far_plan, query_far, keys_far)
+            )
+            queries.append(query_far)
+            far_grads.append((keys_far[:half], swap(keys_far[half:], "ctx", 1)))
+        for pair in range(pairs):
+            one, other = far_grads[pair]
+            part = (one.astype(jnp.float32) + other.astype(jnp.float32)).astype(jnp.bfloat16)
+            near_plan, part = lax.optimization_barrier((near_plan, part))
+            far_parts.append(swap(part, "ctx", 2))
+            query_near, keys_near = attend_backward(
+                query_rows, grad_rows, pair, near_keys[pair], near_plan,
+                pair_lse[pair], pair_out[pair], chunk,
+            )
+            near_plan, query_near, keys_near = lax.optimization_barrier(
+                (near_plan, query_near, keys_near)
+            )
+            queries[pair] = (queries[pair] + query_near).T
+            home.append((keys_near[:half], swap(keys_near[half:], "ctx", 1)))
+        home = [
+            one.astype(jnp.float32) + other.astype(jnp.float32) + far.astype(jnp.float32)
+            for (one, other), far in zip(home, far_parts)
+        ]
         query_grad = jnp.concatenate(queries, 1).reshape(batch, frames, heads, HEAD)
         key_grad, value_grad = (
             jnp.concatenate([part[:, side * PAIR :][:, :PAIR] for part in home], 1).reshape(
@@ -688,22 +752,23 @@
         .reshape(rows, 3, local_width)
         .astype(jnp.bfloat16)
     )
+    normed_part = jnp.einsum(
+        "nke,dke->nd", proj_grad, proj_in, preferred_element_type=jnp.float32
+    ).astype(jnp.bfloat16)
+    normed_part, proj_late = lax.optimization_barrier((normed_part, proj_grad))
     proj_in_grad = jnp.einsum(
-        "nd,nke->dke", normed_two, proj_grad, preferred_element_type=jnp.float32
-    )
-    normed_grad = tensor_total(
-        jnp.einsum("nke,dke->nd", proj_grad, proj_in, preferred_element_type=jnp.float32)
-    )
+        "nd,nke->dke", normed_two, proj_late, preferred_element_type=jnp.float32
+    )
+    normed_grad = tensor_total(normed_part)
     stream_grad, gain_two = norm_back_two(normed_grad)
     grad_one = grad_two + stream_grad
     stream_grad, gain_one, up_one_grad, down_one_grad = feed_backward(
-        0.5 * grad_one, saved_one, up_one, down_one
+        0.5 * grad_one, saved_one, up_one, down_one, True
     )
     input_grad = grad_one + stream_grad
-    gain_terms = jnp.stack([gain_one, gain_two, gain_three, gain_four, gain_five])
-    gain_total, kernel_total = flat_sum(
-        [gain_terms, kernel_local], [(("ctx",), 2), (("fsdp",), 3)]
-    )
+    share = 1.0 / lax.axis_size("tp")
+    gain_one, gain_two = sum_by_swaps([gain_one, gain_two * share], ("ctx", "fsdp", "tp"))
+    gain_total = jnp.stack([gain_one, gain_two, gain_three, gain_four, gain_five])
     proj_in_grad = reduce_by_swaps(proj_in_grad)
     down_one_grad = reduce_by_swaps(down_one_grad)
     up_one_grad = reduce_by_swaps(up_one_grad)

time: 660 us -> 630 us (0.955)
  blocking collectives: 34.4 us -> 22 us
  Pallas kernels: 119 us -> 109 us
  other arithmetic: 117 us -> 110 us
    pallas_call x4 -> x2, Pallas kernels: 33 us -> 18.4 us  [group_sum(): pl.pallas_call(functools.partial(group_sum_kernel, axes, sizes), out_shap...]
    all_gather x2 -> x0, blocking collectives: 13.1 us -> none  [reduce_grads(): whole = lax.all_gather(part, 'ctx', axis=0, tiled=True)]
    ppermute x28 -> x48, starting transfers between devices: 19 us -> 31.5 us  [swap(): lax.ppermute(values, axis, [(i, i ^ bit) for i in range(lax.axis_size(axi...]
    mul x2, other arithmetic: 22 us -> 9.98 us  [gate_linear(): return values[:, 0] * jax.nn.sigmoid(values[:, 1]) * live_rows]
    ppermute x8, starting transfers between devices: 11.3 us -> 3.96 us  [tensor_total(): other = lax.ppermute(low, 'tp', [(0, 1), (1, 0)])]
    unnamed x287 -> x213, local copies, waits for them, and re-layouts: 27.1 us -> 33.1 us
    ppermute x28 -> x48, waiting for transfers between devices: 71.1 us -> 67.3 us  [swap(): lax.ppermute(values, axis, [(i, i ^ bit) for i in range(lax.axis_size(axi...]
    pallas_call x2 -> x4, Pallas kernels: 50.5 us -> 53.5 us  [attend_backward(): pl.pallas_call(attend_backward_kernel, grid_spec=pltpu.PrefetchScalarGrid...]
  transfers between devices with their start and end apart: 45 -> 65, of which waited for: 23 -> 27; matrix products, arithmetic and copies ran while one was open for 17% -> 24% of each run, Pallas kernels for 17% -> 16%
where the time goes in v4:
time: 630 us; the launch traced here: 620 us
  waiting for transfers between devices  207 us (33%)
  other arithmetic  110 us (17%)
  Pallas kernels  109 us (17%)
  local copies, waits for them, and re-layouts  61.6 us (10%)
  matrix products  51.7 us (8%)
  starting transfers between devices  42.5 us (7%)
  blocking collectives  22 us (3%)
  between operations  17.1 us (3%)
    ppermute x8, waiting for transfers between devices, tensor_total(): other = lax.ppermute(low, 'tp', [(0, 1), (1, 0)])  97.6 us
    ppermute x48, waiting for transfers between devices, swap(): lax.ppermute(values, axis, [(i, i ^ bit) for i in range(lax.axis_size(axi...  67.3 us
    pallas_call x4, Pallas kernels, attend_backward(): pl.pallas_call(attend_backward_kernel, grid_spec=pltpu.PrefetchScalarGrid...  53.5 us
    all_gather x3, waiting for transfers between devices, gather_weights(): whole = lax.all_gather(mine, ('fsdp', 'ctx'), axis=0, tiled=True)  40 us
    pallas_call x4, Pallas kernels, attend_forward(): pl.pallas_call(functools.partial(attend_forward_kernel, last), grid_spec=...  36.9 us
    unnamed x213, local copies, waits for them, and re-layouts  33.1 us
    ppermute x48, starting transfers between devices, swap(): lax.ppermute(values, axis, [(i, i ^ bit) for i in range(lax.axis_size(axi...  31.5 us
    all_gather x1, blocking collectives, gather_weights(): whole = lax.all_gather(mine, ('fsdp', 'ctx'), axis=0, tiled=True)  22 us
  transfers between devices with their start and end apart: 65, of which 27 were waited for; matrix products, arithmetic and copies ran while one was open for 24% of the time, Pallas kernels for 16%

profile of v4, /device:TPU:0, one launch (start us, length us, event | category | flops | bytes accessed | tf_op | source)
XLA Modules:
  0.0 620.2 jit_solution(503295437203299613)
XLA Ops:
  10.8 2.6 reduce_sum.609
  15.0 40.0 %all-gather.4.cloned.1.call-done = bf16[512,2048]{1,0:T(8,128)(2,1)} async-done(((bf16[32,2048]{1,0:T(8,128)(2,1)}), bf16[512,2048]{1,0:T(8,128)(2,1)}) %all-gather.4.cloned.1.call-update) | async-done | bytes 2097168 | tf_op jit(solution)/shard_map/all_gather | solution.py:323
  54.9 5.2 multiply_convert_fusion.1
  60.2 2.3 convolution_convert_fusion.7
  65.1 22.0 %all_gather.13 = bf16[512,768]{1,0:T(8,128)(2,1)S(1)} all-gather(bf16[32,768]{1,0:T(8,128)(2,1)S(1)} %copy.109), channel_id=1, replica_groups=mesh['fsdp'=4,'ctx'=4,'tp'=2] {'fsdp','ctx'}, dimensions={0}, use_global_device_ids=true | all-gather | bytes 835584 | tf_op jit(solution)/shard_map/all_gather | solution.py:323
  89.7 2.1 fusion.246
  102.0 9.3 %attend_forward.4 = (f32[128,1024]{1,0:T(8,128)S(1)}, f32[2,1,1024]{2,1,0:T(1,128)S(1)}, f32[2,1,1024]{2,1,0:T(1,128)S(1)}) custom-call(s32[5]{0:T(128)S(1)} %stack.338.meta_ref, bf16[1024,256]{1,0:T(8,128)(2,1)S(1)} %copy.115.q_ref, bf16[2048,256]{1,0:T(8,128)(2,1)S(1)} %pad_maximum_fusion.3.k_ref.v_ref, bf16[2048,256]{1,0:T(8,128)(2,1)S(1)} %pad_maximum_fusion.3.k_ref.v_ref), custom_call_target="tpu_custom_call" | custom-call | flops 4294967296 | bytes 1835008 | tf_op jit(solution)/shard_map/attend_forward/pallas_call | solution.py:86
  113.8 9.2 %attend_forward.5 = (f32[128,1024]{1,0:T(8,128)S(1)}, f32[2,1,1024]{2,1,0:T(1,128)S(1)}, f32[2,1,1024]{2,1,0:T(1,128)S(1)}) custom-call(s32[5]{0:T(128)S(1)} %stack.338.meta_ref, bf16[1024,256]{1,0:T(8,128)(2,1)S(1)} %copy.115.q_ref, bf16[2048,256]{1,0:T(8,128)(2,1)S(1)} %pad_maximum_fusion.4.k_ref.v_ref, bf16[2048,256]{1,0:T(8,128)(2,1)S(1)} %pad_maximum_fusion.4.k_ref.v_ref), custom_call_target="tpu_custom_call" | custom-call | flops 4294967296 | bytes 1835008 | tf_op jit(solution)/shard_map/attend_forward/pallas_call | solution.py:86
  125.8 9.2 %attend_forward.6 = (f32[128,1024]{1,0:T(8,128)S(1)}, f32[2,1,1024]{2,1,0:T(1,128)S(1)}) custom-call(s32[5]{0:T(128)S(1)} %stack.343.meta_ref, bf16[1024,256]{1,0:T(8,128)(2,1)S(1)} %copy.115.q_ref, bf16[2048,256]{1,0:T(8,128)(2,1)S(1)} %constant_dynamic-update-slice_fusion.k_ref.v_ref, bf16[2048,256]{1,0:T(8,128)(2,1)S(1)} %constant_dynamic-update-slice_fusion.k_ref.v_ref, ...), custom_call_target="tpu_custom_call" | custom-call | flops 4294967296 | bytes 1835008 | tf_op jit(solution)/shard_map/attend_forward/pallas_call | solution.py:86
  135.1 9.2 %attend_forward.7 = (f32[128,1024]{1,0:T(8,128)S(1)}, f32[2,1,1024]{2,1,0:T(1,128)S(1)}) custom-call(s32[5]{0:T(128)S(1)} %stack.343.meta_ref, bf16[1024,256]{1,0:T(8,128)(2,1)S(1)} %copy.115.q_ref, bf16[2048,256]{1,0:T(8,128)(2,1)S(1)} %constant_dynamic-update-slice_fusion.2.k_ref.v_ref, ...), custom_call_target="tpu_custom_call" | custom-call | flops 4294967296 | bytes 1835008 | tf_op jit(solution)/shard_map/attend_forward/pallas_call | solution.py:86
  147.0 2.0 copy.180
  150.6 20.6 %collective-permute-done.7 = bf16[1024,512]{0,1:T(8,128)(2,1)} collective-permute-done((bf16[1024,512]{0,1:T(8,128)(2,1)S(1)}, bf16[1024,512]{0,1:T(8,128)(2,1)}, u32[]{:S(2)}, u32[]{:S(2)}) %collective-permute-start.7) | collective-permute-done | bytes 1048608 | tf_op jit(solution)/shard_map/ppermute | solution.py:238
  171.2 2.4 fusion.245
  182.2 8.8 %multiply_reduce_fusion.14 = (f32[256]{0:T(256)S(1)}, f32[256]{0:T(256)S(1)}, f32[1,1024,256]{2,1,0:T(8,128)}) fusion(f32[1024]{0:T(1024)S(1)} %fusion.207, bf16[1,15,256]{2,1,0:T(8,128)(2,1)S(1)} %collective-permute-done.9, bf16[1,1024,256]{2,1,0:T(8,128)(2,1)S(1)} %fusion.105, f32[256]{0:T(256)S(1)} %bitcast.486, f32[256]{0:T(256)S(1)} %bitcast.488, ...), kind=kLoop, calls=%fused_computation.153 | loop fusion | flops 48758272 | bytes 1626112 | tf_op jit(solution)/shard_map/reduce_sum | solution.py:619
  192.3 10.4 %group_sum_0.1 = f32[8,128]{1,0:T(8,128)} custom-call(f32[8,128]{1,0:T(8,128)} %fusion.204.x_ref), custom_call_target="tpu_custom_call" | custom-call | tf_op jit(solution)/shard_map/group_sum_0/pallas_call | solution.py:289
  203.5 2.1 convolution_convert_fusion.6
  205.9 24.9 %collective-permute-done.10 = bf16[1024,512]{0,1:T(8,128)(2,1)S(1)} collective-permute-done((bf16[1024,512]{0,1:T(8,128)(2,1)S(1)}, bf16[1024,512]{0,1:T(8,128)(2,1)S(1)}, u32[]{:S(2)}, u32[]{:S(2)}) %collective-permute-start.10) | collective-permute-done | bytes 1048608 | tf_op jit(solution)/shard_map/ppermute | solution.py:238
  234.6 5.9 multiply_convert_fusion
  240.5 2.3 convolution_convert_fusion.5
  243.1 2.9 copy.123
  246.0 21.5 %collective-permute-done.11 = bf16[1024,512]{0,1:T(8,128)(2,1)} collective-permute-done((bf16[1024,512]{0,1:T(8,128)(2,1)}, bf16[1024,512]{0,1:T(8,128)(2,1)}, u32[]{:S(2)}, u32[]{:S(2)}) %collective-permute-start.11) | collective-permute-done | bytes 1048608 | tf_op jit(solution)/shard_map/ppermute | solution.py:238
  267.4 2.7 fusion.242
  274.4 2.3 copy-done.99
  276.7 2.4 fusion.2
  279.1 2.9 fusion.257
  282.4 3.3 copy.161
  285.7 3.6 convolution_convert_fusion.3
  289.3 2.9 convolution_convert_fusion.4
  293.8 12.1 %collective-permute-done.12 = bf16[1024,512]{0,1:T(8,128)(2,1)} collective-permute-done((bf16[1024,512]{0,1:T(8,128)(2,1)}, bf16[1024,512]{0,1:T(8,128)(2,1)}, u32[]{:S(2)}, u32[]{:S(2)}) %collective-permute-start.12) | collective-permute-done | bytes 1048608 | tf_op jit(solution)/shard_map/ppermute | solution.py:238
  305.9 2.8 multiply_reduce_fusion.7
  308.7 3.4 multiply_reduce_fusion
  312.1 3.2 add_add_fusion.7
  315.4 2.9 fusion.99
  320.2 8.0 %group_sum_1.1 = f32[8,128]{1,0:T(8,128)} custom-call(f32[8,128]{1,0:T(8,128)} %fusion.203.x_ref), custom_call_target="tpu_custom_call" | custom-call | tf_op jit(solution)/shard_map/group_sum_1/pallas_call | solution.py:289
  329.0 4.8 fusion.90
  340.9 2.2 stack.429
  344.4 3.0 collective-permute-start.14
  348.9 9.7 %fusion.43 = (f32[1024,1,256]{2,0,1:T(8,128)S(1)}, f32[1024,1,256]{2,0,1:T(8,128)S(1)}) fusion(f32[1024,2,256]{2,0,1:T(8,128)} %copy-done.11, f32[1024]{0:T(1024)S(1)} %fusion.207, bf16[1,1024,256]{2,1,0:T(8,128)(2,1)S(1)} %get-tuple-element.226, bf16[1,15,256]{2,1,0:T(8,128)(2,1)S(1)} %collective-permute-done.14, f32[256]{0:T(256)S(1)} %bitcast.487, ...), kind=kLoop, calls=%fused_computation.235 | loop fusion | flops 49807360 | bytes 4769792 | tf_op jit(solution)/shard_map/transpose(jvp())/mul | solution.py:604
  361.5 3.1 collective-permute-start.55
  367.8 18.6 %collective-permute-done.15 = bf16[1024,512]{0,1:T(8,128)(2,1)S(1)} collective-permute-done((bf16[1024,512]{0,1:T(8,128)(2,1)S(1)}, bf16[1024,512]{0,1:T(8,128)(2,1)S(1)}, u32[]{:S(2)}, u32[]{:S(2)}) %collective-permute-start.15) | collective-permute-done | bytes 1048608 | tf_op jit(solution)/shard_map/ppermute | solution.py:238
  393.1 13.4 %attend_backward.4 = (f32[128,1024]{1,0:T(8,128)S(1)}, bf16[2048,256]{1,0:T(8,128)(2,1)S(1)}) custom-call(s32[5]{0:T(128)S(1)} %stack.343.meta_ref, bf16[1024,256]{1,0:T(8,128)(2,1)S(1)} %copy.115.q_ref, bf16[1024,256]{1,0:T(8,128)(2,1)S(1)} %copy.128.g_ref, f32[128,1024]{1,0:T(8,128)S(1)} %get-tuple-element.94.o_ref, ...), custom_call_target="tpu_custom_call" | custom-call | flops 8053063680 | bytes 3670016 | tf_op jit(solution)/shard_map/attend_backward/pallas_call | solution.py:157
  407.5 13.2 %attend_backward.5 = (f32[128,1024]{1,0:T(8,128)S(1)}, bf16[2048,256]{1,0:T(8,128)(2,1)S(1)}) custom-call(s32[5]{0:T(128)S(1)} %stack.343.meta_ref, bf16[1024,256]{1,0:T(8,128)(2,1)S(1)} %copy.115.q_ref, bf16[1024,256]{1,0:T(8,128)(2,1)S(1)} %copy.128.g_ref, f32[128,1024]{1,0:T(8,128)S(1)} %get-tuple-element.103.o_ref, ...), custom_call_target="tpu_custom_call" | custom-call | flops 8053063680 | bytes 3670016 | tf_op jit(solution)/shard_map/attend_backward/pallas_call | solution.py:157
  421.7 13.2 %attend_backward.6 = (f32[128,1024]{1,0:T(8,128)S(1)}, bf16[2048,256]{1,0:T(8,128)(2,1)S(1)}) custom-call(s32[5]{0:T(128)S(1)} %stack.338.meta_ref, bf16[1024,256]{1,0:T(8,128)(2,1)S(1)} %copy.115.q_ref, bf16[1024,256]{1,0:T(8,128)(2,1)S(1)} %copy.128.g_ref, f32[128,1024]{1,0:T(8,128)S(1)} %get-tuple-element.94.o_ref, ...), custom_call_target="tpu_custom_call" | custom-call | flops 8053063680 | bytes 3670016 | tf_op jit(solution)/shard_map/attend_backward/pallas_call | solution.py:157
  437.4 13.6 %attend_backward.7 = (f32[128,1024]{1,0:T(8,128)S(1)}, bf16[2048,256]{1,0:T(8,128)(2,1)S(1)}) custom-call(s32[5]{0:T(128)S(1)} %stack.338.meta_ref, bf16[1024,256]{1,0:T(8,128)(2,1)S(1)} %copy.115.q_ref, bf16[1024,256]{1,0:T(8,128)(2,1)S(1)} %copy.128.g_ref, f32[128,1024]{1,0:T(8,128)S(1)} %get-tuple-element.103.o_ref, ...), custom_call_target="tpu_custom_call" | custom-call | flops 8053063680 | bytes 3670016 | tf_op jit(solution)/shard_map/attend_backward/pallas_call | solution.py:157
  453.1 12.4 %collective-permute-done.21 = bf16[1024,256]{1,0:T(8,128)(2,1)S(1)} collective-permute-done((bf16[1024,256]{1,0:T(8,128)(2,1)S(1)}, bf16[1024,256]{1,0:T(8,128)(2,1)S(1)}, u32[]{:S(2)}, u32[]{:S(2)}) %collective-permute-start.21) | collective-permute-done | bytes 524320 | tf_op jit(solution)/shard_map/ppermute | solution.py:361
  471.9 2.4 bitcast_convert_fusion
  477.1 3.5 reshape_reshape.3
  502.7 5.9 collective-permute-done.52
  512.9 6.3 %collective-permute-done.48 = bf16[2,32,768]{2,1,0:T(8,128)(2,1)S(1)} collective-permute-done((bf16[2,32,768]{2,1,0:T(8,128)(2,1)S(1)}, bf16[2,32,768]{2,1,0:T(8,128)(2,1)S(1)}, u32[]{:S(2)}, u32[]{:S(2)}) %collective-permute-start.48) | collective-permute-done | bytes 98336 | tf_op jit(solution)/shard_map/ppermute | solution.py:361
  520.7 5.2 collective-permute-done.49
  532.0 2.4 multiply_reduce_fusion.2
  534.6 2.6 add_add_fusion.5
  537.7 2.5 fusion.5
  548.6 2.9 convolution_convert_fusion.2
  552.9 2.3 collective-permute-done.26
  556.1 3.7 collective-permute-done.27
  573.1 5.8 collective-permute-done.41
  579.1 4.6 collective-permute-done.35
  586.0 4.1 collective-permute-done.36
  591.1 4.2 collective-permute-done.37
  597.0 2.7 collective-permute-done.38
  602.2 2.1 fusion.234
  604.3 3.5 add_bitcast_fusion
  607.8 2.9 copy.162
  (529 shorter events, 159.2 us)
Async XLA Ops:
  7.2 47.8 %all-gather.4.cloned.1.call-start = ((), (), s32[]{:S(2)}) async-start(), calls=%async_computation.2 | async-start | bytes 2228224 | tf_op jit(solution)/shard_map/all_gather | solution.py:323
  8.8 135.7 %all-gather.6.cloned.1.call-start = ((), (), s32[]{:S(2)}) async-start(), calls=%async_computation.3 | async-start | bytes 1114112 | tf_op jit(solution)/shard_map/all_gather | solution.py:323
  62.5 27.2 %collective-permute-start = (bf16[1024,512]{0,1:T(8,128)(2,1)}, bf16[1024,512]{0,1:T(8,128)(2,1)}, u32[]{:S(2)}, u32[]{:S(2)}) collective-permute-start(bf16[1024,512]{0,1:T(8,128)(2,1)} %convolution_convert_fusion.7), channel_id=1, source_target_pairs={{0,1},{1,0},{2,3},{3,2},{4,5},{5,4},{6,7},{7,6},{8,9},{9,8},{10,11... | collective-permute-start | bytes 3145736 | tf_op jit(solution)/shard_map/ppermute | solution.py:238
  64.6 170.0 %all-gather.8.cloned.1.call-start = ((), (), s32[]{:S(2)}) async-start(), calls=%async_computation.4 | async-start | bytes 2228224 | tf_op jit(solution)/shard_map/all_gather | solution.py:323
  97.0 3.8 collective-permute-start.2
  97.5 15.2 %collective-permute-start.1 = (bf16[1024,256]{1,0:T(8,128)(2,1)}, bf16[1024,256]{1,0:T(8,128)(2,1)}, u32[]{:S(2)}, u32[]{:S(2)}) collective-permute-start(bf16[1024,256]{1,0:T(8,128)(2,1)} %pad_maximum_fusion.12), channel_id=1, source_target_pairs={{0,4},{2,6},{4,0},{6,2},{1,5},{3,7},{5,1},{7,3},{8,12},{10,14},{12... | collective-permute-start | bytes 1572872 | tf_op jit(solution)/shard_map/ppermute | solution.py:361
  98.5 14.2 %collective-permute-start.4 = (bf16[1024,256]{1,0:T(8,128)(2,1)}, bf16[1024,256]{1,0:T(8,128)(2,1)}, u32[]{:S(2)}, u32[]{:S(2)}) collective-permute-start(bf16[1024,256]{1,0:T(8,128)(2,1)} %pad_maximum_fusion.13), channel_id=1, source_target_pairs={{0,2},{2,0},{4,6},{6,4},{1,3},{3,1},{5,7},{7,5},{8,10},{10,8},{12,... | collective-permute-start | bytes 1572872 | tf_op jit(solution)/shard_map/ppermute | solution.py:361
  98.6 24.4 %collective-permute-start.3 = (bf16[1024,256]{1,0:T(8,128)(2,1)}, bf16[1024,256]{1,0:T(8,128)(2,1)}, u32[]{:S(2)}, u32[]{:S(2)}) collective-permute-start(bf16[1024,256]{1,0:T(8,128)(2,1)} %pad_maximum_fusion.13), channel_id=1, source_target_pairs={{0,4},{2,6},{4,0},{6,2},{1,5},{3,7},{5,1},{7,3},{8,12},{10,14},{12... | collective-permute-start | bytes 1572872 | tf_op jit(solution)/shard_map/ppermute | solution.py:361
  112.7 13.1 %collective-permute-start.5 = (bf16[1024,256]{1,0:T(8,128)(2,1)}, bf16[1024,256]{1,0:T(8,128)(2,1)S(1)}, u32[]{:S(2)}, u32[]{:S(2)}) collective-permute-start(bf16[1024,256]{1,0:T(8,128)(2,1)} %collective-permute-done.1), channel_id=1, source_target_pairs={{0,2},{2,0},{4,6},{6,4},{1,3},{3,1},{5,7},{7,5},{8,10},{10,8},{12,... | collective-permute-start | bytes 1572872 | tf_op jit(solution)/shard_map/ppermute | solution.py:361
  123.1 12.0 %collective-permute-start.6 = (bf16[1024,256]{1,0:T(8,128)(2,1)}, bf16[1024,256]{1,0:T(8,128)(2,1)S(1)}, u32[]{:S(2)}, u32[]{:S(2)}) collective-permute-start(bf16[1024,256]{1,0:T(8,128)(2,1)} %collective-permute-done.3), channel_id=1, source_target_pairs={{0,2},{2,0},{4,6},{6,4},{1,3},{3,1},{5,7},{7,5},{8,10},{10,8},{12,... | collective-permute-start | bytes 1572872 | tf_op jit(solution)/shard_map/ppermute | solution.py:361
  146.0 25.2 %collective-permute-start.7 = (bf16[1024,512]{0,1:T(8,128)(2,1)S(1)}, bf16[1024,512]{0,1:T(8,128)(2,1)}, u32[]{:S(2)}, u32[]{:S(2)}) collective-permute-start(bf16[1024,512]{0,1:T(8,128)(2,1)S(1)} %convolution_convert_fusion), channel_id=1, source_target_pairs={{0,1},{1,0},{2,3},{3,2},{4,5},{5,4},{6,7},{7,6},{8,9},{9,8},{10,11... | collective-permute-start | bytes 3145736 | tf_op jit(solution)/shard_map/ppermute | solution.py:238
  150.6 347.3 %reduce-scatter.7.cloned.1.call-start = ((), (), s32[]{:S(2)}) async-start(), calls=%async_computation.6 | async-start | bytes 1114112
  177.3 3.2 collective-permute-start.8
  178.6 3.5 collective-permute-start.9
  205.5 25.2 %collective-permute-start.10 = (bf16[1024,512]{0,1:T(8,128)(2,1)S(1)}, bf16[1024,512]{0,1:T(8,128)(2,1)S(1)}, u32[]{:S(2)}, u32[]{:S(2)}) collective-permute-start(bf16[1024,512]{0,1:T(8,128)(2,1)S(1)} %convolution_convert_fusion.6), channel_id=1, source_target_pairs={{0,1},{1,0},{2,3},{3,2},{4,5},{5,4},{6,7},{7,6},{8,9},{9,8},{10,11... | collective-permute-start | bytes 3145736 | tf_op jit(solution)/shard_map/ppermute | solution.py:238
  242.8 24.6 %collective-permute-start.11 = (bf16[1024,512]{0,1:T(8,128)(2,1)}, bf16[1024,512]{0,1:T(8,128)(2,1)}, u32[]{:S(2)}, u32[]{:S(2)}) collective-permute-start(bf16[1024,512]{0,1:T(8,128)(2,1)} %convolution_convert_fusion.5), channel_id=1, source_target_pairs={{0,1},{1,0},{2,3},{3,2},{4,5},{5,4},{6,7},{7,6},{8,9},{9,8},{10,11... | collective-permute-start | bytes 3145736 | tf_op jit(solution)/shard_map/ppermute | solution.py:238
  282.1 23.8 %collective-permute-start.12 = (bf16[1024,512]{0,1:T(8,128)(2,1)}, bf16[1024,512]{0,1:T(8,128)(2,1)}, u32[]{:S(2)}, u32[]{:S(2)}) collective-permute-start(bf16[1024,512]{0,1:T(8,128)(2,1)} %get-tuple-element.323), channel_id=1, source_target_pairs={{0,1},{1,0},{2,3},{3,2},{4,5},{5,4},{6,7},{7,6},{8,9},{9,8},{10,11... | collective-permute-start | bytes 3145736 | tf_op jit(solution)/shard_map/ppermute | solution.py:238
  343.1 5.8 collective-permute-start.13
  344.4 4.5 collective-permute-start.14
  347.5 14.0 %collective-permute-start.54 = (f32[64,128]{1,0:T(8,128)S(1)}, f32[64,128]{1,0:T(8,128)S(1)}, u32[]{:S(2)}, u32[]{:S(2)}) collective-permute-start(f32[64,128]{1,0:T(8,128)S(1)} %pad_bitcast_fusion), channel_id=1, source_target_pairs={{0,2},{2,0},{4,6},{6,4},{1,3},{3,1},{5,7},{7,5},{8,10},{10,8},{12,... | collective-permute-start | bytes 98312 | tf_op jit(solution)/shard_map/ppermute | solution.py:361
  360.4 26.0 %collective-permute-start.15 = (bf16[1024,512]{0,1:T(8,128)(2,1)S(1)}, bf16[1024,512]{0,1:T(8,128)(2,1)S(1)}, u32[]{:S(2)}, u32[]{:S(2)}) collective-permute-start(bf16[1024,512]{0,1:T(8,128)(2,1)S(1)} %bitcast_convert_fusion.1), channel_id=1, source_target_pairs={{0,1},{1,0},{2,3},{3,2},{4,5},{5,4},{6,7},{7,6},{8,9},{9,8},{10,11... | collective-permute-start | bytes 3145736 | tf_op jit(solution)/shard_map/ppermute | solution.py:238
  361.5 5.0 collective-permute-start.55
  367.1 115.9 %collective-permute-start.56 = (f32[64,128]{1,0:T(8,128)}, f32[64,128]{1,0:T(8,128)}, u32[]{:S(2)}, u32[]{:S(2)}) collective-permute-start(f32[64,128]{1,0:T(8,128)} %fusion.275), channel_id=1, source_target_pairs={{0,8},{8,0},{16,24},{24,16},{1,9},{9,1},{17,25},{25,17},{2,10},{10... | collective-permute-start | bytes 98312 | tf_op jit(solution)/shard_map/ppermute | solution.py:361
  392.8 153.0 %reduce-scatter.5.cloned.1.call-start = ((), (), s32[]{:S(2)}) async-start(), calls=%async_computation.5 | async-start | bytes 2228224 | tf_op jit(solution)/shard_map/reduce_scatter | solution.py:341
  393.1 14.1 %collective-permute-start.29 = (f32[16,128]{1,0:T(8,128)S(1)}, f32[16,128]{1,0:T(8,128)S(1)}, u32[]{:S(2)}, u32[]{:S(2)}) collective-permute-start(f32[16,128]{1,0:T(8,128)S(1)} %fusion.202), channel_id=1, source_target_pairs={{0,2},{2,0},{4,6},{6,4},{1,3},{3,1},{5,7},{7,5},{8,10},{10,8},{12,... | collective-permute-start | bytes 24584 | tf_op jit(solution)/shard_map/ppermute | solution.py:361
  406.6 14.9 %collective-permute-start.16 = (bf16[1024,256]{1,0:T(8,128)(2,1)S(1)}, bf16[1024,256]{1,0:T(8,128)(2,1)S(1)}, u32[]{:S(2)}, u32[]{:S(2)}) collective-permute-start(bf16[1024,256]{1,0:T(8,128)(2,1)S(1)} %slice.734), channel_id=1, source_target_pairs={{0,2},{2,0},{4,6},{6,4},{1,3},{3,1},{5,7},{7,5},{8,10},{10,8},{12,... | collective-permute-start | bytes 1572872 | tf_op jit(solution)/shard_map/ppermute | solution.py:361
  407.2 13.7 %collective-permute-start.30 = (f32[16,128]{1,0:T(8,128)S(1)}, f32[16,128]{1,0:T(8,128)S(1)}, u32[]{:S(2)}, u32[]{:S(2)}) collective-permute-start(f32[16,128]{1,0:T(8,128)S(1)} %fusion.227), channel_id=1, source_target_pairs={{0,4},{2,6},{4,0},{6,2},{1,5},{3,7},{5,1},{7,3},{8,12},{10,14},{12... | collective-permute-start | bytes 24584 | tf_op jit(solution)/shard_map/ppermute | solution.py:361
  420.8 16.4 %collective-permute-start.17 = (bf16[1024,256]{1,0:T(8,128)(2,1)S(1)}, bf16[1024,256]{1,0:T(8,128)(2,1)S(1)}, u32[]{:S(2)}, u32[]{:S(2)}) collective-permute-start(bf16[1024,256]{1,0:T(8,128)(2,1)S(1)} %slice.736), channel_id=1, source_target_pairs={{0,2},{2,0},{4,6},{6,4},{1,3},{3,1},{5,7},{7,5},{8,10},{10,8},{12,... | collective-permute-start | bytes 1572872 | tf_op jit(solution)/shard_map/ppermute | solution.py:361
  434.9 16.8 %collective-permute-start.18 = (bf16[1024,256]{1,0:T(8,128)(2,1)S(1)}, bf16[1024,256]{1,0:T(8,128)(2,1)S(1)}, u32[]{:S(2)}, u32[]{:S(2)}) collective-permute-start(bf16[1024,256]{1,0:T(8,128)(2,1)S(1)} %slice.738), channel_id=1, source_target_pairs={{0,2},{2,0},{4,6},{6,4},{1,3},{3,1},{5,7},{7,5},{8,10},{10,8},{12,... | collective-permute-start | bytes 1572872 | tf_op jit(solution)/shard_map/ppermute | solution.py:361
  435.5 17.1 %collective-permute-start.19 = (bf16[1024,256]{1,0:T(8,128)(2,1)S(1)}, bf16[1024,256]{1,0:T(8,128)(2,1)S(1)}, u32[]{:S(2)}, u32[]{:S(2)}) collective-permute-start(bf16[1024,256]{1,0:T(8,128)(2,1)S(1)} %add_convert_fusion.4), channel_id=1, source_target_pairs={{0,4},{2,6},{4,0},{6,2},{1,5},{3,7},{5,1},{7,3},{8,12},{10,14},{12... | collective-permute-start | bytes 1572872 | tf_op jit(solution)/shard_map/ppermute | solution.py:361
  451.2 14.3 %collective-permute-start.21 = (bf16[1024,256]{1,0:T(8,128)(2,1)S(1)}, bf16[1024,256]{1,0:T(8,128)(2,1)S(1)}, u32[]{:S(2)}, u32[]{:S(2)}) collective-permute-start(bf16[1024,256]{1,0:T(8,128)(2,1)S(1)} %add_convert_fusion.3), channel_id=1, source_target_pairs={{0,4},{2,6},{4,0},{6,2},{1,5},{3,7},{5,1},{7,3},{8,12},{10,14},{12... | collective-permute-start | bytes 1572872 | tf_op jit(solution)/shard_map/ppermute | solution.py:361
  451.8 32.9 %collective-permute-start.31 = (f32[16,128]{1,0:T(8,128)}, f32[16,128]{1,0:T(8,128)}, u32[]{:S(2)}, u32[]{:S(2)}) collective-permute-start(f32[16,128]{1,0:T(8,128)} %fusion.276), channel_id=1, source_target_pairs={{0,8},{8,0},{16,24},{24,16},{1,9},{9,1},{17,25},{25,17},{2,10},{10... | collective-permute-start | bytes 24584 | tf_op jit(solution)/shard_map/ppermute | solution.py:361
  482.4 12.6 %collective-permute-start.46 = (bf16[2,2,2,32,768]{4,3,2,1,0:T(8,128)(2,1)}, bf16[2,2,2,32,768]{4,3,2,1,0:T(8,128)(2,1)S(1)}, u32[]{:S(2)}, u32[]{:S(2)}) collective-permute-start(bf16[2,2,2,32,768]{4,3,2,1,0:T(8,128)(2,1)} %dynamic-slice_bitcast_fusion.2), channel_id=1, source_target_pairs={{0,2},{2,0},{4,6},{6,4},{1,3},{3,1},{5,7},{7,5},{8,10},{10,8},{12,... | collective-permute-start | bytes 1179656 | tf_op jit(solution)/shard_map/ppermute | solution.py:361
  483.8 6.6 %collective-permute-start.57 = (f32[64,128]{1,0:T(8,128)S(1)}, f32[64,128]{1,0:T(8,128)S(1)}, u32[]{:S(2)}, u32[]{:S(2)}) collective-permute-start(f32[64,128]{1,0:T(8,128)S(1)} %add.750), channel_id=1, source_target_pairs={{0,16},{8,24},{16,0},{24,8},{1,17},{9,25},{17,1},{25,9},{2,18},{10... | collective-permute-start | bytes 98312 | tf_op jit(solution)/shard_map/ppermute | solution.py:361
  485.4 4.5 collective-permute-start.32
  490.0 3.8 collective-permute-start.33
  497.6 13.3 %collective-permute-start.47 = (bf16[2,2,32,768]{3,2,1,0:T(8,128)(2,1)}, bf16[2,2,32,768]{3,2,1,0:T(8,128)(2,1)}, u32[]{:S(2)}, u32[]{:S(2)}) collective-permute-start(bf16[2,2,32,768]{3,2,1,0:T(8,128)(2,1)} %dynamic-slice_bitcast_fusion.5), channel_id=1, source_target_pairs={{0,4},{2,6},{4,0},{6,2},{1,5},{3,7},{5,1},{7,3},{8,12},{10,14},{12... | collective-permute-start | bytes 589832 | tf_op jit(solution)/shard_map/ppermute | solution.py:361
  498.9 9.7 %collective-permute-start.52 = (bf16[32,1024]{0,1:T(8,128)(2,1)S(1)}, bf16[32,1024]{0,1:T(8,128)(2,1)}, u32[]{:S(2)}, u32[]{:S(2)}) collective-permute-start(bf16[32,1024]{0,1:T(8,128)(2,1)S(1)} %copy.178), channel_id=1, source_target_pairs={{0,4},{2,6},{4,0},{6,2},{1,5},{3,7},{5,1},{7,3},{8,12},{10,14},{12... | collective-permute-start | bytes 196616 | tf_op jit(solution)/shard_map/ppermute | solution.py:361
  502.0 28.2 %collective-permute-start.22 = (bf16[1024,512]{0,1:T(8,128)(2,1)S(1)}, bf16[1024,512]{0,1:T(8,128)(2,1)}, u32[]{:S(2)}, u32[]{:S(2)}) collective-permute-start(bf16[1024,512]{0,1:T(8,128)(2,1)S(1)} %bitcast_convert_fusion), channel_id=1, source_target_pairs={{0,1},{1,0},{2,3},{3,2},{4,5},{5,4},{6,7},{7,6},{8,9},{9,8},{10,11... | collective-permute-start | bytes 3145736 | tf_op jit(solution)/shard_map/ppermute | solution.py:238
  510.7 9.9 %collective-permute-start.53 = (bf16[2,32,1024]{2,1,0:T(8,128)(2,1)S(1)}, bf16[2,32,1024]{2,1,0:T(8,128)(2,1)S(1)}, u32[]{:S(2)}, u32[]{:S(2)}) collective-permute-start(bf16[2,32,1024]{2,1,0:T(8,128)(2,1)S(1)} %maximum_select_fusion.12), channel_id=1, source_target_pairs={{0,2},{2,0},{4,6},{6,4},{1,3},{3,1},{5,7},{7,5},{8,10},{10,8},{12,... | collective-permute-start | bytes 393224 | tf_op jit(solution)/shard_map/ppermute | solution.py:361
  511.9 7.2 %collective-permute-start.48 = (bf16[2,32,768]{2,1,0:T(8,128)(2,1)S(1)}, bf16[2,32,768]{2,1,0:T(8,128)(2,1)S(1)}, u32[]{:S(2)}, u32[]{:S(2)}) collective-permute-start(bf16[2,32,768]{2,1,0:T(8,128)(2,1)S(1)} %dynamic-slice_bitcast_fusion.8), channel_id=1, source_target_pairs={{0,8},{8,0},{16,24},{24,16},{1,9},{9,1},{17,25},{25,17},{2,10},{10... | collective-permute-start | bytes 294920 | tf_op jit(solution)/shard_map/ppermute | solution.py:361
  519.2 6.7 %collective-permute-start.49 = (bf16[32,768]{1,0:T(8,128)(2,1)S(1)}, bf16[32,768]{1,0:T(8,128)(2,1)S(1)}, u32[]{:S(2)}, u32[]{:S(2)}) collective-permute-start(bf16[32,768]{1,0:T(8,128)(2,1)S(1)} %dynamic-slice_bitcast_fusion.11), channel_id=1, source_target_pairs={{0,16},{8,24},{16,0},{24,8},{1,17},{9,25},{17,1},{25,9},{2,18},{10... | collective-permute-start | bytes 147464 | tf_op jit(solution)/shard_map/ppermute | solution.py:361
  525.9 4.2 collective-permute-start.50
  530.1 12.8 %collective-permute-start.51 = (bf16[2,32,768]{2,1,0:T(8,128)(2,1)S(1)}, bf16[2,32,768]{2,1,0:T(8,128)(2,1)S(1)}, u32[]{:S(2)}, u32[]{:S(2)}) collective-permute-start(bf16[2,32,768]{2,1,0:T(8,128)(2,1)S(1)} %maximum_select_fusion.14), channel_id=1, source_target_pairs={{0,2},{2,0},{4,6},{6,4},{1,3},{3,1},{5,7},{7,5},{8,10},{10,8},{12,... | collective-permute-start | bytes 294920 | tf_op jit(solution)/shard_map/ppermute | solution.py:361
  542.4 4.0 collective-permute-start.24
  545.8 17.5 %collective-permute-start.58 = (bf16[32,2048]{1,0:T(8,128)(2,1)}, bf16[32,2048]{1,0:T(8,128)(2,1)S(1)}, u32[]{:S(2)}, u32[]{:S(2)}) collective-permute-start(bf16[32,2048]{1,0:T(8,128)(2,1)} %reduce-scatter.5.cloned.1.call-done), channel_id=1, source_target_pairs={{0,4},{2,6},{4,0},{6,2},{1,5},{3,7},{5,1},{7,3},{8,12},{10,14},{12... | collective-permute-start | bytes 393224 | tf_op jit(solution)/shard_map/ppermute | solution.py:361
  547.0 4.5 collective-permute-start.25
  551.5 3.7 collective-permute-start.26
  555.2 4.5 collective-permute-start.27
  556.0 12.3 %collective-permute-start.40 = (bf16[2,2,2,32,1024]{4,3,2,1,0:T(8,128)(2,1)}, bf16[2,2,2,32,1024]{4,3,2,1,0:T(8,128)(2,1)}, u32[]{:S(2)}, u32[]{:S(2)}) collective-permute-start(bf16[2,2,2,32,1024]{4,3,2,1,0:T(8,128)(2,1)} %dynamic-slice_bitcast_fusion), channel_id=1, source_target_pairs={{0,2},{2,0},{4,6},{6,4},{1,3},{3,1},{5,7},{7,5},{8,10},{10,8},{12,... | collective-permute-start | bytes 1572872 | tf_op jit(solution)/shard_map/ppermute | solution.py:361
  559.7 3.6 collective-permute-start.28
  561.9 8.7 %collective-permute-start.34 = (bf16[2,2,2,32,1024]{4,3,2,1,0:T(8,128)(2,1)}, bf16[2,2,2,32,1024]{4,3,2,1,0:T(8,128)(2,1)}, u32[]{:S(2)}, u32[]{:S(2)}) collective-permute-start(bf16[2,2,2,32,1024]{4,3,2,1,0:T(8,128)(2,1)} %dynamic-slice_bitcast_fusion.1), channel_id=1, source_target_pairs={{0,2},{2,0},{4,6},{6,4},{1,3},{3,1},{5,7},{7,5},{8,10},{10,8},{12,... | collective-permute-start | bytes 1572872 | tf_op jit(solution)/shard_map/ppermute | solution.py:361
  561.9 38.5 %collective-permute-start.23 = (bf16[1024,512]{0,1:T(8,128)(2,1)S(1)}, bf16[1024,512]{0,1:T(8,128)(2,1)}, u32[]{:S(2)}, u32[]{:S(2)}) collective-permute-start(bf16[1024,512]{0,1:T(8,128)(2,1)S(1)} %get-tuple-element.138), channel_id=1, source_target_pairs={{0,1},{1,0},{2,3},{3,2},{4,5},{5,4},{6,7},{7,6},{8,9},{9,8},{10,11... | collective-permute-start | bytes 3145736 | tf_op jit(solution)/shard_map/ppermute | solution.py:238
  564.1 2.1 collective-permute-start.59
  569.7 9.2 %collective-permute-start.41 = (bf16[2,2,32,1024]{3,2,1,0:T(8,128)(2,1)S(1)}, bf16[2,2,32,1024]{3,2,1,0:T(8,128)(2,1)S(1)}, u32[]{:S(2)}, u32[]{:S(2)}) collective-permute-start(bf16[2,2,32,1024]{3,2,1,0:T(8,128)(2,1)S(1)} %dynamic-slice_bitcast_fusion.3), channel_id=1, source_target_pairs={{0,4},{2,6},{4,0},{6,2},{1,5},{3,7},{5,1},{7,3},{8,12},{10,14},{12... | collective-permute-start | bytes 786440 | tf_op jit(solution)/shard_map/ppermute | solution.py:361
  571.9 11.8 %collective-permute-start.35 = (bf16[2,2,32,1024]{3,2,1,0:T(8,128)(2,1)S(1)}, bf16[2,2,32,1024]{3,2,1,0:T(8,128)(2,1)S(1)}, u32[]{:S(2)}, u32[]{:S(2)}) collective-permute-start(bf16[2,2,32,1024]{3,2,1,0:T(8,128)(2,1)S(1)} %dynamic-slice_bitcast_fusion.4), channel_id=1, source_target_pairs={{0,4},{2,6},{4,0},{6,2},{1,5},{3,7},{5,1},{7,3},{8,12},{10,14},{12... | collective-permute-start | bytes 786440 | tf_op jit(solution)/shard_map/ppermute | solution.py:361
  579.0 5.0 collective-permute-start.42
  583.8 6.3 %collective-permute-start.36 = (bf16[2,32,1024]{2,1,0:T(8,128)(2,1)S(1)}, bf16[2,32,1024]{2,1,0:T(8,128)(2,1)S(1)}, u32[]{:S(2)}, u32[]{:S(2)}) collective-permute-start(bf16[2,32,1024]{2,1,0:T(8,128)(2,1)S(1)} %dynamic-slice_bitcast_fusion.7), channel_id=1, source_target_pairs={{0,8},{8,0},{16,24},{24,16},{1,9},{9,1},{17,25},{25,17},{2,10},{10... | collective-permute-start | bytes 393224 | tf_op jit(solution)/shard_map/ppermute | solution.py:361
  584.1 6.1 collective-permute-start.43
  590.1 5.2 collective-permute-start.37
  590.2 6.1 collective-permute-start.44
  595.4 4.3 collective-permute-start.38
  597.0 13.7 %collective-permute-start.45 = (bf16[2,32,1024]{2,1,0:T(8,128)(2,1)}, bf16[2,32,1024]{2,1,0:T(8,128)(2,1)}, u32[]{:S(2)}, u32[]{:S(2)}) collective-permute-start(bf16[2,32,1024]{2,1,0:T(8,128)(2,1)} %maximum_select_fusion.10), channel_id=1, source_target_pairs={{0,2},{2,0},{4,6},{6,4},{1,3},{3,1},{5,7},{7,5},{8,10},{10,8},{12,... | collective-permute-start | bytes 393224 | tf_op jit(solution)/shard_map/ppermute | solution.py:361
  600.4 12.2 %collective-permute-start.39 = (bf16[2,32,1024]{2,1,0:T(8,128)(2,1)}, bf16[2,32,1024]{2,1,0:T(8,128)(2,1)S(1)}, u32[]{:S(2)}, u32[]{:S(2)}) collective-permute-start(bf16[2,32,1024]{2,1,0:T(8,128)(2,1)} %maximum_select_fusion.8), channel_id=1, source_target_pairs={{0,2},{2,0},{4,6},{6,4},{1,3},{3,1},{5,7},{7,5},{8,10},{10,8},{12,... | collective-permute-start | bytes 393224 | tf_op jit(solution)/shard_map/ppermute | solution.py:361
  (101 other events, 1104.4 us)
Sparse Core Ops, SparseCore 0:
  10.7 44.1 all-gather.3
  64.7 36.2 all-gather.5
  150.7 39.2 all-gather.7
  392.9 55.1 reduce-scatter.6
  483.1 60.4 reduce-scatter.4

commit v5 on v4

--- a/solution.py
+++ b/solution.py
@@ -210,6 +210,13 @@
     return cells
 
 
+def halo_parts(cells, width):
+    count = lax.axis_size("ctx")
+    left = lax.ppermute(cells[-width:], "ctx", [(i, i + 1) for i in range(count - 1)])
+    right = lax.ppermute(cells[:width], "ctx", [(i + 1, i) for i in range(count - 1)])
+    return (left, cells, right)
+
+
 def layer_norm(values, gain):
     center = values - jnp.mean(values, -1, keepdims=True)
     spread = jnp.mean(center * center, -1, keepdims=True)
@@ -237,6 +244,115 @@
         return lax.psum(low, "tp").astype(jnp.float32)
     other = lax.ppermute(low, "tp", [(0, 1), (1, 0)])
     return low.astype(jnp.float32) + other.astype(jnp.float32)
+
+
+def fill_wide(wide, left_ref, body_ref, right_ref):
+    frames, reach = body_ref.shape[0], left_ref.shape[0]
+    wide[1 : 1 + reach] = left_ref[...].astype(jnp.float32)
+    wide[1 + reach : 1 + reach + frames] = body_ref[...].astype(jnp.float32)
+    wide[1 + reach + frames : 1 + 2 * reach + frames] = right_ref[...].astype(jnp.float32)
+
+
+def conv_forward_kernel(
+    live_ref, left_ref, body_ref, right_ref, weight_ref, o_ref, sums_ref, wide
+):
+    frames, channels = o_ref.shape
+    block = 64
+    fill_wide(wide, left_ref, body_ref, right_ref)
+    sums_ref[...] = jnp.zeros_like(sums_ref)
+
+    @pl.loop(0, frames // block)
+    def _(step):
+        row = pl.multiple_of(step * block, block)
+        spot = row + lax.broadcasted_iota(jnp.int32, (block, 1), 0)
+        live = (spot < live_ref[0]).astype(jnp.float32)
+        for lane in range(0, channels, PAIR):
+            lanes = slice(lane, lane + PAIR)
+            total = jnp.zeros((block, PAIR), jnp.float32)
+            near = wide[pl.ds(row, block + 32), lanes]
+            for tap in range(KERNEL):
+                total = total + weight_ref[tap : tap + 1, lanes] * near[tap + 1 : tap + 1 + block]
+            o_ref[pl.ds(row, block), lanes] = total
+            kept = live * total
+            sums_ref[0:8, lanes] += jnp.sum(kept.reshape(block // 8, 8, PAIR), 0)
+            sums_ref[8:16, lanes] += jnp.sum((kept * total).reshape(block // 8, 8, PAIR), 0)
+
+
+def conv_forward(parts, weight, live_frames):
+    frames, channels = parts[1].shape
+    out, sums = pl.pallas_call(
+        conv_forward_kernel,
+        out_shape=[
+            jax.ShapeDtypeStruct((frames, channels), jnp.float32),
+            jax.ShapeDtypeStruct((16, channels), jnp.float32),
+        ],
+        in_specs=[
+            pl.BlockSpec(memory_space=pltpu.SMEM),
+        ]
+        + [pl.BlockSpec(memory_space=pltpu.VMEM)] * 4,
+        out_specs=[pl.BlockSpec(memory_space=pltpu.VMEM)] * 2,
+        scratch_shapes=[pltpu.VMEM((frames + 32, channels), jnp.float32)],
+        cost_estimate=pl.CostEstimate(
+            flops=2 * KERNEL * frames * channels,
+            bytes_accessed=6 * frames * channels,
+            transcendentals=0,
+        ),
+        name="conv_forward",
+    )(live_frames, *parts, weight)
+    sums = jnp.sum(sums.reshape(2, 8, channels), 1)
+    return (out, sums[0], sums[1])
+
+
+def conv_backward_kernel(
+    left_ref, body_ref, right_ref, left_grad, body_grad, right_grad, weight_ref,
+    o_ref, taps_ref, wide, grads,
+):
+    frames, channels = o_ref.shape
+    block = 64
+    reach = KERNEL // 2
+    fill_wide(wide, left_ref, body_ref, right_ref)
+    fill_wide(grads, left_grad, body_grad, right_grad)
+    taps_ref[...] = jnp.zeros_like(taps_ref)
+
+    @pl.loop(0, frames // block)
+    def _(step):
+        row = pl.multiple_of(step * block, block)
+        for lane in range(0, channels, PAIR):
+            lanes = slice(lane, lane + PAIR)
+            total = jnp.zeros((block, PAIR), jnp.float32)
+            near = grads[pl.ds(row, block + 32), lanes]
+            for tap in range(KERNEL):
+                start = 2 * reach - tap
+                total = total + weight_ref[tap : tap + 1, lanes] * near[start + 1 : start + 1 + block]
+            o_ref[pl.ds(row, block), lanes] = total
+            own = near[reach + 1 : reach + 1 + block]
+            value = wide[pl.ds(row, block + 32), lanes]
+            for tap in range(KERNEL):
+                product = own * value[tap + 1 : tap + 1 + block]
+                taps_ref[8 * tap : 8 * tap + 8, lanes] += jnp.sum(
+                    product.reshape(block // 8, 8, PAIR), 0
+                )
+
+
+def conv_backward(parts, grad_parts, weight):
+    frames, channels = parts[1].shape
+    out, taps = pl.pallas_call(
+        conv_backward_kernel,
+        out_shape=[
+            jax.ShapeDtypeStruct((frames, channels), jnp.float32),
+            jax.ShapeDtypeStruct((8 * KERNEL, channels), jnp.float32),
+        ],
+        in_specs=[pl.BlockSpec(memory_space=pltpu.VMEM)] * 7,
+        out_specs=[pl.BlockSpec(memory_space=pltpu.VMEM)] * 2,
+        scratch_shapes=[pltpu.VMEM((frames + 32, channels), jnp.float32)] * 2,
+        cost_estimate=pl.CostEstimate(
+            flops=4 * KERNEL * frames * channels,
+            bytes_accessed=8 * frames * channels,
+            transcendentals=0,
+        ),
+        name="conv_backward",
+    )(*parts, *grad_parts, weight)
+    return (out, jnp.sum(taps.reshape(KERNEL, 8, channels), 1))
 
 
 def group_sum_kernel(axes, sizes, x_ref, o_ref, slots, send_sem, recv_sem):
@@ -331,6 +447,23 @@
     return pieces
 
 
+def gather_both(up, down):
+    part = up.shape[0] // lax.axis_size("ctx")
+    start = lax.axis_index("ctx") * part
+    mine = jnp.stack([lax.dynamic_slice_in_dim(shard, start, part, 0) for shard in (up, down)], 1)
+    both = double(mine, "tp", 1, 2).reshape(part, -1)
+    whole = lax.all_gather(both, ("fsdp", "ctx"), axis=0, tiled=True)
+    middle = whole.shape[1] // 2
+    return (whole[:, :middle], whole[:, middle:])
+
+
+def reduce_both(part):
+    own = halve(part.reshape(part.shape[0], 2, 2, -1), "tp", 1, 2)
+    whole = double(double(own, "ctx", 2, 0), "ctx", 1, 1)
+    whole = whole.reshape(-1, 2, own.shape[2]).astype(jnp.float32)
+    return (whole[:, 0], whole[:, 1])
+
+
 def pack_grads(*grads):
     return jnp.concatenate(
         [grad.astype(jnp.bfloat16).reshape(grad.shape[0], -1) for grad in grads], 1
@@ -435,17 +568,17 @@
     )
 
 
-def feed_forward(stream, gain, weight_up, weight_down):
+def feed_forward(stream, gain, weight_up, weight_down, total):
     normed, norm_back = jax.vjp(layer_norm, stream, gain)
     normed_low = normed.astype(jnp.bfloat16)
     hidden = jnp.dot(normed_low, weight_up, preferred_element_type=jnp.float32)
     active, active_back = jax.vjp(swish, hidden)
     active_low = active.astype(jnp.bfloat16)
-    branch = tensor_total(product_rows(active_low, weight_down))
+    branch = total(product_rows(active_low, weight_down))
     return (branch, (norm_back, normed_low, active_back, active_low))
 
 
-def feed_backward(branch_grad, saved, weight_up, weight_down, gain_early):
+def feed_backward(branch_grad, saved, weight_up, weight_down, gain_early, total):
     norm_back, normed_low, active_back, active_low = saved
     grad_low = branch_grad.astype(jnp.bfloat16)
     down_grad = product_cols(grad_low, active_low)
@@ -454,11 +587,14 @@
     ].astype(jnp.bfloat16)
     up_grad = product_cols(normed_low, hidden_grad)
     normed_part = product_rows(hidden_grad, weight_up)
+    if not gain_early:
+        stream_grad, gain_part = norm_back(total(normed_part))
+        return (stream_grad, gain_part, up_grad, down_grad)
     _, gain_part = norm_back(normed_part)
-    normed_low_grad = normed_part.astype(jnp.bfloat16)
-    if gain_early:
-        gain_part, normed_low_grad = lax.optimization_barrier((gain_part, normed_low_grad))
-    stream_grad, _ = norm_back(tensor_total(normed_low_grad))
+    gain_part, normed_low_grad = lax.optimization_barrier(
+        (gain_part, normed_part.astype(jnp.bfloat16))
+    )
+    stream_grad, _ = norm_back(total(normed_low_grad))
     return (stream_grad, gain_part, up_grad, down_grad)
 
 
@@ -534,7 +670,9 @@
     proj_out, conv_in, conv_out = gather_weights(attend_out, mixer_in, mixer_out)
     stream = layer_input.reshape(rows, width)
     cotangent = out_grad.reshape(rows, width)
-    branch_one, saved_one = feed_forward(stream, norm_gains[0], up_one, down_one)
+    branch_one, saved_one = feed_forward(
+        stream, norm_gains[0], up_one, down_one, tensor_total
+    )
     after_one = stream + 0.5 * branch_one
     normed, norm_back_two = jax.vjp(layer_norm, after_one, norm_gains[1])
     normed_two = normed.astype(jnp.bfloat16)
@@ -555,6 +693,12 @@
         ],
         -1,
     )
+    joined, late_up, late_down = lax.optimization_barrier((joined, final_up, final_down))
+    by_frames = lax.axis_size("tp") == 2 and lax.axis_size("ctx") == 4
+    if by_frames:
+        up_two, down_two = gather_both(late_up, late_down)
+    else:
+        up_two, down_two = gather_weights(late_up, late_down)
     paired = local_width % PAIR == 0 and batch == 1 and lax.axis_size("ctx") == 4
     pairs = local_width // PAIR
     chunk = min(frames, 512)
@@ -593,8 +737,6 @@
         joined_all = lax.all_gather(joined, "ctx", axis=1, tiled=True)
         mixed, log_total = lax.map(attend_one, (query_low, joined_all, lengths))
         mixed_rows = mixed.reshape(rows, local_width)
-    mixed_rows, late_up, late_down = lax.optimization_barrier((mixed_rows, final_up, final_down))
-    up_two, down_two = gather_weights(late_up, late_down)
     after_two = after_one + tensor_total(product_rows(mixed_rows, proj_out))
     normed, norm_back_three = jax.vjp(layer_norm, after_two, norm_gains[2])
     normed_three = normed.astype(jnp.bfloat16)
@@ -607,21 +749,25 @@
     channels = gated.shape[1]
     gated_low = gated.astype(jnp.bfloat16).reshape(batch, frames, channels)
     reach = KERNEL // 2
-    padded = with_halo(gated_low, (("ctx", 1),), reach)
-    filtered = jnp.zeros((batch, frames, channels), jnp.float32)
-    for offset in range(KERNEL):
-        filtered = filtered + depth_kernel[offset] * padded[:, offset : offset + frames].astype(
-            jnp.float32
-        )
+    conv_fused = batch == 1 and channels % PAIR == 0 and frames % 64 == 0
+    if conv_fused:
+        parts = halo_parts(gated_low[0], reach)
+    else:
+        padded = with_halo(gated_low, (("ctx", 1),), reach)
+    if conv_fused:
+        live_frames = lengths - lax.axis_index("ctx") * frames
+        filtered, live_sum, live_square = conv_forward(parts, depth_kernel, live_frames)
+        filtered = filtered[None]
+    else:
+        filtered = jnp.zeros((batch, frames, channels), jnp.float32)
+        for offset in range(KERNEL):
+            filtered = filtered + depth_kernel[offset] * padded[
+                :, offset : offset + frames
+            ].astype(jnp.float32)
+        live_sum = jnp.sum(live_cube * filtered, (0, 1))
+        live_square = jnp.sum(live_cube * filtered * filtered, (0, 1))
     live_count = jnp.full((channels,), jnp.sum(live))
-    sums = flat_sum(
-        [
-            jnp.sum(live_cube * filtered, (0, 1)),
-            jnp.sum(live_cube * filtered * filtered, (0, 1)),
-            live_count,
-        ],
-        [(("fsdp", "ctx"), 0)],
-    )
+    sums = flat_sum([live_sum, live_square, live_count], [(("fsdp", "ctx"), 0)])
     count = sums[2]
     mean = sums[0] / count
     variance = sums[1] / count - mean * mean
@@ -630,20 +776,53 @@
     shifted = unit * batch_norm[0] + batch_norm[1]
     active, active_back = jax.vjp(swish, shifted.reshape(rows, channels))
     active_low = active.astype(jnp.bfloat16)
-    after_three = after_two + tensor_total(product_rows(active_low, conv_out))
-    branch_four, saved_four = feed_forward(after_three, norm_gains[3], up_two, down_two)
+    conv_part = product_rows(active_low, conv_out)
+    if by_frames:
+        own_half = lax.axis_index("tp")
+
+        def half_of(values):
+            return lax.dynamic_slice_in_dim(values, own_half * (rows // 2), rows // 2, 0)
+
+        conv_low = conv_part.astype(jnp.bfloat16).reshape(2, rows // 2, width)
+        conv_send = lax.dynamic_index_in_dim(conv_low, 1 - own_half, 0, keepdims=False)
+        conv_keep = lax.dynamic_index_in_dim(conv_low, own_half, 0, keepdims=False)
+        conv_other = swap(conv_send, "tp", 1)
+        after_three = (
+            half_of(after_two) + conv_keep.astype(jnp.float32) + conv_other.astype(jnp.float32)
+        )
+        cotangent = half_of(cotangent)
+        total = lambda values: values.astype(jnp.float32)
+        share = 1.0
+    else:
+        after_three = after_two + tensor_total(conv_part)
+        total = tensor_total
+        share = 1.0 / lax.axis_size("tp")
+    branch_four, saved_four = feed_forward(after_three, norm_gains[3], up_two, down_two, total)
     after_four = after_three + 0.5 * branch_four
     result, final_back = jax.vjp(layer_norm, after_four, norm_gains[4])
     grad_four, gain_five = final_back(cotangent)
     stream_grad, gain_four, up_two_grad, down_two_grad = feed_backward(
-        0.5 * grad_four, saved_four, up_two, down_two, False
-    )
+        0.5 * grad_four, saved_four, up_two, down_two, False, total
+    )
+    gain_four, gain_five = gain_four * share, gain_five * share
     grad_three = grad_four + stream_grad
-    early, grad_three = lax.optimization_barrier(
-        (pack_grads(up_two_grad, down_two_grad), grad_three)
-    )
-    up_two_grad, down_two_grad = reduce_grads(early, final_up.shape, final_down.shape)
-    branch_low = grad_three.astype(jnp.bfloat16)
+    if by_frames:
+        branch_low, result_low = lax.optimization_barrier(
+            (grad_three.astype(jnp.bfloat16), result.astype(jnp.bfloat16))
+        )
+        branch_low = double(branch_low, "tp", 1, 0).reshape(rows, width)
+        early, branch_low, result_low = lax.optimization_barrier(
+            (pack_grads(up_two_grad, down_two_grad), branch_low, result_low)
+        )
+        result = double(result_low, "tp", 1, 0).astype(jnp.float32)
+        grad_three = branch_low.astype(jnp.float32)
+        both_part = lax.psum_scatter(early, ("fsdp", "ctx"), scatter_dimension=0, tiled=True)
+    else:
+        early, grad_three = lax.optimization_barrier(
+            (pack_grads(up_two_grad, down_two_grad), grad_three)
+        )
+        up_two_grad, down_two_grad = reduce_grads(early, final_up.shape, final_down.shape)
+        branch_low = grad_three.astype(jnp.bfloat16)
     conv_out_grad = product_cols(branch_low, active_low)
     shifted_grad = active_back(jnp.dot(branch_low, conv_out, preferred_element_type=jnp.float32))[
         0
@@ -659,19 +838,23 @@
         rescale * batch_norm[0] * shifted_grad
         + live_cube * (first_grad + 2.0 * filtered * second_grad)
     ).astype(jnp.bfloat16)
-    padded_grad = with_halo(filtered_grad, (("ctx", 1),), reach)
-    filtered_wide = filtered_grad.astype(jnp.float32)
-    gated_grad = jnp.zeros((batch, frames, channels), jnp.float32)
-    kernel_terms = []
-    for offset in range(KERNEL):
-        start = 2 * reach - offset
-        gated_grad = gated_grad + depth_kernel[offset] * padded_grad[
-            :, start : start + frames
-        ].astype(jnp.float32)
-        kernel_terms.append(
-            jnp.sum(filtered_wide * padded[:, offset : offset + frames].astype(jnp.float32), (0, 1))
-        )
-    kernel_local = jnp.stack(kernel_terms)
+    if conv_fused:
+        grad_parts = halo_parts(filtered_grad[0], reach)
+        gated_grad, kernel_local = conv_backward(parts, grad_parts, depth_kernel)
+    else:
+        padded_grad = with_halo(filtered_grad, (("ctx", 1),), reach)
+        filtered_wide = filtered_grad.astype(jnp.float32)
+        gated_grad = jnp.zeros((batch, frames, channels), jnp.float32)
+        kernel_terms = []
+        for offset in range(KERNEL):
+            start = 2 * reach - offset
+            gated_grad = gated_grad + depth_kernel[offset] * padded_grad[
+                :, start : start + frames
+            ].astype(jnp.float32)
+            kernel_terms.append(
+                jnp.sum(filtered_wide * padded[:, offset : offset + frames].astype(jnp.float32), (0, 1))
+            )
+        kernel_local = jnp.stack(kernel_terms)
     gates_grad = gate_back(gated_grad.reshape(rows, channels))[0].astype(jnp.bfloat16)
     (kernel_total,) = sum_by_swaps([kernel_local], ("ctx", "fsdp"))
     conv_in_grad = jnp.einsum(
@@ -683,7 +866,7 @@
     stream_grad, gain_three = norm_back_three(normed_grad)
     share = 1.0 / lax.axis_size("tp")
     gain_three, gain_four, gain_five = sum_by_swaps(
-        [gain_three * share, gain_four, gain_five * share], ("ctx", "fsdp", "tp")
+        [gain_three * share, gain_four, gain_five], ("ctx", "fsdp", "tp")
     )
     grad_two = grad_three + stream_grad
     branch_low = grad_two.astype(jnp.bfloat16)
@@ -762,8 +945,11 @@
     normed_grad = tensor_total(normed_part)
     stream_grad, gain_two = norm_back_two(normed_grad)
     grad_one = grad_two + stream_grad
+    if by_frames:
+        grad_one, both_part = lax.optimization_barrier((grad_one, both_part))
+        up_two_grad, down_two_grad = reduce_both(both_part)
     stream_grad, gain_one, up_one_grad, down_one_grad = feed_backward(
-        0.5 * grad_one, saved_one, up_one, down_one, True
+        0.5 * grad_one, saved_one, up_one, down_one, True, tensor_total
     )
     input_grad = grad_one + stream_grad
     share = 1.0 / lax.axis_size("tp")

time: 630 us -> 599 us (0.951)
  waiting for transfers between devices: 207 us -> 157 us
  other arithmetic: 110 us -> 85.6 us
  Pallas kernels: 109 us -> 127 us
  local copies, waits for them, and re-layouts: 61.6 us -> 75 us
  starting transfers between devices: 42.5 us -> 55.7 us
    ppermute x8 -> x5, waiting for transfers between devices: 97.6 us -> 43.2 us  [tensor_total(): other = lax.ppermute(low, 'tp', [(0, 1), (1, 0)])]
    reduce_sum x7 -> x2, other arithmetic: 21.5 us -> 0.8 us  [the longest x1 0.73 us: conv_forward(): sums = jnp.sum(sums.reshape(2, 8, channels), 1)]
    pallas_call x0 -> x2, Pallas kernels: none -> 18.8 us  [the longest x1 10.8 us: conv_backward(): pl.pallas_call(conv_backward_kernel, out_shape=[jax.ShapeDtypeStruct((fra...]
    ppermute x48 -> x53, starting transfers between devices: 31.5 us -> 42.5 us  [swap(): lax.ppermute(values, axis, [(i, i ^ bit) for i in range(lax.axis_size(axi...]
    mul x3 -> x0, other arithmetic: 9.99 us -> none  [the longest x2 9.98 us: gate_linear(): return values[:, 0] * jax.nn.sigmoid(values[:, 1]) * live_rows]
    dynamic_slice x0 -> x5, local copies, waits for them, and re-layouts: none -> 7.36 us  [the longest x2 3.72 us: half_of(): lax.dynamic_slice_in_dim(values, own_half * (rows // 2), rows // 2, 0)]
    convert_element_type x0 -> x4, other arithmetic: none -> 7.31 us  [the longest x1 3.17 us: per_device(): result = double(result_low, 'tp', 1, 0).astype(jnp.float32)]
    unnamed x213 -> x200, local copies, waits for them, and re-layouts: 33.1 us -> 29.1 us
  transfers between devices with their start and end apart: 65 -> 67, of which waited for: 27 -> 27; matrix products, arithmetic and copies ran while one was open for 24% -> 25% of each run, Pallas kernels for 16% -> 18%
where the time goes in v5:
time: 599 us; the launch traced here: 589 us
  waiting for transfers between devices  157 us (26%)
  Pallas kernels  127 us (21%)
  other arithmetic  85.6 us (14%)
  local copies, waits for them, and re-layouts  75 us (13%)
  starting transfers between devices  55.7 us (9%)
  matrix products  50.4 us (8%)
  blocking collectives  22 us (4%)
  between operations  17.1 us (3%)
    ppermute x53, waiting for transfers between devices, swap(): lax.ppermute(values, axis, [(i, i ^ bit) for i in range(lax.axis_size(axi...  70.9 us
    pallas_call x4, Pallas kernels, attend_backward(): pl.pallas_call(attend_backward_kernel, grid_spec=pltpu.PrefetchScalarGrid...  53.1 us
    ppermute x5, waiting for transfers between devices, tensor_total(): other = lax.ppermute(low, 'tp', [(0, 1), (1, 0)])  43.2 us
    ppermute x53, starting transfers between devices, swap(): lax.ppermute(values, axis, [(i, i ^ bit) for i in range(lax.axis_size(axi...  42.5 us
    all_gather x2, waiting for transfers between devices, gather_weights(): whole = lax.all_gather(mine, ('fsdp', 'ctx'), axis=0, tiled=True)  38.7 us
    pallas_call x4, Pallas kernels, attend_forward(): pl.pallas_call(functools.partial(attend_forward_kernel, last), grid_spec=...  36.7 us
    unnamed x200, local copies, waits for them, and re-layouts  29.1 us
    all_gather x1, blocking collectives, gather_weights(): whole = lax.all_gather(mine, ('fsdp', 'ctx'), axis=0, tiled=True)  22 us
  transfers between devices with their start and end apart: 67, of which 27 were waited for; matrix products, arithmetic and copies ran while one was open for 25% of the time, Pallas kernels for 18%

profile of v5, /device:TPU:0, one launch (start us, length us, event | category | flops | bytes accessed | tf_op | source)
XLA Modules:
  0.0 589.2 jit_solution(6515612307508634509)
XLA Ops:
  9.0 2.9 copy.163
  16.3 38.7 %all-gather.4.cloned.1.call-done = bf16[512,2048]{1,0:T(8,128)(2,1)} async-done(((bf16[32,2048]{1,0:T(8,128)(2,1)}), bf16[512,2048]{1,0:T(8,128)(2,1)}) %all-gather.4.cloned.1.call-update) | async-done | bytes 2097168 | tf_op jit(solution)/shard_map/all_gather | solution.py:439
  54.9 5.9 %multiply_convert_fusion.1 = (bf16[1024,1024]{1,0:T(8,128)(2,1)S(1)}, f32[1024,1024]{1,0:T(8,128)}) fusion(bf16[512,2048]{1,0:T(8,128)(2,1)} %all-gather.4.cloned.1.call-done, f32[1,1024,512]{1,2,0:T(8,128)} %copy.163, f32[512]{0:T(512)S(1)} %bitcast.419, f32[1024]{0:T(1024)S(1)} %fusion.78, f32[1024]{0:T(1024)S(1)} %broadcast_multiply_fusion.2), kind=kOutput, calls=%fused_computation.11 | convolution fusion | flops 1081081856 | bytes 9447424 | tf_op jit(solution)/shard_map/dot_general | solution.py:574
  60.9 2.3 convolution_convert_fusion.6
  65.8 22.0 %all_gather.13 = bf16[512,768]{1,0:T(8,128)(2,1)S(1)} all-gather(bf16[32,768]{1,0:T(8,128)(2,1)S(1)} %copy.165), channel_id=1, replica_groups=mesh['fsdp'=4,'ctx'=4,'tp'=2] {'fsdp','ctx'}, dimensions={0}, use_global_device_ids=true | all-gather | bytes 835584 | tf_op jit(solution)/shard_map/all_gather | solution.py:439
  90.4 2.8 fusion.115
  98.3 2.0 copy.168
  107.5 1.9 collective-permute-start.3
  117.4 9.2 %attend_forward.4 = (f32[128,1024]{1,0:T(8,128)S(1)}, f32[2,1,1024]{2,1,0:T(1,128)S(1)}, f32[2,1,1024]{2,1,0:T(1,128)S(1)}) custom-call(s32[5]{0:T(128)S(1)} %stack.293.meta_ref, bf16[1024,256]{1,0:T(8,128)(2,1)S(1)} %copy.170.q_ref, bf16[2048,256]{1,0:T(8,128)(2,1)S(1)} %pad_maximum_fusion.3.k_ref.v_ref, bf16[2048,256]{1,0:T(8,128)(2,1)S(1)} %pad_maximum_fusion.3.k_ref.v_ref), custom_call_target="tpu_custom_call" | custom-call | flops 4294967296 | bytes 1835008 | tf_op jit(solution)/shard_map/attend_forward/pallas_call | solution.py:86
  128.1 9.2 %attend_forward.5 = (f32[128,1024]{1,0:T(8,128)S(1)}, f32[2,1,1024]{2,1,0:T(1,128)S(1)}, f32[2,1,1024]{2,1,0:T(1,128)S(1)}) custom-call(s32[5]{0:T(128)S(1)} %stack.293.meta_ref, bf16[1024,256]{1,0:T(8,128)(2,1)S(1)} %copy-done.5, bf16[2048,256]{1,0:T(8,128)(2,1)S(1)} %pad_maximum_fusion.4.k_ref.v_ref, bf16[2048,256]{1,0:T(8,128)(2,1)S(1)} %pad_maximum_fusion.4.k_ref.v_ref), custom_call_target="tpu_custom_call" | custom-call | flops 4294967296 | bytes 1835008 | tf_op jit(solution)/shard_map/attend_forward/pallas_call | solution.py:86
  139.8 9.2 %attend_forward.6 = (f32[128,1024]{1,0:T(8,128)S(1)}, f32[2,1,1024]{2,1,0:T(1,128)S(1)}) custom-call(s32[5]{0:T(128)S(1)} %stack.298.meta_ref, bf16[1024,256]{1,0:T(8,128)(2,1)S(1)} %copy-done.5, bf16[2048,256]{1,0:T(8,128)(2,1)S(1)} %constant_dynamic-update-slice_fusion.k_ref.v_ref, bf16[2048,256]{1,0:T(8,128)(2,1)S(1)} %constant_dynamic-update-slice_fusion.k_ref.v_ref, ...), custom_call_target="tpu_custom_call" | custom-call | flops 4294967296 | bytes 1835008 | tf_op jit(solution)/shard_map/attend_forward/pallas_call | solution.py:86
  149.1 9.2 %attend_forward.7 = (f32[128,1024]{1,0:T(8,128)S(1)}, f32[2,1,1024]{2,1,0:T(1,128)S(1)}) custom-call(s32[5]{0:T(128)S(1)} %stack.298.meta_ref, bf16[1024,256]{1,0:T(8,128)(2,1)S(1)} %copy-done.5, bf16[2048,256]{1,0:T(8,128)(2,1)S(1)} %constant_dynamic-update-slice_fusion.2.k_ref.v_ref, bf16[2048,256]{1,0:T(8,128)(2,1)S(1)} %constant_dynamic-update-slice_fusion.2.k_ref.v_ref, ...), custom_call_target="tpu_custom_call" | custom-call | flops 4294967296 | bytes 1835008 | tf_op jit(solution)/shard_map/attend_forward/pallas_call | solution.py:86
  159.2 2.6 convolution_convert_fusion.2
  161.8 2.0 collective-permute-start.7
  164.7 2.1 copy.239
  166.7 20.9 %collective-permute-done.7 = bf16[1024,512]{0,1:T(8,128)(2,1)} collective-permute-done((bf16[1024,512]{0,1:T(8,128)(2,1)}, bf16[1024,512]{0,1:T(8,128)(2,1)}, u32[]{:S(2)}, u32[]{:S(2)}) %collective-permute-start.7) | collective-permute-done | bytes 1048608 | tf_op jit(solution)/shard_map/ppermute | solution.py:245
  187.7 2.7 fusion.114
  198.5 2.2 collective-permute-done.9.right_ref
  201.3 8.0 %conv_forward.1 = (f32[1024,256]{1,0:T(8,128)}, f32[16,256]{1,0:T(8,128)}) custom-call(s32[1]{0:T(128)S(6)} %sub.157.live_ref, bf16[15,256]{1,0:T(8,128)(2,1)} %copy-done.77, bf16[1024,256]{1,0:T(8,128)(2,1)} %copy-done.24, bf16[15,256]{1,0:T(8,128)(2,1)} %copy-done.78, f32[31,256]{1,0:T(8,128)} %weight_ref.3), custom_call_target="tpu_custom_call" | custom-call | flops 16252928 | bytes 1572864 | tf_op jit(solution)/shard_map/conv_forward/pallas_call | solution.py:283
  211.2 10.0 %group_sum_0.1 = f32[8,128]{1,0:T(8,128)} custom-call(f32[8,128]{1,0:T(8,128)} %fusion.74.x_ref), custom_call_target="tpu_custom_call" | custom-call | tf_op jit(solution)/shard_map/group_sum_0/pallas_call | solution.py:405
  224.9 2.0 copy.178
  228.8 2.7 copy.179
  231.5 2.0 copy.240
  233.6 7.6 %collective-permute-done.10 = bf16[512,512]{0,1:T(8,128)(2,1)} collective-permute-done((bf16[512,512]{0,1:T(8,128)(2,1)}, bf16[512,512]{0,1:T(8,128)(2,1)}, u32[]{:S(2)}, u32[]{:S(2)}) %collective-permute-start.10) | collective-permute-done | bytes 524320 | tf_op jit(solution)/shard_map/ppermute | solution.py:494
  243.8 3.4 fusion.14
  252.5 2.7 fusion.2
  261.0 2.5 pad_maximum_fusion
  263.5 10.0 %collective-permute-done.12 = bf16[512,512]{0,1:T(8,128)(2,1)} collective-permute-done((bf16[512,512]{0,1:T(8,128)(2,1)}, bf16[512,512]{0,1:T(8,128)(2,1)}, u32[]{:S(2)}, u32[]{:S(2)}) %collective-permute-start.12) | collective-permute-done | bytes 524320 | tf_op jit(solution)/shard_map/ppermute | solution.py:494
  275.5 3.0 fusion.108
  279.1 8.0 %group_sum_1.1 = f32[8,128]{1,0:T(8,128)} custom-call(f32[8,128]{1,0:T(8,128)} %fusion.73.x_ref), custom_call_target="tpu_custom_call" | custom-call | tf_op jit(solution)/shard_map/group_sum_1/pallas_call | solution.py:405
  290.4 2.0 collective-permute-start.14
  296.2 10.8 %conv_backward.1 = (f32[1024,256]{1,0:T(8,128)}, f32[248,256]{1,0:T(8,128)}) custom-call(bf16[15,256]{1,0:T(8,128)(2,1)} %copy-done.77, bf16[1024,256]{1,0:T(8,128)(2,1)} %copy-done.24, bf16[15,256]{1,0:T(8,128)(2,1)} %copy-done.78, bf16[15,256]{1,0:T(8,128)(2,1)} %copy-done.82, bf16[1024,256]{1,0:T(8,128)(2,1)} %copy-done.29, bf16[15,256]{1,0:T(8,128)(2,1)} %copy-done.83, ...), custom_call_target="tpu_custom_call" | custom-call | flops 32505856 | bytes 2097152 | tf_op jit(solution)/shard_map/conv_backward/pallas_call | solution.py:339
  307.0 2.3 fusion.28
  312.5 22.2 %collective-permute-done.16 = bf16[1024,512]{0,1:T(8,128)(2,1)S(1)} collective-permute-done((bf16[1024,512]{0,1:T(8,128)(2,1)S(1)}, bf16[1024,512]{0,1:T(8,128)(2,1)S(1)}, u32[]{:S(2)}, u32[]{:S(2)}) %collective-permute-start.16) | collective-permute-done | bytes 1048608 | tf_op jit(solution)/shard_map/ppermute | solution.py:245
  339.0 2.3 convolution_convert_fusion.8
  345.6 3.7 collective-permute-done.56
  354.2 13.2 %attend_backward.4 = (f32[128,1024]{1,0:T(8,128)S(1)}, bf16[2048,256]{1,0:T(8,128)(2,1)S(1)}) custom-call(s32[5]{0:T(128)S(1)} %stack.298.meta_ref, bf16[1024,256]{1,0:T(8,128)(2,1)S(1)} %copy-done.6, bf16[1024,256]{1,0:T(8,128)(2,1)S(1)} %copy.187.g_ref, f32[128,1024]{1,0:T(8,128)S(1)} %get-tuple-element.104.o_ref, ...), custom_call_target="tpu_custom_call" | custom-call | flops 8053063680 | bytes 3670016 | tf_op jit(solution)/shard_map/attend_backward/pallas_call | solution.py:157
  368.4 13.2 %attend_backward.5 = (f32[128,1024]{1,0:T(8,128)S(1)}, bf16[2048,256]{1,0:T(8,128)(2,1)S(1)}) custom-call(s32[5]{0:T(128)S(1)} %stack.298.meta_ref, bf16[1024,256]{1,0:T(8,128)(2,1)S(1)} %copy-done.6, bf16[1024,256]{1,0:T(8,128)(2,1)S(1)} %copy.187.g_ref, f32[128,1024]{1,0:T(8,128)S(1)} %get-tuple-element.113.o_ref, ...), custom_call_target="tpu_custom_call" | custom-call | flops 8053063680 | bytes 3670016 | tf_op jit(solution)/shard_map/attend_backward/pallas_call | solution.py:157
  382.5 13.2 %attend_backward.6 = (f32[128,1024]{1,0:T(8,128)S(1)}, bf16[2048,256]{1,0:T(8,128)(2,1)S(1)}) custom-call(s32[5]{0:T(128)S(1)} %stack.293.meta_ref, bf16[1024,256]{1,0:T(8,128)(2,1)S(1)} %copy-done.6, bf16[1024,256]{1,0:T(8,128)(2,1)S(1)} %copy.187.g_ref, f32[128,1024]{1,0:T(8,128)S(1)} %get-tuple-element.104.o_ref, ...), custom_call_target="tpu_custom_call" | custom-call | flops 8053063680 | bytes 3670016 | tf_op jit(solution)/shard_map/attend_backward/pallas_call | solution.py:157
  398.3 13.4 %attend_backward.7 = (f32[128,1024]{1,0:T(8,128)S(1)}, bf16[2048,256]{1,0:T(8,128)(2,1)S(1)}) custom-call(s32[5]{0:T(128)S(1)} %stack.293.meta_ref, bf16[1024,256]{1,0:T(8,128)(2,1)S(1)} %copy-done.6, bf16[1024,256]{1,0:T(8,128)(2,1)S(1)} %copy.187.g_ref, f32[128,1024]{1,0:T(8,128)S(1)} %get-tuple-element.113.o_ref, ...), custom_call_target="tpu_custom_call" | custom-call | flops 8053063680 | bytes 3670016 | tf_op jit(solution)/shard_map/attend_backward/pallas_call | solution.py:157
  414.8 11.4 %collective-permute-done.22 = bf16[1024,256]{1,0:T(8,128)(2,1)S(1)} collective-permute-done((bf16[1024,256]{1,0:T(8,128)(2,1)S(1)}, bf16[1024,256]{1,0:T(8,128)(2,1)S(1)}, u32[]{:S(2)}, u32[]{:S(2)}) %collective-permute-start.22) | collective-permute-done | bytes 524320 | tf_op jit(solution)/shard_map/ppermute | solution.py:494
  432.6 2.4 bitcast_convert_fusion
  437.7 3.4 reshape_reshape.3
  453.5 3.2 fusion.36
  456.7 3.1 copy.182
  464.7 2.1 collective-permute-start.53
  469.1 6.1 %collective-permute-done.53 = bf16[32,1024]{0,1:T(8,128)(2,1)} collective-permute-done((bf16[32,1024]{0,1:T(8,128)(2,1)S(1)}, bf16[32,1024]{0,1:T(8,128)(2,1)}, u32[]{:S(2)}, u32[]{:S(2)}) %collective-permute-start.53) | collective-permute-done | bytes 65568 | tf_op jit(solution)/shard_map/ppermute | solution.py:494
  479.5 4.3 collective-permute-done.49
  483.8 1.9 collective-permute-start.50
  485.8 3.6 collective-permute-done.50
  499.8 2.5 multiply_reduce_fusion.1
  502.3 3.8 add_add_fusion.3
  506.0 5.7 fusion.5
  513.4 2.3 convolution_convert_fusion.4
  521.1 3.5 convolution_convert_fusion.3
  524.6 2.9 collective-permute-start.28
  542.9 4.7 collective-permute-done.42
  549.3 3.1 collective-permute-done.36
  555.7 2.6 collective-permute-done.37
  558.3 2.7 collective-permute-start.38
  563.6 2.3 collective-permute-start.39
  570.7 2.2 fusion.107
  572.9 3.5 add_bitcast_fusion
  576.4 3.0 copy.222
  (527 shorter events, 180.0 us)
Async XLA Ops:
  7.2 47.8 %all-gather.4.cloned.1.call-start = ((), (), s32[]{:S(2)}) async-start(), calls=%async_computation.2 | async-start | bytes 2228224 | tf_op jit(solution)/shard_map/all_gather | solution.py:439
  8.9 150.2 %all-gather.6.cloned.1.call-start = ((), (), s32[]{:S(2)}) async-start(), calls=%async_computation.3 | async-start | bytes 1114112 | tf_op jit(solution)/shard_map/all_gather | solution.py:439
  63.2 27.2 %collective-permute-start = (bf16[1024,512]{0,1:T(8,128)(2,1)}, bf16[1024,512]{0,1:T(8,128)(2,1)}, u32[]{:S(2)}, u32[]{:S(2)}) collective-permute-start(bf16[1024,512]{0,1:T(8,128)(2,1)} %convolution_convert_fusion.6), channel_id=1, source_target_pairs={{0,1},{1,0},{2,3},{3,2},{4,5},{5,4},{6,7},{7,6},{8,9},{9,8},{10,11... | collective-permute-start | bytes 3145736 | tf_op jit(solution)/shard_map/ppermute | solution.py:245
  65.3 178.5 %all-gather.8.cloned.1.call-start = ((), (), s32[]{:S(2)}) async-start(), calls=%async_computation.4 | async-start | bytes 4456448 | tf_op jit(solution)/shard_map/all_gather | solution.py:455
  103.6 12.6 %collective-permute-start.2 = (bf16[1024,256]{1,0:T(8,128)(2,1)}, bf16[1024,256]{1,0:T(8,128)(2,1)}, u32[]{:S(2)}, u32[]{:S(2)}) collective-permute-start(bf16[1024,256]{1,0:T(8,128)(2,1)} %pad_maximum_fusion.8), channel_id=1, source_target_pairs={{0,2},{2,0},{4,6},{6,4},{1,3},{3,1},{5,7},{7,5},{8,10},{10,8},{12,... | collective-permute-start | bytes 1572872 | tf_op jit(solution)/shard_map/ppermute | solution.py:494
  104.0 22.5 %collective-permute-start.1 = (bf16[1024,256]{1,0:T(8,128)(2,1)}, bf16[1024,256]{1,0:T(8,128)(2,1)}, u32[]{:S(2)}, u32[]{:S(2)}) collective-permute-start(bf16[1024,256]{1,0:T(8,128)(2,1)} %pad_maximum_fusion.8), channel_id=1, source_target_pairs={{0,4},{2,6},{4,0},{6,2},{1,5},{3,7},{5,1},{7,3},{8,12},{10,14},{12... | collective-permute-start | bytes 1572872 | tf_op jit(solution)/shard_map/ppermute | solution.py:494
  105.8 5.8 collective-permute-start.11
  107.3 19.5 %collective-permute-start.4 = (bf16[1024,256]{1,0:T(8,128)(2,1)}, bf16[1024,256]{1,0:T(8,128)(2,1)}, u32[]{:S(2)}, u32[]{:S(2)}) collective-permute-start(bf16[1024,256]{1,0:T(8,128)(2,1)} %pad_maximum_fusion.9), channel_id=1, source_target_pairs={{0,2},{2,0},{4,6},{6,4},{1,3},{3,1},{5,7},{7,5},{8,10},{10,8},{12,... | collective-permute-start | bytes 1572872 | tf_op jit(solution)/shard_map/ppermute | solution.py:494
  107.5 29.8 %collective-permute-start.3 = (bf16[1024,256]{1,0:T(8,128)(2,1)}, bf16[1024,256]{1,0:T(8,128)(2,1)}, u32[]{:S(2)}, u32[]{:S(2)}) collective-permute-start(bf16[1024,256]{1,0:T(8,128)(2,1)} %pad_maximum_fusion.9), channel_id=1, source_target_pairs={{0,4},{2,6},{4,0},{6,2},{1,5},{3,7},{5,1},{7,3},{8,12},{10,14},{12... | collective-permute-start | bytes 1572872 | tf_op jit(solution)/shard_map/ppermute | solution.py:494
  115.7 348.0 %reduce-scatter.7.cloned.1.call-start = ((), (), s32[]{:S(2)}) async-start(), calls=%async_computation.6 | async-start | bytes 1114112
  126.6 13.2 %collective-permute-start.5 = (bf16[1024,256]{1,0:T(8,128)(2,1)}, bf16[1024,256]{1,0:T(8,128)(2,1)S(1)}, u32[]{:S(2)}, u32[]{:S(2)}) collective-permute-start(bf16[1024,256]{1,0:T(8,128)(2,1)} %collective-permute-done.1), channel_id=1, source_target_pairs={{0,2},{2,0},{4,6},{6,4},{1,3},{3,1},{5,7},{7,5},{8,10},{10,8},{12,... | collective-permute-start | bytes 1572872 | tf_op jit(solution)/shard_map/ppermute | solution.py:494
  137.3 11.8 %collective-permute-start.6 = (bf16[1024,256]{1,0:T(8,128)(2,1)}, bf16[1024,256]{1,0:T(8,128)(2,1)S(1)}, u32[]{:S(2)}, u32[]{:S(2)}) collective-permute-start(bf16[1024,256]{1,0:T(8,128)(2,1)} %collective-permute-done.3), channel_id=1, source_target_pairs={{0,2},{2,0},{4,6},{6,4},{1,3},{3,1},{5,7},{7,5},{8,10},{10,8},{12,... | collective-permute-start | bytes 1572872 | tf_op jit(solution)/shard_map/ppermute | solution.py:494
  161.8 25.9 %collective-permute-start.7 = (bf16[1024,512]{0,1:T(8,128)(2,1)}, bf16[1024,512]{0,1:T(8,128)(2,1)}, u32[]{:S(2)}, u32[]{:S(2)}) collective-permute-start(bf16[1024,512]{0,1:T(8,128)(2,1)} %convolution_convert_fusion.2), channel_id=1, source_target_pairs={{0,1},{1,0},{2,3},{3,2},{4,5},{5,4},{6,7},{7,6},{8,9},{9,8},{10,11... | collective-permute-start | bytes 3145736 | tf_op jit(solution)/shard_map/ppermute | solution.py:245
  194.9 3.6 collective-permute-start.8
  196.4 4.3 collective-permute-start.9
  226.9 14.2 %collective-permute-start.10 = (bf16[512,512]{0,1:T(8,128)(2,1)}, bf16[512,512]{0,1:T(8,128)(2,1)}, u32[]{:S(2)}, u32[]{:S(2)}) collective-permute-start(bf16[512,512]{0,1:T(8,128)(2,1)} %bitcast.394), channel_id=1, source_target_pairs={{0,1},{1,0},{2,3},{3,2},{4,5},{5,4},{6,7},{7,6},{8,9},{9,8},{10,11... | collective-permute-start | bytes 1572872 | tf_op jit(solution)/shard_map/ppermute | solution.py:494
  260.1 13.4 %collective-permute-start.12 = (bf16[512,512]{0,1:T(8,128)(2,1)}, bf16[512,512]{0,1:T(8,128)(2,1)}, u32[]{:S(2)}, u32[]{:S(2)}) collective-permute-start(bf16[512,512]{0,1:T(8,128)(2,1)} %add_convert_fusion.6), channel_id=1, source_target_pairs={{0,1},{1,0},{2,3},{3,2},{4,5},{5,4},{6,7},{7,6},{8,9},{9,8},{10,11... | collective-permute-start | bytes 1572872 | tf_op jit(solution)/shard_map/ppermute | solution.py:494
  290.4 3.3 collective-permute-start.14
  292.4 3.2 collective-permute-start.15
  310.1 24.7 %collective-permute-start.16 = (bf16[1024,512]{0,1:T(8,128)(2,1)S(1)}, bf16[1024,512]{0,1:T(8,128)(2,1)S(1)}, u32[]{:S(2)}, u32[]{:S(2)}) collective-permute-start(bf16[1024,512]{0,1:T(8,128)(2,1)S(1)} %bitcast_convert_fusion.1), channel_id=1, source_target_pairs={{0,1},{1,0},{2,3},{3,2},{4,5},{5,4},{6,7},{7,6},{8,9},{9,8},{10,11... | collective-permute-start | bytes 3145736 | tf_op jit(solution)/shard_map/ppermute | solution.py:245
  342.6 163.4 %reduce-scatter.5.cloned.1.call-start = ((), (), s32[]{:S(2)}) async-start(), calls=%async_computation.5 | async-start | bytes 4456448 | tf_op jit(solution)/shard_map/reduce_scatter | solution.py:819
  345.4 3.9 collective-permute-start.56
  349.3 4.0 collective-permute-start.57
  350.7 102.8 %collective-permute-start.13 = (bf16[512,512]{0,1:T(8,128)(2,1)}, bf16[512,512]{0,1:T(8,128)(2,1)}, u32[]{:S(2)}, u32[]{:S(2)}) collective-permute-start(bf16[512,512]{0,1:T(8,128)(2,1)} %get-tuple-element.120), channel_id=1, source_target_pairs={{0,1},{1,0},{2,3},{3,2},{4,5},{5,4},{6,7},{7,6},{8,9},{9,8},{10,11... | collective-permute-start | bytes 1572872 | tf_op jit(solution)/shard_map/ppermute | solution.py:494
  354.2 13.9 %collective-permute-start.30 = (f32[16,128]{1,0:T(8,128)S(1)}, f32[16,128]{1,0:T(8,128)S(1)}, u32[]{:S(2)}, u32[]{:S(2)}) collective-permute-start(f32[16,128]{1,0:T(8,128)S(1)} %fusion.72), channel_id=1, source_target_pairs={{0,2},{2,0},{4,6},{6,4},{1,3},{3,1},{5,7},{7,5},{8,10},{10,8},{12,... | collective-permute-start | bytes 24584 | tf_op jit(solution)/shard_map/ppermute | solution.py:494
  367.5 14.9 %collective-permute-start.17 = (bf16[1024,256]{1,0:T(8,128)(2,1)S(1)}, bf16[1024,256]{1,0:T(8,128)(2,1)S(1)}, u32[]{:S(2)}, u32[]{:S(2)}) collective-permute-start(bf16[1024,256]{1,0:T(8,128)(2,1)S(1)} %slice.270), channel_id=1, source_target_pairs={{0,2},{2,0},{4,6},{6,4},{1,3},{3,1},{5,7},{7,5},{8,10},{10,8},{12,... | collective-permute-start | bytes 1572872 | tf_op jit(solution)/shard_map/ppermute | solution.py:494
  368.1 13.7 %collective-permute-start.31 = (f32[16,128]{1,0:T(8,128)S(1)}, f32[16,128]{1,0:T(8,128)S(1)}, u32[]{:S(2)}, u32[]{:S(2)}) collective-permute-start(f32[16,128]{1,0:T(8,128)S(1)} %fusion.99), channel_id=1, source_target_pairs={{0,4},{2,6},{4,0},{6,2},{1,5},{3,7},{5,1},{7,3},{8,12},{10,14},{12... | collective-permute-start | bytes 24584 | tf_op jit(solution)/shard_map/ppermute | solution.py:494
  381.7 16.5 %collective-permute-start.18 = (bf16[1024,256]{1,0:T(8,128)(2,1)S(1)}, bf16[1024,256]{1,0:T(8,128)(2,1)S(1)}, u32[]{:S(2)}, u32[]{:S(2)}) collective-permute-start(bf16[1024,256]{1,0:T(8,128)(2,1)S(1)} %slice.272), channel_id=1, source_target_pairs={{0,2},{2,0},{4,6},{6,4},{1,3},{3,1},{5,7},{7,5},{8,10},{10,8},{12,... | collective-permute-start | bytes 1572872 | tf_op jit(solution)/shard_map/ppermute | solution.py:494
  395.8 16.7 %collective-permute-start.19 = (bf16[1024,256]{1,0:T(8,128)(2,1)S(1)}, bf16[1024,256]{1,0:T(8,128)(2,1)S(1)}, u32[]{:S(2)}, u32[]{:S(2)}) collective-permute-start(bf16[1024,256]{1,0:T(8,128)(2,1)S(1)} %slice.274), channel_id=1, source_target_pairs={{0,2},{2,0},{4,6},{6,4},{1,3},{3,1},{5,7},{7,5},{8,10},{10,8},{12,... | collective-permute-start | bytes 1572872 | tf_op jit(solution)/shard_map/ppermute | solution.py:494
  396.4 17.0 %collective-permute-start.20 = (bf16[1024,256]{1,0:T(8,128)(2,1)S(1)}, bf16[1024,256]{1,0:T(8,128)(2,1)S(1)}, u32[]{:S(2)}, u32[]{:S(2)}) collective-permute-start(bf16[1024,256]{1,0:T(8,128)(2,1)S(1)} %add_convert_fusion.4), channel_id=1, source_target_pairs={{0,4},{2,6},{4,0},{6,2},{1,5},{3,7},{5,1},{7,3},{8,12},{10,14},{12... | collective-permute-start | bytes 1572872 | tf_op jit(solution)/shard_map/ppermute | solution.py:494
  411.8 3.0 collective-permute-start.21
  411.9 14.3 %collective-permute-start.22 = (bf16[1024,256]{1,0:T(8,128)(2,1)S(1)}, bf16[1024,256]{1,0:T(8,128)(2,1)S(1)}, u32[]{:S(2)}, u32[]{:S(2)}) collective-permute-start(bf16[1024,256]{1,0:T(8,128)(2,1)S(1)} %add_convert_fusion.3), channel_id=1, source_target_pairs={{0,4},{2,6},{4,0},{6,2},{1,5},{3,7},{5,1},{7,3},{8,12},{10,14},{12... | collective-permute-start | bytes 1572872 | tf_op jit(solution)/shard_map/ppermute | solution.py:494
  412.5 34.0 %collective-permute-start.58 = (f32[64,128]{1,0:T(8,128)}, f32[64,128]{1,0:T(8,128)}, u32[]{:S(2)}, u32[]{:S(2)}) collective-permute-start(f32[64,128]{1,0:T(8,128)} %add.523), channel_id=1, source_target_pairs={{0,16},{8,24},{16,0},{24,8},{1,17},{9,25},{17,1},{25,9},{2,18},{10... | collective-permute-start | bytes 98312 | tf_op jit(solution)/shard_map/ppermute | solution.py:494
  413.4 30.7 %collective-permute-start.32 = (f32[16,128]{1,0:T(8,128)}, f32[16,128]{1,0:T(8,128)}, u32[]{:S(2)}, u32[]{:S(2)}) collective-permute-start(f32[16,128]{1,0:T(8,128)} %fusion.141), channel_id=1, source_target_pairs={{0,8},{8,0},{16,24},{24,16},{1,9},{9,1},{17,25},{25,17},{2,10},{10... | collective-permute-start | bytes 24584 | tf_op jit(solution)/shard_map/ppermute | solution.py:494
  442.8 18.2 %collective-permute-start.47 = (bf16[2,2,2,32,768]{4,3,2,1,0:T(8,128)(2,1)}, bf16[2,2,2,32,768]{4,3,2,1,0:T(8,128)(2,1)S(1)}, u32[]{:S(2)}, u32[]{:S(2)}) collective-permute-start(bf16[2,2,2,32,768]{4,3,2,1,0:T(8,128)(2,1)} %dynamic-slice_bitcast_fusion.2), channel_id=1, source_target_pairs={{0,2},{2,0},{4,6},{6,4},{1,3},{3,1},{5,7},{7,5},{8,10},{10,8},{12,... | collective-permute-start | bytes 1179656 | tf_op jit(solution)/shard_map/ppermute | solution.py:494
  445.4 5.4 collective-permute-start.33
  452.2 7.6 %collective-permute-start.34 = (f32[16,128]{1,0:T(8,128)}, f32[16,128]{1,0:T(8,128)}, u32[]{:S(2)}, u32[]{:S(2)}) collective-permute-start(f32[16,128]{1,0:T(8,128)} %add.495), channel_id=1, source_target_pairs={{0,1},{1,0},{2,3},{3,2},{4,5},{5,4},{6,7},{7,6},{8,9},{9,8},{10,11... | collective-permute-start | bytes 24584 | tf_op jit(solution)/shard_map/ppermute | solution.py:494
  463.6 13.8 %collective-permute-start.48 = (bf16[2,2,32,768]{3,2,1,0:T(8,128)(2,1)}, bf16[2,2,32,768]{3,2,1,0:T(8,128)(2,1)}, u32[]{:S(2)}, u32[]{:S(2)}) collective-permute-start(bf16[2,2,32,768]{3,2,1,0:T(8,128)(2,1)} %dynamic-slice_bitcast_fusion.5), channel_id=1, source_target_pairs={{0,4},{2,6},{4,0},{6,2},{1,5},{3,7},{5,1},{7,3},{8,12},{10,14},{12... | collective-permute-start | bytes 589832 | tf_op jit(solution)/shard_map/ppermute | solution.py:494
  464.7 10.5 %collective-permute-start.53 = (bf16[32,1024]{0,1:T(8,128)(2,1)S(1)}, bf16[32,1024]{0,1:T(8,128)(2,1)}, u32[]{:S(2)}, u32[]{:S(2)}) collective-permute-start(bf16[32,1024]{0,1:T(8,128)(2,1)S(1)} %copy.238), channel_id=1, source_target_pairs={{0,4},{2,6},{4,0},{6,2},{1,5},{3,7},{5,1},{7,3},{8,12},{10,14},{12... | collective-permute-start | bytes 196616 | tf_op jit(solution)/shard_map/ppermute | solution.py:494
  468.1 29.8 %collective-permute-start.23 = (bf16[1024,512]{0,1:T(8,128)(2,1)S(1)}, bf16[1024,512]{0,1:T(8,128)(2,1)}, u32[]{:S(2)}, u32[]{:S(2)}) collective-permute-start(bf16[1024,512]{0,1:T(8,128)(2,1)S(1)} %bitcast_convert_fusion), channel_id=1, source_target_pairs={{0,1},{1,0},{2,3},{3,2},{4,5},{5,4},{6,7},{7,6},{8,9},{9,8},{10,11... | collective-permute-start | bytes 3145736 | tf_op jit(solution)/shard_map/ppermute | solution.py:245
  477.3 8.4 %collective-permute-start.54 = (bf16[2,32,1024]{2,1,0:T(8,128)(2,1)S(1)}, bf16[2,32,1024]{2,1,0:T(8,128)(2,1)S(1)}, u32[]{:S(2)}, u32[]{:S(2)}) collective-permute-start(bf16[2,32,1024]{2,1,0:T(8,128)(2,1)S(1)} %maximum_select_fusion.15), channel_id=1, source_target_pairs={{0,2},{2,0},{4,6},{6,4},{1,3},{3,1},{5,7},{7,5},{8,10},{10,8},{12,... | collective-permute-start | bytes 393224 | tf_op jit(solution)/shard_map/ppermute | solution.py:494
  478.5 5.2 collective-permute-start.49
  483.8 5.6 collective-permute-start.50
  489.4 4.2 collective-permute-start.51
  513.2 3.7 collective-permute-start.25
  516.9 3.7 collective-permute-start.26
  518.4 9.2 %collective-permute-start.59 = (bf16[32,2,1024]{2,0,1:T(8,128)(2,1)S(1)}, bf16[32,2,1024]{2,0,1:T(8,128)(2,1)S(1)}, u32[]{:S(2)}, u32[]{:S(2)}) collective-permute-start(bf16[32,2,1024]{2,0,1:T(8,128)(2,1)S(1)} %bitcast.406), channel_id=1, source_target_pairs={{0,1},{1,0},{2,3},{3,2},{4,5},{5,4},{6,7},{7,6},{8,9},{9,8},{10,11... | collective-permute-start | bytes 393224 | tf_op jit(solution)/shard_map/ppermute | solution.py:494
  520.6 4.0 collective-permute-start.27
  524.6 4.6 collective-permute-start.28
  527.6 5.5 collective-permute-start.60
  529.2 7.9 %collective-permute-start.41 = (bf16[2,2,2,32,1024]{4,3,2,1,0:T(8,128)(2,1)}, bf16[2,2,2,32,1024]{4,3,2,1,0:T(8,128)(2,1)}, u32[]{:S(2)}, u32[]{:S(2)}) collective-permute-start(bf16[2,2,2,32,1024]{4,3,2,1,0:T(8,128)(2,1)} %dynamic-slice_bitcast_fusion), channel_id=1, source_target_pairs={{0,2},{2,0},{4,6},{6,4},{1,3},{3,1},{5,7},{7,5},{8,10},{10,8},{12,... | collective-permute-start | bytes 1572872 | tf_op jit(solution)/shard_map/ppermute | solution.py:494
  529.2 3.9 collective-permute-start.29
  531.8 8.0 %collective-permute-start.35 = (bf16[2,2,2,32,1024]{4,3,2,1,0:T(8,128)(2,1)}, bf16[2,2,2,32,1024]{4,3,2,1,0:T(8,128)(2,1)}, u32[]{:S(2)}, u32[]{:S(2)}) collective-permute-start(bf16[2,2,2,32,1024]{4,3,2,1,0:T(8,128)(2,1)} %dynamic-slice_bitcast_fusion.1), channel_id=1, source_target_pairs={{0,2},{2,0},{4,6},{6,4},{1,3},{3,1},{5,7},{7,5},{8,10},{10,8},{12,... | collective-permute-start | bytes 1572872 | tf_op jit(solution)/shard_map/ppermute | solution.py:494
  531.9 36.9 %collective-permute-start.24 = (bf16[1024,512]{0,1:T(8,128)(2,1)S(1)}, bf16[1024,512]{0,1:T(8,128)(2,1)}, u32[]{:S(2)}, u32[]{:S(2)}) collective-permute-start(bf16[1024,512]{0,1:T(8,128)(2,1)S(1)} %get-tuple-element.155), channel_id=1, source_target_pairs={{0,1},{1,0},{2,3},{3,2},{4,5},{5,4},{6,7},{7,6},{8,9},{9,8},{10,11... | collective-permute-start | bytes 3145736 | tf_op jit(solution)/shard_map/ppermute | solution.py:245
  538.4 9.2 %collective-permute-start.42 = (bf16[2,2,32,1024]{3,2,1,0:T(8,128)(2,1)S(1)}, bf16[2,2,32,1024]{3,2,1,0:T(8,128)(2,1)S(1)}, u32[]{:S(2)}, u32[]{:S(2)}) collective-permute-start(bf16[2,2,32,1024]{3,2,1,0:T(8,128)(2,1)S(1)} %dynamic-slice_bitcast_fusion.3), channel_id=1, source_target_pairs={{0,4},{2,6},{4,0},{6,2},{1,5},{3,7},{5,1},{7,3},{8,12},{10,14},{12... | collective-permute-start | bytes 786440 | tf_op jit(solution)/shard_map/ppermute | solution.py:494
  541.1 11.3 %collective-permute-start.36 = (bf16[2,2,32,1024]{3,2,1,0:T(8,128)(2,1)S(1)}, bf16[2,2,32,1024]{3,2,1,0:T(8,128)(2,1)S(1)}, u32[]{:S(2)}, u32[]{:S(2)}) collective-permute-start(bf16[2,2,32,1024]{3,2,1,0:T(8,128)(2,1)S(1)} %dynamic-slice_bitcast_fusion.4), channel_id=1, source_target_pairs={{0,4},{2,6},{4,0},{6,2},{1,5},{3,7},{5,1},{7,3},{8,12},{10,14},{12... | collective-permute-start | bytes 786440 | tf_op jit(solution)/shard_map/ppermute | solution.py:494
  547.8 6.4 %collective-permute-start.43 = (bf16[2,32,1024]{2,1,0:T(8,128)(2,1)S(1)}, bf16[2,32,1024]{2,1,0:T(8,128)(2,1)S(1)}, u32[]{:S(2)}, u32[]{:S(2)}) collective-permute-start(bf16[2,32,1024]{2,1,0:T(8,128)(2,1)S(1)} %dynamic-slice_bitcast_fusion.6), channel_id=1, source_target_pairs={{0,8},{8,0},{16,24},{24,16},{1,9},{9,1},{17,25},{25,17},{2,10},{10... | collective-permute-start | bytes 393224 | tf_op jit(solution)/shard_map/ppermute | solution.py:494
  552.5 5.7 collective-permute-start.37
  554.2 6.8 %collective-permute-start.44 = (bf16[32,1024]{1,0:T(8,128)(2,1)S(1)}, bf16[32,1024]{1,0:T(8,128)(2,1)S(1)}, u32[]{:S(2)}, u32[]{:S(2)}) collective-permute-start(bf16[32,1024]{1,0:T(8,128)(2,1)S(1)} %dynamic-slice_bitcast_fusion.9), channel_id=1, source_target_pairs={{0,16},{8,24},{16,0},{24,8},{1,17},{9,25},{17,1},{25,9},{2,18},{10... | collective-permute-start | bytes 196616 | tf_op jit(solution)/shard_map/ppermute | solution.py:494
  558.3 5.2 collective-permute-start.38
  561.0 5.0 collective-permute-start.45
  563.6 4.5 collective-permute-start.39
  566.6 12.8 %collective-permute-start.46 = (bf16[2,32,1024]{2,1,0:T(8,128)(2,1)}, bf16[2,32,1024]{2,1,0:T(8,128)(2,1)}, u32[]{:S(2)}, u32[]{:S(2)}) collective-permute-start(bf16[2,32,1024]{2,1,0:T(8,128)(2,1)} %maximum_select_fusion.13), channel_id=1, source_target_pairs={{0,2},{2,0},{4,6},{6,4},{1,3},{3,1},{5,7},{7,5},{8,10},{10,8},{12,... | collective-permute-start | bytes 393224 | tf_op jit(solution)/shard_map/ppermute | solution.py:494
  568.8 12.5 %collective-permute-start.40 = (bf16[2,32,1024]{2,1,0:T(8,128)(2,1)}, bf16[2,32,1024]{2,1,0:T(8,128)(2,1)S(1)}, u32[]{:S(2)}, u32[]{:S(2)}) collective-permute-start(bf16[2,32,1024]{2,1,0:T(8,128)(2,1)} %maximum_select_fusion.11), channel_id=1, source_target_pairs={{0,2},{2,0},{4,6},{6,4},{1,3},{3,1},{5,7},{7,5},{8,10},{10,8},{12,... | collective-permute-start | bytes 393224 | tf_op jit(solution)/shard_map/ppermute | solution.py:494
  (97 other events, 831.6 us)
Sparse Core Ops, SparseCore 0:
  10.7 44.1 all-gather.3
  65.4 36.2 all-gather.5
  115.8 50.0 all-gather.7
  342.7 56.3 reduce-scatter.6
  402.8 71.9 reduce-scatter.4
